TPU v7x, 128 devices: a whole 4x4x4 slice. The times are simulated.
128 devices in a mesh: rows: 8 (over z, y_lo), cols: 16 (over x, y_hi, core).
Axes of the slice: x: 4, y: 4 (y_hi: 2, y_lo: 2; y = y_hi * 2 + y_lo), z: 4, core: 2. Of those that a mesh axis runs over, the one named last changes fastest.
Arguments:
- imagery: bfloat16 [128, 256, 192], P('rows', 'cols'), may hold values from -6 to 6
- cotangent: bfloat16 [128, 256, 192], P('rows', 'cols'), may hold values from -6 to 6
- norm_gain: float32 [2, 192], replicated, may hold values from 0.5 to 1.5
- norm_bias: float32 [2, 192], replicated, may hold values from -3 to 3
- qkv_weight: bfloat16 [2, 192, 576], replicated, may hold values from -0.4375 to 0.4375
- qkv_bias: float32 [2, 576], replicated, may hold values from -3 to 3
- rel_table: float32 [2, 6, 225], replicated, may hold values from -4 to 330
- proj_weight: bfloat16 [2, 192, 192], replicated, may hold values from -0.4375 to 0.4375
- proj_bias: float32 [2, 192], replicated, may hold values from -3 to 3
- mlp_gain: float32 [2, 192], replicated, may hold values from 0.5 to 1.5
- mlp_bias: float32 [2, 192], replicated, may hold values from -3 to 3
- up_weight: bfloat16 [2, 192, 768], replicated, may hold values from -0.4375 to 0.4375
- up_bias: float32 [2, 768], replicated, may hold values from -3 to 3
- down_weight: bfloat16 [2, 768, 192], replicated, may hold values from -0.21875 to 0.21875
- down_bias: float32 [2, 192], replicated, may hold values from -3 to 3
Outputs:
- output: bfloat16 [128, 256, 192], P('rows', 'cols')
- imagery_grad: bfloat16 [128, 256, 192], P('rows', 'cols')
- norm_gain_grad: float32 [2, 192], replicated
- norm_bias_grad: float32 [2, 192], replicated
- qkv_weight_grad: float32 [2, 192, 576], replicated
- qkv_bias_grad: float32 [2, 576], replicated
- rel_table_grad: float32 [2, 6, 225], replicated
- proj_weight_grad: float32 [2, 192, 192], replicated
- proj_bias_grad: float32 [2, 192], replicated
- mlp_gain_grad: float32 [2, 192], replicated
- mlp_bias_grad: float32 [2, 192], replicated
- up_weight_grad: float32 [2, 192, 768], replicated
- up_bias_grad: float32 [2, 768], replicated
- down_weight_grad: float32 [2, 768, 192], replicated
- down_bias_grad: float32 [2, 192], replicated
All inputs are finite; a program needn't handle non-finite values.
Results may differ from a plain program's by a relative error of at most 0.02.
Values may be sent and summed in bfloat16 or wider, within the bound.
No kernel may reach another device: no remote copies, remote signals or barrier semaphores. Data moves between devices by JAX's collectives and lax.ppermute only.
A program may use at most 128 MiB of HBM per device.

v0:
```python
import jax
import jax.numpy as jnp
from jax import lax
from jax.experimental import pallas as pl
from jax.experimental.pallas import tpu as pltpu
from jax.sharding import PartitionSpec as P

F32 = jnp.float32
BF16 = jnp.bfloat16
C = 192
HEADS = 6
DIM = 32
MLP = 768
TILE = 16
TOK = TILE * TILE
SPAN = 15
SCALE = DIM**-0.5
EPSILON = 1e-05
FLAT = 4096
SMALL = 3456
MASKED = -1e30


def dot_tn(a, b):
    return lax.dot_general(a, b, (((0,), (0,)), ((), ())), preferred_element_type=F32)


def dot_nn(a, b):
    return lax.dot_general(a, b, (((1,), (0,)), ((), ())), preferred_element_type=F32)


def dot_nt(a, b):
    return lax.dot_general(a, b, (((1,), (1,)), ((), ())), preferred_element_type=F32)


def iota(shape, dim):
    return lax.broadcasted_iota(jnp.int32, shape, dim)


def split3(value):
    high = value.astype(BF16)
    rest = value - high.astype(F32)
    mid = rest.astype(BF16)
    return high, mid, (rest - mid.astype(F32)).astype(BF16)


def window_row(r, wc):
    return ((r // 8) * 2 + wc) * 64 + (r % 8) * 8


def halves():
    return iota((64, 128), 1) < 64


def stack_windows(value, left):
    zero = jnp.zeros_like(value)
    return jnp.concatenate([jnp.where(left, value, zero), jnp.where(left, zero, value)], axis=0).astype(BF16)


def own_window(full, left):
    return jnp.where(left, full[:64], full[64:])


def norm_fwd(x):
    center = x - jnp.mean(x, axis=0, keepdims=True)
    rstd = lax.rsqrt(jnp.mean(center * center, axis=0, keepdims=True) + EPSILON)
    return center * rstd, rstd


def norm_bwd(dn, xhat, rstd, gain):
    dxh = dn * gain
    along = jnp.mean(dxh * xhat, axis=0, keepdims=True)
    return rstd * (dxh - jnp.mean(dxh, axis=0, keepdims=True) - xhat * along)


def spread(lane_q):
    q = lane_q % 64
    return (q // 8) * SPAN + q % 8


VEC_NAMES = ("ng", "nb", "pb", "mg", "mb", "db", "qb", "ub")


def load_columns(vec, par):
    for i, name in enumerate(VEC_NAMES):
        n = par[name].shape[-1]
        vec[i : i + 1, 0:n] = par[name][0]
    return vec[...].T


def position_bias(par, table, bias):
    table[...] = jnp.zeros((8, 256), F32)
    table[0:HEADS, 0 : SPAN * SPAN] = par["rel"][0]
    select = (iota((128, 128), 0) == spread(iota((128, 128), 1))).astype(BF16)
    for h in range(HEADS):
        row = jnp.broadcast_to(table[h : h + 1, :], (8, 256))
        rows = []
        for ky in range(8):
            shift = (249 - SPAN * (7 - ky)) % 256
            rows.append(pltpu.roll(row, shift, 1, stride=1, stride_axis=0)[:, 0:128])
        high, mid, low = split3(jnp.concatenate(rows, axis=0))
        bias[h] = dot_nn(high, select) + (dot_nn(mid, select) + dot_nn(low, select))


def same_zone(p, last_row, last_col):
    k = iota((64, 128), 0)
    lane = iota((64, 128), 1)
    q = lane % 64
    rows = ((q // 8) < 4) == ((k // 8) < 4)
    cols = ((q % 8) < 4) == ((k % 8) < 4)
    keep = jnp.logical_or(cols, jnp.logical_or(lane < 64, jnp.logical_not(last_col)))
    if p == 1:
        keep = jnp.logical_and(keep, jnp.logical_or(rows, jnp.logical_not(last_row)))
    return keep


def forward(x, par, cols, bias, res, zones):
    left = halves()
    xhat, _ = norm_fwd(x)
    normed = (xhat * cols[0:C, 0:1] + cols[0:C, 1:2]).astype(BF16)
    res["packed"][...] = (dot_tn(par["qw"][0], normed) + cols[0:576, 6:7]).astype(BF16)
    for p in range(2):
        lanes = slice(128 * p, 128 * p + 128)
        for h in range(HEADS):
            q = res["packed"][DIM * h : DIM * h + DIM, lanes]
            k = res["packed"][C + DIM * h : C + DIM * h + DIM, lanes]
            v = res["packed"][2 * C + DIM * h : 2 * C + DIM * h + DIM, lanes]
            s = own_window(dot_tn(k, q), left) * SCALE + bias[h]
            if zones is not None:
                s = jnp.where(zones[p], s, MASKED)
            e = jnp.exp(s - jnp.max(s, axis=0, keepdims=True))
            a = e * (1.0 / jnp.sum(e, axis=0, keepdims=True))
            res["attn"][p * HEADS + h] = a.astype(BF16)
            res["mixed"][DIM * h : DIM * h + DIM, lanes] = dot_nn(v, stack_windows(a, left)).astype(BF16)
    middle = x + dot_tn(par["pw"][0], res["mixed"][...]) + cols[0:C, 2:3]
    res["middle"][...] = middle.astype(BF16)
    middle = res["middle"][...].astype(F32)
    xhat, _ = norm_fwd(middle)
    normed = (xhat * cols[0:C, 3:4] + cols[0:C, 4:5]).astype(BF16)
    for i in range(0, MLP, 128):
        u = dot_tn(par["uw"][0, :, i : i + 128], normed) + cols[i : i + 128, 7:8]
        half = 0.5 + 0.5 * lax.erf(u * (0.5**0.5))
        res["hidden"][i : i + 128, :] = (u * half).astype(BF16)
        res["slope"][i : i + 128, :] = (half + u * (jnp.exp(-0.5 * u * u) * 0.3989422804014327)).astype(BF16)
    out = middle + dot_tn(par["dw"][0], res["hidden"][...]) + cols[0:C, 5:6]
    return out.astype(BF16)


def put_row(small, at, row):
    n = row.shape[-1]
    for i in range(0, n, 128):
        w = min(128, n - i)
        small[at + i // 128 : at + i // 128 + 1, 0:w] = row[0:1, i : i + w]


def backward(dout, x, par, cols, res, flat, small, du_ref, dpacked, rel_sum):
    left = halves()
    ones = jnp.ones((8, TOK), BF16)
    none = jnp.zeros((64, TOK), BF16)
    small[...] = jnp.zeros(small.shape, F32)
    middle = res["middle"][...].astype(F32)
    xhat, rstd = norm_fwd(middle)
    normed = (xhat * cols[0:C, 3:4] + cols[0:C, 4:5]).astype(BF16)
    flat[2304:3072, :] = dot_nt(res["hidden"][...], dout[0:128]).astype(BF16)
    tail = dot_nt(res["hidden"][0:384, :], jnp.concatenate([dout[128:192], none], axis=0))
    tail = tail + dot_nt(res["hidden"][384:768, :], jnp.concatenate([none, dout[128:192]], axis=0))
    flat[3072:3456, :] = tail.astype(BF16)
    put_row(small, 21, dot_nt(ones, dout))
    for i in range(0, MLP, 128):
        dh = dot_nn(par["dw"][0, i : i + 128, :], dout).astype(BF16).astype(F32)
        du = (dh * res["slope"][i : i + 128, :].astype(F32)).astype(BF16)
        du_ref[i : i + 128, :] = du
        flat[1152 + C * (i // 128) : 1152 + C * (i // 128) + C, :] = dot_nt(normed, du).astype(BF16)
    put_row(small, 15, dot_nt(ones, du_ref[...]))
    dn = dot_nn(par["uw"][0], du_ref[...]).astype(BF16)
    put_row(small, 13, dot_nt(ones, dn))
    dn = dn.astype(F32)
    put_row(small, 11, dot_nt(ones, (dn * xhat).astype(BF16)))
    dmid = (dout.astype(F32) + norm_bwd(dn, xhat, rstd, cols[0:C, 3:4])).astype(BF16)
    put_row(small, 9, dot_nt(ones, dmid))
    flat[960:1152, :] = dot_nt(res["mixed"][...], dmid[0:128]).astype(BF16)
    dmixed = dot_nn(par["pw"][0], dmid).astype(BF16)
    for h in range(HEADS):
        drel = None
        for p in range(2):
            lanes = slice(128 * p, 128 * p + 128)
            q = res["packed"][DIM * h : DIM * h + DIM, lanes]
            k = res["packed"][C + DIM * h : C + DIM * h + DIM, lanes]
            v = res["packed"][2 * C + DIM * h : 2 * C + DIM * h + DIM, lanes]
            a = res["attn"][p * HEADS + h].astype(F32)
            dm = dmixed[DIM * h : DIM * h + DIM, lanes]
            da = own_window(dot_tn(v, dm), left).astype(BF16).astype(F32)
            ds = a * (da - jnp.sum(da * a, axis=0, keepdims=True))
            drel = ds if drel is None else drel + ds
            wide = stack_windows(ds * SCALE, left)
            dpacked[DIM * h : DIM * h + DIM, lanes] = dot_nn(k, wide).astype(BF16)
            dpacked[C + DIM * h : C + DIM * h + DIM, lanes] = dot_nt(q, wide).astype(BF16)
            dpacked[2 * C + DIM * h : 2 * C + DIM * h + DIM, lanes] = dot_nt(dm, stack_windows(a, left)).astype(BF16)
        rel_sum[h] = drel
    mirror = ((127 - iota((128, 128), 0)) == spread(iota((128, 128), 1))).astype(BF16)
    for h in range(HEADS):
        high, mid, _ = split3(rel_sum[h])
        back = dot_nt(high, mirror) + dot_nt(mid, mirror)
        total = jnp.zeros((8, 256), F32)
        for ky in range(8):
            wide = jnp.concatenate([back[8 * ky : 8 * ky + 8], jnp.zeros((8, 128), F32)], axis=1)
            total = total + pltpu.roll(wide, 121 - SPAN * (7 - ky), 1, stride=1, stride_axis=0)
        total = jnp.sum(total, axis=0, keepdims=True)
        small[24 + h : 25 + h, :] = total[:, 0:128]
        small[32 + h : 33 + h, :] = total[:, 128:256]
    xhat, rstd = norm_fwd(x)
    normed = (xhat * cols[0:C, 0:1] + cols[0:C, 1:2]).astype(BF16)
    for j in range(4):
        flat[C * j : C * j + C, :] = dot_nt(normed, dpacked[128 * j : 128 * j + 128, :]).astype(BF16)
    tail = dot_nt(normed, jnp.concatenate([dpacked[512:576, :], none], axis=0))
    tail = tail + dot_nt(res["mixed"][...], jnp.concatenate([none, dmid[128:192]], axis=0))
    flat[768:960, :] = tail.astype(BF16)
    put_row(small, 4, dot_nt(ones, dpacked[...]))
    dn = dot_nn(par["qw"][0], dpacked[...]).astype(BF16)
    put_row(small, 2, dot_nt(ones, dn))
    dn = dn.astype(F32)
    put_row(small, 0, dot_nt(ones, (dn * xhat).astype(BF16)))
    flat[SMALL : SMALL + 48, :] = small[...].astype(BF16)
    flat[SMALL + 48 : FLAT, :] = jnp.zeros((FLAT - SMALL - 48, 128), BF16)
    return dmid.astype(F32) + norm_bwd(dn, xhat, rstd, cols[0:C, 0:1])


def to_channels(pieces):
    return jnp.concatenate(pieces, axis=0).T[0:C]


def to_tokens(value):
    return jnp.concatenate([value, jnp.zeros((64, TOK), F32)], axis=0).T


def grid_put(grid, tokens):
    for r in range(TILE):
        for wc in range(2):
            at = window_row(r, wc)
            grid[r, 8 * wc : 8 * wc + 8, :] = tokens[at : at + 8]


def grid_get(grid, row_at, col_at):
    pieces = []
    for wr in range(2):
        for wc in range(2):
            for ir in range(8):
                at = col_at + 8 * wc
                pieces.append(grid[row_at + 8 * wr + ir, at : at + 8, :])
    return pieces


def emit_strips(grid, edge, strips, which, row_at, col_at):
    col_out, row_out, corner_out = strips
    for r in range(TILE):
        edge[4 * r : 4 * r + 4, :] = grid[r, col_at : col_at + 4, :]
    col_out[64 * which : 64 * which + 64, :] = edge[:, 0:C].astype(BF16)
    for r in range(4):
        row_out[64 * which + 16 * r : 64 * which + 16 * r + 16, :] = grid[row_at + r, 0:TILE, 0:C].astype(BF16)
    for r in range(4):
        edge[4 * r : 4 * r + 4, :] = grid[row_at + r, col_at : col_at + 4, :]
    corner_out[16 * which : 16 * which + 16, :] = edge[0:16, 0:C].astype(BF16)


def fill_grid(grid, edge, own, strips, which, own_row, own_col, strip_row, strip_col):
    col_in, row_in, corner_in = strips
    for r in range(TILE):
        grid[own_row + r, own_col : own_col + TILE, 0:C] = own[r].astype(F32)
    edge[:, 0:C] = col_in[64 * which : 64 * which + 64, :].astype(F32)
    for r in range(TILE):
        grid[own_row + r, strip_col : strip_col + 4, :] = edge[4 * r : 4 * r + 4, :]
    for r in range(4):
        at = 64 * which + 16 * r
        grid[strip_row + r, own_col : own_col + TILE, 0:C] = row_in[at : at + 16, :].astype(F32)
    edge[0:16, 0:C] = corner_in[16 * which : 16 * which + 16, :].astype(F32)
    for r in range(4):
        grid[strip_row + r, strip_col : strip_col + 4, :] = edge[4 * r : 4 * r + 4, :]


PAR_NAMES = ("ng", "nb", "qw", "qb", "rel", "pw", "pb", "mg", "mb", "uw", "ub", "dw", "db")
RES_NAMES = ("packed", "attn", "mixed", "middle", "hidden", "slope")
RES_SHAPES = ((576, TOK), (12, 64, 128), (C, TOK), (C, TOK), (MLP, TOK), (MLP, TOK))


def first_forward(*refs):
    imagery, cotangent = refs[0:2]
    par = dict(zip(PAR_NAMES, refs[2:15]))
    own, xt = refs[15:17]
    strips = refs[17:20]
    res = dict(zip(RES_NAMES, refs[20:26]))
    grid, edge, vec, table, bias = refs[26:]
    cols = load_columns(vec, par)
    position_bias(par, table, bias)
    for r in range(TILE):
        grid[r, 0:TILE, 0:C] = cotangent[r].astype(F32)
    emit_strips(grid, edge, strips, 1, 0, 0)
    for r in range(TILE):
        grid[r, 0:TILE, 0:C] = imagery[r].astype(F32)
    x = to_channels(grid_get(grid, 0, 0))
    xt[...] = x.astype(BF16)
    out = forward(x, par, cols, bias, res, None)
    grid_put(grid, to_tokens(out.astype(F32)))
    for r in range(TILE):
        own[r] = grid[r, 0:TILE, 0:C].astype(BF16)
    emit_strips(grid, edge, strips, 0, 0, 0)


def second_block(*refs):
    own_in, cotangent = refs[0:2]
    strips_in = refs[2:5]
    par = dict(zip(PAR_NAMES, refs[5:18]))
    out_own, back_own = refs[18:20]
    strips = refs[20:23]
    flat = refs[23]
    grid, edge, vec, table, bias = refs[24:29]
    small, du_ref, dpacked, rel_sum = refs[29:33]
    res = dict(zip(RES_NAMES, refs[33:39]))
    cols = load_columns(vec, par)
    position_bias(par, table, bias)
    last_row = lax.axis_index("rows") == lax.axis_size("rows") - 1
    last_col = lax.axis_index("cols") == lax.axis_size("cols") - 1
    zones = [same_zone(p, last_row, last_col) for p in range(2)]
    fill_grid(grid, edge, own_in, strips_in, 0, 0, 0, 16, 16)
    x = to_channels(grid_get(grid, 4, 4))
    fill_grid(grid, edge, cotangent, strips_in, 1, 0, 0, 16, 16)
    dout = to_channels(grid_get(grid, 4, 4)).astype(BF16)
    out = forward(x, par, cols, bias, res, zones)
    grid_put(grid, to_tokens(out.astype(F32)))
    for r in range(TILE):
        out_own[r] = grid[r, 0:TILE, 0:C].astype(BF16)
    emit_strips(grid, edge, strips, 0, 12, 12)
    dx = backward(dout, x, par, cols, res, flat, small, du_ref, dpacked, rel_sum)
    grid_put(grid, to_tokens(dx))
    for r in range(TILE):
        back_own[r] = grid[r, 0:TILE, 0:C].astype(BF16)
    emit_strips(grid, edge, strips, 1, 12, 12)


def first_backward(*refs):
    out_in, back_in = refs[0:2]
    strips_in = refs[2:5]
    par = dict(zip(PAR_NAMES, refs[5:18]))
    xt = refs[18]
    res = dict(zip(RES_NAMES, refs[19:25]))
    output, grad, flat = refs[25:28]
    grid, edge, vec = refs[28:31]
    small, du_ref, dpacked, rel_sum = refs[31:35]
    cols = load_columns(vec, par)
    fill_grid(grid, edge, out_in, strips_in, 0, 4, 8, 0, 4)
    for r in range(TILE):
        output[r] = grid[r, 4:20, 0:C].astype(BF16)
    fill_grid(grid, edge, back_in, strips_in, 1, 4, 8, 0, 4)
    dout = to_channels(grid_get(grid, 0, 4)).astype(BF16)
    x = xt[...].astype(F32)
    dx = backward(dout, x, par, cols, res, flat, small, du_ref, dpacked, rel_sum)
    grid_put(grid, to_tokens(dx))
    for r in range(TILE):
        grad[r] = grid[r, 0:TILE, 0:C].astype(BF16)


def sum_spread(parts, out):
    n, rows, _ = parts.shape
    total = jnp.zeros((rows, 128), F32)
    for i in range(n):
        total = total + parts[i].astype(F32)
    total = total.astype(BF16)
    for i in range(n):
        out[i] = total


def unpack(one, two, *outs):
    ng, nb, qw, qb, rel, pw, pb, mg, mb, uw, ub, dw, db, small = outs
    factor = outs_factor
    flip = (iota((256, 256), 0) + iota((256, 256), 1) == 255).astype(BF16)
    for b, flat in enumerate((one, two)):

        def rows(at, n):
            return flat[at : at + n, :].astype(F32) * factor

        for j in range(4):
            qw[b, :, 128 * j : 128 * j + 128] = rows(C * j, C)
        tail = rows(768, C)
        qw[b, :, 512:576] = tail[:, 0:64]
        pw[b, :, 128:192] = pltpu.roll(tail, 64, 1)[:, 0:64]
        pw[b, :, 0:128] = rows(960, C)
        for j in range(6):
            uw[b, :, 128 * j : 128 * j + 128] = rows(1152 + C * j, C)
        dw[b, :, 0:128] = rows(2304, MLP)
        tail = rows(3072, 384)
        dw[b, 0:384, 128:192] = tail[:, 0:64]
        dw[b, 384:768, 128:192] = pltpu.roll(tail, 64, 1)[:, 0:64]
        small[...] = rows(SMALL, 48)
        for at, ref in ((0, ng), (2, nb), (4, qb), (9, pb), (11, mg), (13, mb), (15, ub), (21, db)):
            n = ref.shape[-1]
            for i in range(0, n, 128):
                w = min(128, n - i)
                ref[b : b + 1, i : i + w] = small[at + i // 128 : at + i // 128 + 1, 0:w]
        table = jnp.concatenate([flat[SMALL + 24 : SMALL + 32, :], flat[SMALL + 32 : SMALL + 40, :]], axis=1)
        rel[b] = (dot_nn(table, flip) * factor)[0:HEADS, 0 : SPAN * SPAN]


outs_factor = float(128 * 256) ** (-0.5)


def whole(shape):
    zeros = (0,) * len(shape)
    return pl.BlockSpec(shape, lambda *_: zeros)


def block_of(array, b):
    if array.ndim == 2:
        array = array.reshape(2, 1, array.shape[-1])
    tail = (0,) * (array.ndim - 1)
    return array, pl.BlockSpec((1,) + array.shape[1:], lambda *_: (b,) + tail)


def call(kernel, name, args, params, b, more, outs, scratch, flops):
    specs = [whole(a.shape) for a in args]
    values = list(args)
    for p in params:
        value, spec = block_of(p, b)
        values.append(value)
        specs.append(spec)
    for a in more:
        values.append(a)
        specs.append(whole(a.shape))
    return pl.pallas_call(
        kernel,
        grid=(1,),
        in_specs=specs,
        out_specs=[whole(o.shape) for o in outs],
        out_shape=outs,
        scratch_shapes=scratch,
        name=name,
        cost_estimate=pl.CostEstimate(flops=flops, transcendentals=0, bytes_accessed=4000000),
    )(*values)


def shaped(shape, dtype=BF16):
    return jax.ShapeDtypeStruct(shape, dtype)


def exchange(strips, step):
    n_rows = lax.axis_size("rows")
    n_cols = lax.axis_size("cols")
    col_strip, row_strip, corner = strips
    along = [(c, (c + step) % n_cols) for c in range(n_cols)]
    down = [(r, (r + step) % n_rows) for r in range(n_rows)]
    both = [
        (r * n_cols + c, ((r + step) % n_rows) * n_cols + (c + step) % n_cols)
        for r in range(n_rows)
        for c in range(n_cols)
    ]
    return [
        lax.ppermute(col_strip, "cols", along),
        lax.ppermute(row_strip, "rows", down),
        lax.ppermute(corner, ("rows", "cols"), both),
    ]


def reduce_flat(flat):
    axes = ("rows", "cols")
    n = lax.axis_size("rows") * lax.axis_size("cols")
    parts = lax.all_to_all(flat.reshape(n, FLAT // n, 128), axes, 0, 0, tiled=True)
    spread_out = pl.pallas_call(sum_spread, out_shape=shaped(parts.shape), name="sum_spread")(parts)
    return lax.all_to_all(spread_out, axes, 0, 0, tiled=True).reshape(FLAT, 128)


def per_device(imagery, cotangent, *params):
    tile = (TILE, TILE, C)
    strips = [shaped((128, C)), shaped((128, C)), shaped((32, C))]
    residuals = [shaped(s) for s in RES_SHAPES]
    grid = pltpu.VMEM((24, 24, 256), F32)
    edge = pltpu.VMEM((64, 256), F32)
    vec = pltpu.VMEM((128, MLP), F32)
    tables = [pltpu.VMEM((8, 256), F32), pltpu.VMEM((HEADS, 64, 128), F32)]
    work = [
        pltpu.VMEM((48, 128), F32),
        pltpu.VMEM((MLP, TOK), BF16),
        pltpu.VMEM((576, TOK), BF16),
        pltpu.VMEM((HEADS, 64, 128), F32),
    ]
    one = call(
        first_forward,
        "first_forward",
        (imagery, cotangent),
        params,
        0,
        (),
        [shaped(tile), shaped((C, TOK))] + strips + residuals,
        [grid, edge, vec] + tables,
        5 * 10**9,
    )
    own, xt, res = one[0], one[1], one[5:]
    got = exchange(one[2:5], -1)
    two = call(
        second_block,
        "second_block",
        (own, cotangent, *got),
        params,
        1,
        (),
        [shaped(tile), shaped(tile)] + strips + [shaped((FLAT, 128))],
        [grid, edge, vec] + tables + work + [pltpu.VMEM(s, BF16) for s in RES_SHAPES],
        10**10,
    )
    got = exchange(two[2:5], 1)
    output, grad, flat_one = call(
        first_backward,
        "first_backward",
        (two[0], two[1], *got),
        params,
        0,
        (xt, *res),
        [shaped(tile), shaped(tile), shaped((FLAT, 128))],
        [grid, edge, vec] + work,
        5 * 10**9,
    )
    sum_two = reduce_flat(two[5])
    sum_one = reduce_flat(flat_one)
    grads = pl.pallas_call(
        unpack,
        out_shape=[shaped(p.shape, F32) for p in params],
        scratch_shapes=[pltpu.VMEM((48, 128), F32)],
        name="unpack",
    )(sum_one, sum_two)
    return (output, grad, *grads)


def solution(mesh):
    tile = P("rows", "cols", None)
    return jax.shard_map(
        per_device,
        mesh=mesh,
        in_specs=(tile, tile) + (P(),) * 13,
        out_specs=(tile, tile) + (P(),) * 13,
        check_vma=False,
    )
```

profile of v0, /device:TPU:1, one launch (start us, length us, event | category | flops | bytes accessed | tf_op | source)
XLA Modules:
  0.0 160.2 jit_solution(5615377416859293384)
XLA Ops:
  8.2 1.3 reshape.69.refs_5_.refs_8_
  9.5 1.3 reshape.88.refs_12_.refs_15_
  10.8 1.3 copy.30.refs_6_.refs_9_
  12.1 2.2 %copy.31.refs_13_.refs_16_ = bf16[2,768,192]{2,1,0:T(8,128)(2,1)} copy(bf16[2,768,192]{1,2,0:T(8,128)(2,1)} %param.28) | data formatting | bytes 1179648 | tf_op args[13]
  14.3 5.6 %first_forward.1 = (bf16[16,16,192]{2,1,0:T(8,128)(2,1)}, bf16[192,256]{1,0:T(8,128)(2,1)}, bf16[128,192]{1,0:T(8,128)(2,1)}, bf16[128,192]{1,0:T(8,128)(2,1)}, ...) custom-call(bf16[16,16,192]{2,1,0:T(8,128)(2,1)} %refs_0_.1, ...), custom_call_target="tpu_custom_call" | custom-call | flops 5000000000 | bytes 4000000 | tf_op jit(solution)/shard_map/first_forward/pallas_call | solution.py:427
  19.9 1.4 collective-permute-start
  21.3 4.9 %collective-permute-start.1 = (bf16[128,192]{1,0:T(8,128)(2,1)}, bf16[128,192]{1,0:T(8,128)(2,1)S(1)}, u32[]{:S(2)}, u32[]{:S(2)}) collective-permute-start(bf16[128,192]{1,0:T(8,128)(2,1)} %get-tuple-element.50), channel_id=1, source_target_pairs={{0,112},{16,0},{32,16},{48,32},{64,48},{80,64},{96,80},{112,96},{1... | collective-permute-start | bytes 147464 | tf_op jit(solution)/shard_map/ppermute | solution.py:456
  26.2 5.2 %collective-permute-start.2 = (bf16[32,192]{1,0:T(8,128)(2,1)}, bf16[32,192]{1,0:T(8,128)(2,1)S(1)}, u32[]{:S(2)}, u32[]{:S(2)}) collective-permute-start(bf16[32,192]{1,0:T(8,128)(2,1)} %get-tuple-element.51), channel_id=1, source_target_pairs={{0,127},{1,112},{2,113},{3,114},{4,115},{5,116},{6,117},{7,118},{8... | collective-permute-start | bytes 36872 | tf_op jit(solution)/shard_map/ppermute | solution.py:457
  33.1 10.9 %second_block.1 = (bf16[16,16,192]{2,1,0:T(8,128)(2,1)}, bf16[16,16,192]{2,1,0:T(8,128)(2,1)}, bf16[128,192]{1,0:T(8,128)(2,1)}, bf16[128,192]{1,0:T(8,128)(2,1)...) custom-call(bf16[16,16,192]{2,1,0:T(8,128)(2,1)} %get-tuple-element.48.refs_0_, bf16[16,16,192]{2,1,0:T(8,128)(2,1)} %refs_1_.3, ...), custom_call_target="tpu_custom_call" | custom-call | flops 10000000000 | bytes 4000000 | tf_op jit(solution)/shard_map/second_block/pallas_call | solution.py:427
  44.0 7.9 %all-to-all-start.2 = ((bf16[128,32,128]{2,1,0:T(8,128)(2,1)}), bf16[128,32,128]{2,1,0:T(8,128)(2,1)S(1)}, u32[]{:S(2)}, u32[]{:S(2)}) async-start(bf16[128,32,128]{2,1,0:T(8,128)(2,1)} %bitcast.6), calls=%async_computation.2 | async-start | bytes 2097152 | tf_op jit(solution)/shard_map/all_to_all | solution.py:464
  52.0 3.2 %collective-permute-start.3 = (bf16[128,192]{1,0:T(8,128)(2,1)S(1)}, bf16[128,192]{1,0:T(8,128)(2,1)S(1)}, u32[]{:S(2)}, u32[]{:S(2)}) collective-permute-start(bf16[128,192]{1,0:T(8,128)(2,1)S(1)} %copy-done.6), channel_id=1, source_target_pairs={{0,1},{1,2},{2,3},{3,4},{4,5},{5,6},{6,7},{7,8},{8,9},{9,10},{10,1... | collective-permute-start | bytes 147464 | tf_op jit(solution)/shard_map/ppermute | solution.py:455
  55.5 1.5 collective-permute-start.5
  57.1 13.3 %collective-permute-done.5.refs_4_ = bf16[32,192]{1,0:T(8,128)(2,1)S(1)} collective-permute-done((bf16[32,192]{1,0:T(8,128)(2,1)S(1)}, bf16[32,192]{1,0:T(8,128)(2,1)S(1)}, u32[]{:S(2)}, u32[]{:S(2)}) %collective-permute-start.5) | collective-permute-done | bytes 12320 | tf_op jit(solution)/shard_map/ppermute | solution.py:457
  71.1 7.9 %first_backward.1 = (bf16[16,16,192]{2,1,0:T(8,128)(2,1)}, bf16[16,16,192]{2,1,0:T(8,128)(2,1)}, bf16[4096,128]{1,0:T(8,128)(2,1)}) custom-call(bf16[16,16,192]{2,1,0:T(8,128)(2,1)} %get-tuple-element.52.refs_0_, bf16[16,16,192]{2,1,0:T(8,128)(2,1)} %get-tuple-element.53.refs_1_, bf16[128,192]{1,0:T(8,128)(2,1)} %copy-done.3, bf16[128,192]{1,0:T(8,128)(2,1)} %copy-done.4, ...), custom_call_target="tpu_custom_call" | custom-call | flops 5000000000 | bytes 4000000 | tf_op jit(solution)/shard_map/first_backward/pallas_call | solution.py:427
  78.9 6.2 %all-to-all-start = ((bf16[128,32,128]{2,1,0:T(8,128)(2,1)}), bf16[128,32,128]{2,1,0:T(8,128)(2,1)S(1)}, u32[]{:S(2)}, u32[]{:S(2)}) async-start(bf16[128,32,128]{2,1,0:T(8,128)(2,1)} %bitcast.7), calls=%async_computation | async-start | bytes 2097152 | tf_op jit(solution)/shard_map/all_to_all | solution.py:464
  85.1 2.5 %sum_spread.3 = bf16[128,32,128]{2,1,0:T(8,128)(2,1)} custom-call(bf16[128,32,128]{2,1,0:T(8,128)(2,1)} %copy-done), custom_call_target="tpu_custom_call" | custom-call | tf_op jit(solution)/shard_map/sum_spread/pallas_call | solution.py:465
  87.6 16.5 %all-to-all-done.parts = bf16[128,32,128]{2,1,0:T(8,128)(2,1)S(1)} async-done(((bf16[128,32,128]{2,1,0:T(8,128)(2,1)}), bf16[128,32,128]{2,1,0:T(8,128)(2,1)S(1)}, u32[]{:S(2)}, u32[]{:S(2)}) %all-to-all-start) | async-done | bytes 1048608 | tf_op jit(solution)/shard_map/all_to_all | solution.py:464
  104.1 4.6 %all-to-all-start.3 = ((bf16[128,32,128]{2,1,0:T(8,128)(2,1)}), bf16[128,32,128]{2,1,0:T(8,128)(2,1)S(1)}, u32[]{:S(2)}, u32[]{:S(2)}) async-start(bf16[128,32,128]{2,1,0:T(8,128)(2,1)} %sum_spread.3), calls=%async_computation.3 | async-start | bytes 2097152 | tf_op jit(solution)/shard_map/all_to_all | solution.py:466
  108.7 2.4 %sum_spread.2 = bf16[128,32,128]{2,1,0:T(8,128)(2,1)} custom-call(bf16[128,32,128]{2,1,0:T(8,128)(2,1)} %copy-done.2), custom_call_target="tpu_custom_call" | custom-call | tf_op jit(solution)/shard_map/sum_spread/pallas_call | solution.py:465
  111.1 16.6 %all-to-all-done.3 = bf16[128,32,128]{2,1,0:T(8,128)(2,1)S(1)} async-done(((bf16[128,32,128]{2,1,0:T(8,128)(2,1)}), bf16[128,32,128]{2,1,0:T(8,128)(2,1)S(1)}, u32[]{:S(2)}, u32[]{:S(2)}) %all-to-all-start.3) | async-done | bytes 1048608 | tf_op jit(solution)/shard_map/all_to_all | solution.py:466
  127.7 24.6 %all_to_all.20 = bf16[128,32,128]{2,1,0:T(8,128)(2,1)} all-to-all(bf16[128,32,128]{2,1,0:T(8,128)(2,1)} %sum_spread.2), channel_id=1, replica_groups=mesh['rows'=8,'cols'=16] {'rows','cols'}, dimensions={0} | all-to-all | bytes 2097152 | tf_op jit(solution)/shard_map/all_to_all | solution.py:466
  152.3 3.7 %unpack.1 = (f32[2,192]{1,0:T(2,128)}, f32[2,192]{1,0:T(2,128)}, f32[2,192,576]{2,1,0:T(8,128)}, f32[2,576]{1,0:T(2,128)}, f32[2,6,225]{2,1,0:T(8,128)}, /*index...) custom-call(bf16[4096,128]{1,0:T(8,128)(2,1)} %bitcast.5, ...), custom_call_target="tpu_custom_call" | custom-call | tf_op jit(solution)/shard_map/unpack/pallas_call | solution.py:521
  156.0 1.3 copy.36
  157.3 2.9 %copy.37 = f32[2,768,192]{1,2,0:T(8,128)} copy(f32[2,768,192]{2,1,0:T(8,128)} %get-tuple-element.94) | data formatting | bytes 2359296
  (37 shorter events, 10.4 us)
Async XLA Ops:
  19.9 12.6 %collective-permute-start = (bf16[128,192]{1,0:T(8,128)(2,1)}, bf16[128,192]{1,0:T(8,128)(2,1)S(1)}, u32[]{:S(2)}, u32[]{:S(2)}) collective-permute-start(bf16[128,192]{1,0:T(8,128)(2,1)} %get-tuple-element.49), channel_id=1, source_target_pairs={{0,15},{1,0},{2,1},{3,2},{4,3},{5,4},{6,5},{7,6},{8,7},{9,8},{10,9... | collective-permute-start | bytes 147464 | tf_op jit(solution)/shard_map/ppermute | solution.py:455
  21.3 11.1 %collective-permute-start.1 = (bf16[128,192]{1,0:T(8,128)(2,1)}, bf16[128,192]{1,0:T(8,128)(2,1)S(1)}, u32[]{:S(2)}, u32[]{:S(2)}) collective-permute-start(bf16[128,192]{1,0:T(8,128)(2,1)} %get-tuple-element.50), channel_id=1, source_target_pairs={{0,112},{16,0},{32,16},{48,32},{64,48},{80,64},{96,80},{112,96},{1... | collective-permute-start | bytes 147464 | tf_op jit(solution)/shard_map/ppermute | solution.py:456
  26.2 6.2 %collective-permute-start.2 = (bf16[32,192]{1,0:T(8,128)(2,1)}, bf16[32,192]{1,0:T(8,128)(2,1)S(1)}, u32[]{:S(2)}, u32[]{:S(2)}) collective-permute-start(bf16[32,192]{1,0:T(8,128)(2,1)} %get-tuple-element.51), channel_id=1, source_target_pairs={{0,127},{1,112},{2,113},{3,114},{4,115},{5,116},{6,117},{7,118},{8... | collective-permute-start | bytes 36872 | tf_op jit(solution)/shard_map/ppermute | solution.py:457
  32.5 0.6 copy-start.11
  32.5 0.6 copy-start.7
  32.5 0.6 copy-start.8
  44.0 8.0 %copy-start.6 = (bf16[128,192]{1,0:T(8,128)(2,1)S(1)}, bf16[128,192]{1,0:T(8,128)(2,1)}, u32[]{:S(2)}) copy-start(bf16[128,192]{1,0:T(8,128)(2,1)} %get-tuple-element.54) | copy-start | bytes 147460
  44.0 11.2 %copy-start.5 = (bf16[128,192]{1,0:T(8,128)(2,1)S(1)}, bf16[128,192]{1,0:T(8,128)(2,1)}, u32[]{:S(2)}) copy-start(bf16[128,192]{1,0:T(8,128)(2,1)} %get-tuple-element.55) | copy-start | bytes 147460
  44.0 11.5 %copy-start.10 = (bf16[32,192]{1,0:T(8,128)(2,1)S(1)}, bf16[32,192]{1,0:T(8,128)(2,1)}, u32[]{:S(2)}) copy-start(bf16[32,192]{1,0:T(8,128)(2,1)} %get-tuple-element.56) | copy-start | bytes 36868
  44.0 34.9 %all-to-all-start.2 = ((bf16[128,32,128]{2,1,0:T(8,128)(2,1)}), bf16[128,32,128]{2,1,0:T(8,128)(2,1)S(1)}, u32[]{:S(2)}, u32[]{:S(2)}) async-start(bf16[128,32,128]{2,1,0:T(8,128)(2,1)} %bitcast.6), calls=%async_computation.2 | async-start | bytes 2097152 | tf_op jit(solution)/shard_map/all_to_all | solution.py:464
  52.0 18.3 %collective-permute-start.3 = (bf16[128,192]{1,0:T(8,128)(2,1)S(1)}, bf16[128,192]{1,0:T(8,128)(2,1)S(1)}, u32[]{:S(2)}, u32[]{:S(2)}) collective-permute-start(bf16[128,192]{1,0:T(8,128)(2,1)S(1)} %copy-done.6), channel_id=1, source_target_pairs={{0,1},{1,2},{2,3},{3,4},{4,5},{5,6},{6,7},{7,8},{8,9},{9,10},{10,1... | collective-permute-start | bytes 147464 | tf_op jit(solution)/shard_map/ppermute | solution.py:455
  55.2 15.2 %collective-permute-start.4 = (bf16[128,192]{1,0:T(8,128)(2,1)S(1)}, bf16[128,192]{1,0:T(8,128)(2,1)S(1)}, u32[]{:S(2)}, u32[]{:S(2)}) collective-permute-start(bf16[128,192]{1,0:T(8,128)(2,1)S(1)} %copy-done.5), channel_id=1, source_target_pairs={{0,16},{16,32},{32,48},{48,64},{64,80},{80,96},{96,112},{112,0},{1... | collective-permute-start | bytes 147464 | tf_op jit(solution)/shard_map/ppermute | solution.py:456
  55.5 14.8 %collective-permute-start.5 = (bf16[32,192]{1,0:T(8,128)(2,1)S(1)}, bf16[32,192]{1,0:T(8,128)(2,1)S(1)}, u32[]{:S(2)}, u32[]{:S(2)}) collective-permute-start(bf16[32,192]{1,0:T(8,128)(2,1)S(1)} %copy-done.10), channel_id=1, source_target_pairs={{0,17},{1,18},{2,19},{3,20},{4,21},{5,22},{6,23},{7,24},{8,25},{9,... | collective-permute-start | bytes 36872 | tf_op jit(solution)/shard_map/ppermute | solution.py:457
  70.3 0.6 copy-start.9
  70.3 0.6 copy-start.3
  70.4 0.6 copy-start.4
  78.9 6.2 %copy-start = (bf16[128,32,128]{2,1,0:T(8,128)(2,1)}, bf16[128,32,128]{2,1,0:T(8,128)(2,1)S(1)}, u32[]{:S(2)}) copy-start(bf16[128,32,128]{2,1,0:T(8,128)(2,1)S(1)} %all-to-all-done.2.parts) | copy-start | bytes 3145732
  78.9 25.1 %all-to-all-start = ((bf16[128,32,128]{2,1,0:T(8,128)(2,1)}), bf16[128,32,128]{2,1,0:T(8,128)(2,1)S(1)}, u32[]{:S(2)}, u32[]{:S(2)}) async-start(bf16[128,32,128]{2,1,0:T(8,128)(2,1)} %bitcast.7), calls=%async_computation | async-start | bytes 2097152 | tf_op jit(solution)/shard_map/all_to_all | solution.py:464
  104.0 4.6 %copy-start.2 = (bf16[128,32,128]{2,1,0:T(8,128)(2,1)}, bf16[128,32,128]{2,1,0:T(8,128)(2,1)S(1)}, u32[]{:S(2)}) copy-start(bf16[128,32,128]{2,1,0:T(8,128)(2,1)S(1)} %all-to-all-done.parts) | copy-start | bytes 3145732
  104.1 23.7 %all-to-all-start.3 = ((bf16[128,32,128]{2,1,0:T(8,128)(2,1)}), bf16[128,32,128]{2,1,0:T(8,128)(2,1)S(1)}, u32[]{:S(2)}, u32[]{:S(2)}) async-start(bf16[128,32,128]{2,1,0:T(8,128)(2,1)} %sum_spread.3), calls=%async_computation.3 | async-start | bytes 2097152 | tf_op jit(solution)/shard_map/all_to_all | solution.py:466
  127.7 24.6 %copy-start.1 = (bf16[128,32,128]{2,1,0:T(8,128)(2,1)}, bf16[128,32,128]{2,1,0:T(8,128)(2,1)S(1)}, u32[]{:S(2)}) copy-start(bf16[128,32,128]{2,1,0:T(8,128)(2,1)S(1)} %all-to-all-done.3) | copy-start | bytes 3145732
where the time goes:
time: 161 us; the launch traced here: 160 us
  waiting for transfers between devices  47.6 us (30%)
  starting transfers between devices  35.2 us (22%)
  Pallas kernels  33 us (20%)
  blocking collectives  24.6 us (15%)
  local copies, waits for them, and re-layouts  19.1 us (12%)
    all_to_all x1, blocking collectives, reduce_flat(): return lax.all_to_all(spread_out, axes, 0, 0, tiled=True).reshape(FLAT, 128)  24.6 us
    pallas_call x3, Pallas kernels, call(): pl.pallas_call(kernel, grid=(1,), in_specs=specs, out_specs=[whole(o.shap...  24.3 us
    all_to_all x1, waiting for transfers between devices, reduce_flat(): return lax.all_to_all(spread_out, axes, 0, 0, tiled=True).reshape(FLAT, 128)  16.6 us
    all_to_all x2, waiting for transfers between devices, reduce_flat(): lax.all_to_all(flat.reshape(n, FLAT // n, 128), axes, 0, 0, tiled=True)  16.5 us
    ppermute x2, waiting for transfers between devices, exchange(): lax.ppermute(corner, ('rows', 'cols'), both)  14.3 us
    all_to_all x2, starting transfers between devices, reduce_flat(): lax.all_to_all(flat.reshape(n, FLAT // n, 128), axes, 0, 0, tiled=True)  14.1 us
    reshape x8, local copies, waits for them, and re-layouts, block_of(): array = array.reshape(2, 1, array.shape[-1])  10.1 us
    unnamed x28, local copies, waits for them, and re-layouts  9 us
  transfers between devices with their start and end apart: 9, of which 5 were waited for; matrix products, arithmetic and copies ran while one was open for 0% of the time, Pallas kernels for 8%

commit v1 on v0

v1 whole, which is shorter than its diff:
```python
import functools

import jax
import jax.numpy as jnp
from jax import lax
from jax.experimental import pallas as pl
from jax.experimental.pallas import tpu as pltpu
from jax.sharding import PartitionSpec as P


F32 = jnp.float32
BF16 = jnp.bfloat16
C = 192
HEADS = 6
DIM = 32
MLP = 768
TILE = 16
TOK = TILE * TILE
SPAN = 15
SCALE = DIM**-0.5
EPSILON = 1e-05
FLAT = 3584
SMALL = 3456
MASKED = -1e30


def dot_tn(a, b):
    return lax.dot_general(a, b, (((0,), (0,)), ((), ())), preferred_element_type=F32)


def dot_nn(a, b):
    return lax.dot_general(a, b, (((1,), (0,)), ((), ())), preferred_element_type=F32)


def dot_nt(a, b):
    return lax.dot_general(a, b, (((1,), (1,)), ((), ())), preferred_element_type=F32)


def iota(shape, dim):
    return lax.broadcasted_iota(jnp.int32, shape, dim)


def split3(value):
    high = value.astype(BF16)
    rest = value - high.astype(F32)
    mid = rest.astype(BF16)
    return high, mid, (rest - mid.astype(F32)).astype(BF16)


def window_row(r, wc):
    return ((r // 8) * 2 + wc) * 64 + (r % 8) * 8


def halves():
    return iota((64, 128), 1) < 64


def stack_windows(value, left):
    zero = jnp.zeros_like(value)
    return jnp.concatenate([jnp.where(left, value, zero), jnp.where(left, zero, value)], axis=0).astype(BF16)


def own_window(full, left):
    return jnp.where(left, full[:64], full[64:])


def norm_fwd(x):
    center = x - jnp.mean(x, axis=0, keepdims=True)
    rstd = lax.rsqrt(jnp.mean(center * center, axis=0, keepdims=True) + EPSILON)
    return center * rstd, rstd


def norm_bwd(dn, xhat, rstd, gain):
    dxh = dn * gain
    along = jnp.mean(dxh * xhat, axis=0, keepdims=True)
    return rstd * (dxh - jnp.mean(dxh, axis=0, keepdims=True) - xhat * along)


def spread(lane_q):
    q = lane_q % 64
    return (q // 8) * SPAN + q % 8


VEC_NAMES = ("ng", "nb", "pb", "mg", "mb", "db", "qb", "ub")


def load_columns(vec, par, b):
    for i, name in enumerate(VEC_NAMES):
        n = par[name].shape[-1]
        vec[i : i + 1, 0:n] = par[name][b : b + 1, :]
    return vec[...].T


def position_bias(par, b, table, bias):
    table[...] = jnp.zeros((8, 256), F32)
    for h in range(HEADS):
        table[h : h + 1, 0 : SPAN * SPAN] = par["rel"][h, b : b + 1, :]
    select = (iota((128, 128), 0) == spread(iota((128, 128), 1))).astype(BF16)
    for h in range(HEADS):
        row = jnp.broadcast_to(table[h : h + 1, :], (8, 256))
        rows = []
        for ky in range(8):
            shift = (249 - SPAN * (7 - ky)) % 256
            rows.append(pltpu.roll(row, shift, 1, stride=1, stride_axis=0)[:, 0:128])
        high, mid, low = split3(jnp.concatenate(rows, axis=0))
        bias[h] = dot_nn(high, select) + (dot_nn(mid, select) + dot_nn(low, select))


def same_zone(p, last_row, last_col):
    k = iota((64, 128), 0)
    lane = iota((64, 128), 1)
    q = lane % 64
    rows = ((q // 8) < 4) == ((k // 8) < 4)
    cols = ((q % 8) < 4) == ((k % 8) < 4)
    keep = jnp.logical_or(cols, jnp.logical_or(lane < 64, jnp.logical_not(last_col)))
    if p == 1:
        keep = jnp.logical_and(keep, jnp.logical_or(rows, jnp.logical_not(last_row)))
    return keep


def forward(x, par, need, cols, bias, res, zones, keep):
    left = halves()
    xhat, _ = norm_fwd(x)
    normed = (xhat * cols[0:C, 0:1] + cols[0:C, 1:2]).astype(BF16)
    need("qw")
    res["packed"][...] = (dot_tn(par["qw"][...], normed) + cols[0:576, 6:7]).astype(BF16)
    for p in range(2):
        lanes = slice(128 * p, 128 * p + 128)
        for h in range(HEADS):
            q = res["packed"][DIM * h : DIM * h + DIM, lanes]
            k = res["packed"][C + DIM * h : C + DIM * h + DIM, lanes]
            v = res["packed"][2 * C + DIM * h : 2 * C + DIM * h + DIM, lanes]
            s = own_window(dot_tn(k, q), left) * SCALE + bias[h]
            if zones is not None:
                s = jnp.where(zones[p], s, MASKED)
            e = jnp.exp(s - jnp.max(s, axis=0, keepdims=True))
            a = e * (1.0 / jnp.sum(e, axis=0, keepdims=True))
            res["attn"][p * HEADS + h] = a.astype(BF16)
            res["mixed"][DIM * h : DIM * h + DIM, lanes] = dot_nn(v, stack_windows(a, left)).astype(BF16)
    keep("packed")
    need("pw")
    middle = x + dot_tn(par["pw"][...], res["mixed"][...]) + cols[0:C, 2:3]
    res["middle"][...] = middle.astype(BF16)
    middle = res["middle"][...].astype(F32)
    xhat, _ = norm_fwd(middle)
    normed = (xhat * cols[0:C, 3:4] + cols[0:C, 4:5]).astype(BF16)
    keep("attn", "mixed")
    need("uw")
    for i in range(0, MLP, 128):
        u = dot_tn(par["uw"][:, i : i + 128], normed) + cols[i : i + 128, 7:8]
        half = 0.5 + 0.5 * lax.erf(u * (0.5**0.5))
        res["hidden"][i : i + 128, :] = (u * half).astype(BF16)
        res["slope"][i : i + 128, :] = (half + u * (jnp.exp(-0.5 * u * u) * 0.3989422804014327)).astype(BF16)
    keep("middle")
    need("dw")
    out = middle + dot_nn(par["dw"][...], res["hidden"][...]) + cols[0:C, 5:6]
    return out.astype(BF16)


def put_row(small, at, row):
    n = row.shape[-1]
    for i in range(0, n, 128):
        w = min(128, n - i)
        small[at + i // 128 : at + i // 128 + 1, 0:w] = row[0:1, i : i + w]


def put_pairs(flat, at, lhs, rhs, n):
    for i in range(0, n, 256):
        wide = dot_nt(lhs, rhs[i : i + 256, :]).astype(BF16)
        for j in range(0, 256, 128):
            first = at + C * ((i + j) // 128)
            flat[first : first + C, :] = wide[:, j : j + 128]


def backward(dout, x, par, need, cols, res, flat, small, du_ref, dpacked, rel_sum):
    left = halves()
    ones = jnp.ones((8, TOK), BF16)
    none = jnp.zeros((64, TOK), BF16)
    small[...] = jnp.zeros(small.shape, F32)
    put_row(small, 21, dot_nt(ones, dout))
    need("dw", "slope")
    for i in range(0, MLP, 128):
        dh = dot_tn(par["dw"][:, i : i + 128], dout).astype(BF16).astype(F32)
        du = (dh * res["slope"][i : i + 128, :].astype(F32)).astype(BF16)
        du_ref[i : i + 128, :] = du
    need("middle", "uw")
    middle = res["middle"][...].astype(F32)
    xhat, rstd = norm_fwd(middle)
    normed = (xhat * cols[0:C, 3:4] + cols[0:C, 4:5]).astype(BF16)
    put_pairs(flat, 1152, normed, du_ref, MLP)
    need("hidden")
    put_pairs(flat, 2304, dout, res["hidden"], MLP)
    put_row(small, 15, dot_nt(ones, du_ref[...]))
    dn = dot_nn(par["uw"][...], du_ref[...]).astype(BF16)
    put_row(small, 13, dot_nt(ones, dn))
    dn = dn.astype(F32)
    put_row(small, 11, dot_nt(ones, (dn * xhat).astype(BF16)))
    dmid = (dout.astype(F32) + norm_bwd(dn, xhat, rstd, cols[0:C, 3:4])).astype(BF16)
    need("pw", "mixed")
    put_row(small, 9, dot_nt(ones, dmid))
    flat[960:1152, :] = dot_nt(res["mixed"][...], dmid[0:128]).astype(BF16)
    dmixed = dot_nn(par["pw"][...], dmid).astype(BF16)
    need("packed", "attn")
    for h in range(HEADS):
        drel = None
        for p in range(2):
            lanes = slice(128 * p, 128 * p + 128)
            q = res["packed"][DIM * h : DIM * h + DIM, lanes]
            k = res["packed"][C + DIM * h : C + DIM * h + DIM, lanes]
            v = res["packed"][2 * C + DIM * h : 2 * C + DIM * h + DIM, lanes]
            a = res["attn"][p * HEADS + h].astype(F32)
            dm = dmixed[DIM * h : DIM * h + DIM, lanes]
            da = own_window(dot_tn(v, dm), left).astype(BF16).astype(F32)
            ds = a * (da - jnp.sum(da * a, axis=0, keepdims=True))
            drel = ds if drel is None else drel + ds
            wide = stack_windows(ds * SCALE, left)
            dpacked[DIM * h : DIM * h + DIM, lanes] = dot_nn(k, wide).astype(BF16)
            dpacked[C + DIM * h : C + DIM * h + DIM, lanes] = dot_nt(q, wide).astype(BF16)
            dpacked[2 * C + DIM * h : 2 * C + DIM * h + DIM, lanes] = dot_nt(dm, stack_windows(a, left)).astype(BF16)
        rel_sum[h] = drel
    mirror = ((127 - iota((128, 128), 0)) == spread(iota((128, 128), 1))).astype(BF16)
    for h in range(HEADS):
        high, mid, _ = split3(rel_sum[h])
        back = dot_nt(high, mirror) + dot_nt(mid, mirror)
        total = jnp.zeros((8, 256), F32)
        for ky in range(8):
            wide = jnp.concatenate([back[8 * ky : 8 * ky + 8], jnp.zeros((8, 128), F32)], axis=1)
            total = total + pltpu.roll(wide, 121 - SPAN * (7 - ky), 1, stride=1, stride_axis=0)
        total = jnp.sum(total, axis=0, keepdims=True)
        small[24 + h : 25 + h, :] = total[:, 0:128]
        small[32 + h : 33 + h, :] = total[:, 128:256]
    xhat, rstd = norm_fwd(x)
    normed = (xhat * cols[0:C, 0:1] + cols[0:C, 1:2]).astype(BF16)
    put_pairs(flat, 0, normed, dpacked, 512)
    tail = dot_nt(normed, jnp.concatenate([dpacked[512:576, :], none], axis=0))
    tail = tail + dot_nt(res["mixed"][...], jnp.concatenate([none, dmid[128:192]], axis=0))
    flat[768:960, :] = tail.astype(BF16)
    put_row(small, 4, dot_nt(ones, dpacked[...]))
    need("qw")
    dn = dot_nn(par["qw"][...], dpacked[...]).astype(BF16)
    put_row(small, 2, dot_nt(ones, dn))
    dn = dn.astype(F32)
    put_row(small, 0, dot_nt(ones, (dn * xhat).astype(BF16)))
    flat[SMALL : SMALL + 48, :] = small[...].astype(BF16)
    flat[SMALL + 48 : FLAT, :] = jnp.zeros((FLAT - SMALL - 48, 128), BF16)
    return dmid.astype(F32) + norm_bwd(dn, xhat, rstd, cols[0:C, 0:1])


def to_channels(pieces):
    return jnp.concatenate(pieces, axis=0).T[0:C]


def to_tokens(value):
    return jnp.concatenate([value, jnp.zeros((64, TOK), F32)], axis=0).T


def grid_put(grid, tokens):
    for r in range(TILE):
        for wc in range(2):
            at = window_row(r, wc)
            grid[r, 8 * wc : 8 * wc + 8, :] = tokens[at : at + 8]


def grid_get(grid, row_at, col_at):
    pieces = []
    for wr in range(2):
        for wc in range(2):
            for ir in range(8):
                at = col_at + 8 * wc
                pieces.append(grid[row_at + 8 * wr + ir, at : at + 8, :])
    return pieces


def emit_strips(grid, edge, strips, which, row_at, col_at):
    col_out, row_out, corner_out = strips
    for r in range(TILE):
        edge[4 * r : 4 * r + 4, :] = grid[r, col_at : col_at + 4, :]
    col_out[64 * which : 64 * which + 64, :] = edge[:, 0:C].astype(BF16)
    for r in range(4):
        row_out[64 * which + 16 * r : 64 * which + 16 * r + 16, :] = grid[row_at + r, 0:TILE, 0:C].astype(BF16)
    for r in range(4):
        edge[4 * r : 4 * r + 4, :] = grid[row_at + r, col_at : col_at + 4, :]
    corner_out[16 * which : 16 * which + 16, :] = edge[0:16, 0:C].astype(BF16)


def fill_grid(grid, edge, own, strips, which, own_row, own_col, strip_row, strip_col):
    col_in, row_in, corner_in = strips
    for r in range(TILE):
        grid[own_row + r, own_col : own_col + TILE, 0:C] = own[r].astype(F32)
    edge[:, 0:C] = col_in[64 * which : 64 * which + 64, :].astype(F32)
    for r in range(TILE):
        grid[own_row + r, strip_col : strip_col + 4, :] = edge[4 * r : 4 * r + 4, :]
    for r in range(4):
        at = 64 * which + 16 * r
        grid[strip_row + r, own_col : own_col + TILE, 0:C] = row_in[at : at + 16, :].astype(F32)
    edge[0:16, 0:C] = corner_in[16 * which : 16 * which + 16, :].astype(F32)
    for r in range(4):
        grid[strip_row + r, strip_col : strip_col + 4, :] = edge[4 * r : 4 * r + 4, :]


PAR_NAMES = ("ng", "nb", "qw", "qb", "rel", "pw", "pb", "mg", "mb", "uw", "ub", "dw", "db")
RES_NAMES = ("packed", "attn", "mixed", "middle", "hidden", "slope")
RES_SHAPES = ((576, TOK), (12, 64, 128), (C, TOK), (C, TOK), (MLP, TOK), (MLP, TOK))


class Copies:
    def __init__(self, sems):
        self.sems = sems
        self.used = 0
        self.open = {}

    def start(self, name, source, target):
        self.open[name] = pltpu.make_async_copy(source, target, self.sems.at[self.used])
        self.open[name].start()
        self.used += 1

    def __call__(self, *names):
        for name in names:
            if name in self.open:
                self.open.pop(name).wait()

    def rest(self):
        self(*list(self.open))


def start_params(copies, names, far, par, b):
    for name in names:
        source = far[name].at[b] if name in WEIGHTS else far[name]
        copies.start(name, source, par[name])


WEIGHTS = ("qw", "pw", "uw", "dw")
PAR_SHAPES = dict(
    ng=(2, C), nb=(2, C), qw=(C, 3 * C), qb=(2, 3 * C), rel=(HEADS, 2, SPAN * SPAN), pw=(C, C), pb=(2, C),
    mg=(2, C), mb=(2, C), uw=(C, MLP), ub=(2, MLP), dw=(C, MLP), db=(2, C),
)


def nothing(*_):
    pass


def first_forward(*refs):
    imagery_far, cotangent_far = refs[0:2]
    far = dict(zip(PAR_NAMES, refs[2:15]))
    own = refs[15]
    strips = refs[16:19]
    xt_far = refs[19]
    res_far = dict(zip(RES_NAMES, refs[20:26]))
    grid, edge, vec, table, bias, sems = refs[26:32]
    par = dict(zip(PAR_NAMES, refs[32:45]))
    res = dict(zip(RES_NAMES, refs[45:51]))
    imagery, cotangent, xt = refs[51:]
    need = Copies(sems)
    need.start("imagery", imagery_far, imagery)
    start_params(need, VEC_NAMES, far, par, 0)
    start_params(need, ("qw", "rel", "pw"), far, par, 0)
    need.start("cotangent", cotangent_far, cotangent)
    start_params(need, ("uw", "dw"), far, par, 0)

    def keep(*names):
        for name in names:
            need.start("out " + name, res[name], res_far[name])

    need("imagery")
    for r in range(TILE):
        grid[r, 0:TILE, 0:C] = imagery[r].astype(F32)
    x = to_channels(grid_get(grid, 0, 0))
    xt[...] = x.astype(BF16)
    need(*VEC_NAMES)
    cols = load_columns(vec, par, 0)
    need("rel")
    position_bias(par, 0, table, bias)
    need("cotangent")
    for r in range(TILE):
        grid[r, 0:TILE, 0:C] = cotangent[r].astype(F32)
    emit_strips(grid, edge, strips, 1, 0, 0)
    need.start("out xt", xt, xt_far)
    out = forward(x, par, need, cols, bias, res, None, keep)
    grid_put(grid, to_tokens(out.astype(F32)))
    keep("hidden", "slope")
    for r in range(TILE):
        own[r] = grid[r, 0:TILE, 0:C].astype(BF16)
    emit_strips(grid, edge, strips, 0, 0, 0)
    need.rest()


def second_block(*refs):
    own_in = refs[0]
    strips_in = refs[1:4]
    cotangent_far = refs[4]
    far = dict(zip(PAR_NAMES, refs[5:18]))
    out_own, back_own = refs[18:20]
    strips = refs[20:23]
    flat = refs[23]
    grid, edge, vec, table, bias, sems = refs[24:30]
    par = dict(zip(PAR_NAMES, refs[30:43]))
    small, du_ref, dpacked, rel_sum = refs[43:47]
    res = dict(zip(RES_NAMES, refs[47:53]))
    cotangent = refs[53]
    need = Copies(sems)
    start_params(need, VEC_NAMES, far, par, 1)
    start_params(need, ("rel", "qw", "pw"), far, par, 1)
    need.start("cotangent", cotangent_far, cotangent)
    start_params(need, ("uw", "dw"), far, par, 1)
    last_row = lax.axis_index("rows") == lax.axis_size("rows") - 1
    last_col = lax.axis_index("cols") == lax.axis_size("cols") - 1
    zones = [same_zone(p, last_row, last_col) for p in range(2)]
    fill_grid(grid, edge, own_in, strips_in, 0, 0, 0, 16, 16)
    x = to_channels(grid_get(grid, 4, 4))
    need(*VEC_NAMES)
    cols = load_columns(vec, par, 1)
    need("rel")
    position_bias(par, 1, table, bias)
    out = forward(x, par, need, cols, bias, res, zones, nothing)
    need("cotangent")
    fill_grid(grid, edge, cotangent, strips_in, 1, 0, 0, 16, 16)
    dout = to_channels(grid_get(grid, 4, 4)).astype(BF16)
    grid_put(grid, to_tokens(out.astype(F32)))
    for r in range(TILE):
        out_own[r] = grid[r, 0:TILE, 0:C].astype(BF16)
    emit_strips(grid, edge, strips, 0, 12, 12)
    dx = backward(dout, x, par, need, cols, res, flat, small, du_ref, dpacked, rel_sum)
    grid_put(grid, to_tokens(dx))
    for r in range(TILE):
        back_own[r] = grid[r, 0:TILE, 0:C].astype(BF16)
    emit_strips(grid, edge, strips, 1, 12, 12)
    need.rest()


BACK_NAMES = VEC_NAMES + WEIGHTS


def first_backward(*refs):
    out_in, back_in = refs[0:2]
    strips_in = refs[2:5]
    far = dict(zip(BACK_NAMES, refs[5:17]))
    xt_far = refs[17]
    res_far = dict(zip(RES_NAMES, refs[18:24]))
    output, grad, flat = refs[24:27]
    grid, edge, vec, sems = refs[27:31]
    par = dict(zip(BACK_NAMES, refs[31:43]))
    small, du_ref, dpacked, rel_sum = refs[43:47]
    res = dict(zip(RES_NAMES, refs[47:53]))
    xt = refs[53]
    need = Copies(sems)
    start_params(need, VEC_NAMES + ("dw",), far, par, 0)
    need.start("slope", res_far["slope"], res["slope"])
    need.start("middle", res_far["middle"], res["middle"])
    start_params(need, ("uw",), far, par, 0)
    need.start("hidden", res_far["hidden"], res["hidden"])
    need.start("mixed", res_far["mixed"], res["mixed"])
    start_params(need, ("pw",), far, par, 0)
    need.start("packed", res_far["packed"], res["packed"])
    need.start("attn", res_far["attn"], res["attn"])
    start_params(need, ("qw",), far, par, 0)
    need.start("xt", xt_far, xt)
    fill_grid(grid, edge, back_in, strips_in, 1, 4, 8, 0, 4)
    dout = to_channels(grid_get(grid, 0, 4)).astype(BF16)
    fill_grid(grid, edge, out_in, strips_in, 0, 4, 8, 0, 4)
    for r in range(TILE):
        output[r] = grid[r, 4:20, 0:C].astype(BF16)
    need(*VEC_NAMES)
    cols = load_columns(vec, par, 0)
    need("xt")
    x = xt[...].astype(F32)
    dx = backward(dout, x, par, need, cols, res, flat, small, du_ref, dpacked, rel_sum)
    grid_put(grid, to_tokens(dx))
    for r in range(TILE):
        grad[r] = grid[r, 0:TILE, 0:C].astype(BF16)
    need.rest()


def add_parts(parts, share, fold):
    step = share if share % 8 == 0 else 2 * share
    total = jnp.zeros((step, 128), F32)
    for at in range(0, FLAT, step):
        total = total + parts[at : at + step, :].astype(F32)
    if step == share:
        return total
    fold[0:step, :] = total
    return fold[0:share, :] + fold[share:step, :]


def sum_parts(parts, out, fold):
    out[...] = add_parts(parts, out.shape[0], fold)


def sum_spread(parts, other, out, fold):
    share = other.shape[0]
    total = add_parts(parts, share, fold)
    fold[0:share, :] = other[...]
    fold[share : 2 * share, :] = total
    total = fold[0 : 2 * share, :].astype(BF16)
    for at in range(0, 2 * FLAT, 2 * share):
        out[at : at + 2 * share, :] = total


def unpack(share, both, *outs):
    ng, nb, qw_far, qb, rel, pw_far, pb, mg, mb, uw_far, ub, dw_far, db, wide, flats, qw, pw, uw, dw, sems = outs
    copies = Copies(sems)
    factor = outs_factor
    flip = (iota((256, 256), 0) + iota((256, 256), 1) == 255).astype(BF16)
    wide[...] = both[...].astype(F32) * factor
    for b in range(2):
        flat = flats.at[b]
        for at in range(0, FLAT, share):
            flat[at : at + share, :] = wide[2 * at + (1 - b) * share : 2 * at + (2 - b) * share, :]
        for j in range(4):
            qw[b, :, 128 * j : 128 * j + 128] = flat[C * j : C * j + C, :]
        tail = flat[768:960, :]
        qw[b, :, 512:576] = tail[:, 0:64]
        pw[b, :, 128:192] = pltpu.roll(tail, 64, 1)[:, 0:64]
        pw[b, :, 0:128] = flat[960:1152, :]
        copies.start(("qw", b), qw.at[b], qw_far.at[b])
        copies.start(("pw", b), pw.at[b], pw_far.at[b])
        for j in range(6):
            uw[b, :, 128 * j : 128 * j + 128] = flat[1152 + C * j : 1152 + C * j + C, :]
            dw[b, :, 128 * j : 128 * j + 128] = flat[2304 + C * j : 2304 + C * j + C, :]
        copies.start(("uw", b), uw.at[b], uw_far.at[b])
        copies.start(("dw", b), dw.at[b], dw_far.at[b])
        for at, ref in ((0, ng), (2, nb), (4, qb), (9, pb), (11, mg), (13, mb), (15, ub), (21, db)):
            n = ref.shape[-1]
            at = at + SMALL
            for i in range(0, n, 128):
                w = min(128, n - i)
                ref[b : b + 1, i : i + w] = flat[at + i // 128 : at + i // 128 + 1, 0:w]
        table = jnp.concatenate([flat[SMALL + 24 : SMALL + 32, :], flat[SMALL + 32 : SMALL + 40, :]], axis=1)
        high, mid, low = split3(table)
        table = dot_nn(high, flip) + (dot_nn(mid, flip) + dot_nn(low, flip))
        for h in range(HEADS):
            rel[h, b : b + 1, :] = table[h : h + 1, 0 : SPAN * SPAN]
    copies.rest()


outs_factor = float(128 * 256) ** (-0.5)


VMEM = pl.BlockSpec(memory_space=pltpu.VMEM)


def near(value):
    return pltpu.with_memory_space_constraint(value, pltpu.VMEM)


FAR = pl.BlockSpec(memory_space=pltpu.HBM)


def call(kernel, args, far_args, outs, far_outs, scratch, flops):
    return pl.pallas_call(
        kernel,
        in_specs=[VMEM] * len(args) + [FAR] * len(far_args),
        out_specs=[VMEM] * len(outs) + [FAR] * len(far_outs),
        out_shape=list(outs) + [pltpu.HBM(o.shape, o.dtype) for o in far_outs],
        scratch_shapes=scratch,
        compiler_params=pltpu.CompilerParams(vmem_limit_bytes=30 * 2**20),
        cost_estimate=pl.CostEstimate(flops=flops, transcendentals=0, bytes_accessed=4000000),
    )(*[near(a) for a in args], *[pltpu.with_memory_space_constraint(a, pltpu.HBM) for a in far_args])


def shaped(shape, dtype=BF16):
    return jax.ShapeDtypeStruct(shape, dtype)


def exchange(strips, step):
    n_rows = lax.axis_size("rows")
    n_cols = lax.axis_size("cols")
    col_strip, row_strip, corner = strips
    along = [(c, (c + step) % n_cols) for c in range(n_cols)]
    down = [(r, (r + step) % n_rows) for r in range(n_rows)]
    both = [
        (r * n_cols + c, ((r + step) % n_rows) * n_cols + (c + step) % n_cols)
        for r in range(n_rows)
        for c in range(n_cols)
    ]
    col_strip = lax.ppermute(col_strip, "cols", along)
    row_strip = lax.ppermute(row_strip, "rows", down)
    corner = lax.ppermute(corner, ("rows", "cols"), both)
    return [col_strip, row_strip, corner]


def send_parts(value):
    n = lax.axis_size("rows") * lax.axis_size("cols")
    share = value.shape[0] // n
    shape = (n, share, 128) if share % 8 == 0 else (n, share // 4, 4, 128)
    got = lax.all_to_all(value.reshape(shape), ("rows", "cols"), 0, 0, tiled=True)
    return got.reshape(value.shape)


def both_blocks(imagery, cotangent, *params):
    params = list(params)
    params[4] = params[4].transpose(1, 0, 2)
    params[11] = params[11].swapaxes(1, 2)
    tile = (TILE, TILE, C)
    strips = [pltpu.VMEM(s, BF16) for s in ((128, C), (128, C), (32, C))]
    packed_grads = pltpu.VMEM((FLAT, 128), BF16)
    held = pltpu.VMEM(tile, BF16)
    grid = pltpu.VMEM((24, 24, 256), F32)
    edge = pltpu.VMEM((64, 256), F32)
    vec = pltpu.VMEM((128, MLP), F32)
    tables = [pltpu.VMEM((8, 256), F32), pltpu.VMEM((HEADS, 64, 128), F32)]
    work = [
        pltpu.VMEM((48, 128), F32),
        pltpu.VMEM((MLP, TOK), BF16),
        pltpu.VMEM((576, TOK), BF16),
        pltpu.VMEM((HEADS, 64, 128), F32),
    ]
    par = dict(zip(PAR_NAMES, params))
    par_kinds = {n: BF16 if n in WEIGHTS else F32 for n in PAR_NAMES}
    par_vmem = {n: pltpu.VMEM(PAR_SHAPES[n], par_kinds[n]) for n in PAR_NAMES}
    res_vmem = [pltpu.VMEM(s, BF16) for s in RES_SHAPES]
    sems = pltpu.SemaphoreType.DMA((32,))
    one = call(
        first_forward,
        (),
        (imagery, cotangent, *params),
        [held] + strips,
        [shaped((C, TOK))] + [shaped(s) for s in RES_SHAPES],
        [grid, edge, vec] + tables + [sems] + list(par_vmem.values()) + res_vmem + [held, held, pltpu.VMEM((C, TOK), BF16)],
        5 * 10**9,
    )
    own, got, xt, res = one[0], exchange(one[1:4], -1), one[4], one[5:]
    two = call(
        second_block,
        (own, *got),
        (cotangent, *params),
        [held, held] + strips + [packed_grads],
        [],
        [grid, edge, vec] + tables + [sems] + list(par_vmem.values()) + work + res_vmem + [held],
        10**10,
    )
    got = exchange(two[2:5], 1)
    output, grad, flat_one = call(
        first_backward,
        (two[0], two[1], *got),
        (*[par[n] for n in BACK_NAMES], xt, *res),
        [shaped(tile), shaped(tile), packed_grads],
        [],
        [grid, edge, vec, sems] + [par_vmem[n] for n in BACK_NAMES] + work + res_vmem + [pltpu.VMEM((C, TOK), BF16)],
        5 * 10**9,
    )
    parts_two = send_parts(two[5])
    parts_one = send_parts(flat_one)
    share = FLAT // (lax.axis_size("rows") * lax.axis_size("cols"))
    fold = pltpu.VMEM((max(2 * share, 8), 128), F32)
    sum_two = call(sum_parts, (parts_two,), (), [pltpu.VMEM((share, 128), F32)], [], [fold], 10**6)[0]
    both = call(sum_spread, (parts_one, sum_two), (), [pltpu.VMEM((2 * FLAT, 128), BF16)], [], [fold], 10**6)[0]
    weights = [pltpu.VMEM((2,) + PAR_SHAPES[n], F32) for n in ("qw", "pw", "uw", "dw")]
    grads = pl.pallas_call(
        functools.partial(unpack, share),
        in_specs=[VMEM],
        out_specs=[FAR if n in WEIGHTS else VMEM for n in PAR_NAMES],
        out_shape=[shaped(p.shape, F32) for p in params],
        scratch_shapes=[pltpu.VMEM((2 * FLAT, 128), F32), pltpu.VMEM((2, FLAT, 128), F32)]
        + weights
        + [pltpu.SemaphoreType.DMA((8,))],
        name="unpack",
        compiler_params=pltpu.CompilerParams(vmem_limit_bytes=30 * 2**20),
    )(near(send_parts(both)))
    grads = list(grads)
    grads[4] = grads[4].transpose(1, 0, 2)
    grads[11] = grads[11].swapaxes(1, 2)
    return (output, grad, *grads)


def solution(mesh):
    tile = P("rows", "cols", None)
    return jax.shard_map(
        both_blocks,
        mesh=mesh,
        in_specs=(tile, tile) + (P(),) * 13,
        out_specs=(tile, tile) + (P(),) * 13,
        check_vma=False,
    )
```

time: 161 us -> 122 us (0.76)
  local copies, waits for them, and re-layouts: 19.1 us -> 0 us
  waiting for transfers between devices: 47.6 us -> 30.4 us
  blocking collectives: 24.6 us -> 31.2 us
  Pallas kernels: 33 us -> 28.1 us
  starting transfers between devices: 35.2 us -> 30.6 us
    all_to_all x3 -> x2, waiting for transfers between devices: 33.1 us -> 17.5 us  [send_parts(): lax.all_to_all(value.reshape(shape), ('rows', 'cols'), 0, 0, tiled=True)]
    reshape x8 -> x0, local copies, waits for them, and re-layouts: 10.1 us -> none  [block_of(): array = array.reshape(2, 1, array.shape[-1])]
    unnamed x28 -> x0, local copies, waits for them, and re-layouts: 9 us -> none
    all_to_all x1, blocking collectives: 24.6 us -> 31.2 us  [send_parts(): lax.all_to_all(value.reshape(shape), ('rows', 'cols'), 0, 0, tiled=True)]
    pallas_call x6, Pallas kernels: 33 us -> 28.1 us  [the longest x5 25.3 us: call(): pl.pallas_call(kernel, in_specs=[VMEM] * len(args) + [FAR] * len(far_args...]
    all_to_all x3 -> x2, starting transfers between devices: 18.7 us -> 14.1 us  [send_parts(): lax.all_to_all(value.reshape(shape), ('rows', 'cols'), 0, 0, tiled=True)]
  transfers between devices with their start and end apart: 9 -> 8, of which waited for: 5 -> 4; matrix products, arithmetic and copies ran while one was open for 0% -> 0% of each run, Pallas kernels for 8% -> 7%
where the time goes in v1:
time: 122 us; the launch traced here: 121 us
  blocking collectives  31.2 us (26%)
  starting transfers between devices  30.6 us (25%)
  waiting for transfers between devices  30.4 us (25%)
  Pallas kernels  28.1 us (23%)
    all_to_all x1, blocking collectives, send_parts(): lax.all_to_all(value.reshape(shape), ('rows', 'cols'), 0, 0, tiled=True)  31.2 us
    pallas_call x5, Pallas kernels, call(): pl.pallas_call(kernel, in_specs=[VMEM] * len(args) + [FAR] * len(far_args...  25.3 us
    all_to_all x2, waiting for transfers between devices, send_parts(): lax.all_to_all(value.reshape(shape), ('rows', 'cols'), 0, 0, tiled=True)  17.5 us
    all_to_all x2, starting transfers between devices, send_parts(): lax.all_to_all(value.reshape(shape), ('rows', 'cols'), 0, 0, tiled=True)  14.1 us
    ppermute x2, waiting for transfers between devices, exchange(): corner = lax.ppermute(corner, ('rows', 'cols'), both)  12.7 us
    ppermute x2, starting transfers between devices, exchange(): corner = lax.ppermute(corner, ('rows', 'cols'), both)  6.67 us
    ppermute x2, starting transfers between devices, exchange(): row_strip = lax.ppermute(row_strip, 'rows', down)  5.21 us
    ppermute x2, starting transfers between devices, exchange(): col_strip = lax.ppermute(col_strip, 'cols', along)  4.67 us
  transfers between devices with their start and end apart: 8, of which 4 were waited for; matrix products, arithmetic and copies ran while one was open for 0% of the time, Pallas kernels for 7%

profile of v1, /device:TPU:1, one launch (start us, length us, event | category | flops | bytes accessed | tf_op | source)
XLA Modules:
  0.0 121.2 jit_solution(11070137611892609167)
XLA Ops:
  0.6 5.8 %shard_map.262 = (bf16[16,16,192]{2,1,0:T(8,128)(2,1)S(1)}, bf16[128,192]{1,0:T(8,128)(2,1)S(1)}, bf16[128,192]{1,0:T(8,128)(2,1)S(1)}, bf16[32,192]{1,0:T(8,128...) custom-call(bf16[16,16,192]{2,1,0:T(8,128)(2,1)} %refs_0_.1, ...), custom_call_target="tpu_custom_call" | custom-call | flops 5000000000 | bytes 4000000 | tf_op jit(solution)/shard_map/pallas_call | solution.py:550
  6.5 1.5 %collective-permute-start = (bf16[128,192]{1,0:T(8,128)(2,1)S(1)}, bf16[128,192]{1,0:T(8,128)(2,1)S(1)}, u32[]{:S(2)}, u32[]{:S(2)}) collective-permute-start(bf16[128,192]{1,0:T(8,128)(2,1)S(1)} %get-tuple-element.49), channel_id=1, source_target_pairs={{0,15},{1,0},{2,1},{3,2},{4,3},{5,4},{6,5},{7,6},{8,7},{9,8},{10,9... | collective-permute-start | bytes 147464 | tf_op jit(solution)/shard_map/ppermute | solution.py:576
  7.9 4.9 %collective-permute-start.1 = (bf16[128,192]{1,0:T(8,128)(2,1)S(1)}, bf16[128,192]{1,0:T(8,128)(2,1)S(1)}, u32[]{:S(2)}, u32[]{:S(2)}) collective-permute-start(bf16[128,192]{1,0:T(8,128)(2,1)S(1)} %get-tuple-element.50), channel_id=1, source_target_pairs={{0,112},{16,0},{32,16},{48,32},{64,48},{80,64},{96,80},{112,96},{1... | collective-permute-start | bytes 147464 | tf_op jit(solution)/shard_map/ppermute | solution.py:577
  12.8 5.2 %collective-permute-start.2 = (bf16[32,192]{1,0:T(8,128)(2,1)S(1)}, bf16[32,192]{1,0:T(8,128)(2,1)S(1)}, u32[]{:S(2)}, u32[]{:S(2)}) collective-permute-start(bf16[32,192]{1,0:T(8,128)(2,1)S(1)} %get-tuple-element.51), channel_id=1, source_target_pairs={{0,127},{1,112},{2,113},{3,114},{4,115},{5,116},{6,117},{7,118},{8... | collective-permute-start | bytes 36872 | tf_op jit(solution)/shard_map/ppermute | solution.py:578
  18.0 0.9 collective-permute-done.2.refs_3_
  18.8 0.0 collective-permute-done.refs_1_
  18.8 0.0 collective-permute-done.1.refs_2_
  18.8 10.9 %shard_map.263 = (bf16[16,16,192]{2,1,0:T(8,128)(2,1)S(1)}, bf16[16,16,192]{2,1,0:T(8,128)(2,1)S(1)}, bf16[128,192]{1,0:T(8,128)(2,1)S(1)}, bf16[128,192]{1,0:T(...) custom-call(bf16[16,16,192]{2,1,0:T(8,128)(2,1)S(1)} %get-tuple-element.48.refs_0_, ...), custom_call_target="tpu_custom_call" | custom-call | flops 10000000000 | bytes 4000000 | tf_op jit(solution)/shard_map/pallas_call | solution.py:550
  29.8 7.9 %all-to-all-start.1 = ((bf16[128,7,4,128]{3,2,1,0:T(4,128)(2,1)}), bf16[128,7,4,128]{3,2,1,0:T(4,128)(2,1)S(1)}, u32[]{:S(2)}, u32[]{:S(2)}) async-start(bf16[128,7,4,128]{3,2,1,0:T(4,128)(2,1)} %bitcast.4), calls=%async_computation.1 | async-start | bytes 1835008 | tf_op jit(solution)/shard_map/all_to_all | solution.py:586
  37.7 3.2 %collective-permute-start.3 = (bf16[128,192]{1,0:T(8,128)(2,1)S(1)}, bf16[128,192]{1,0:T(8,128)(2,1)S(1)}, u32[]{:S(2)}, u32[]{:S(2)}) collective-permute-start(bf16[128,192]{1,0:T(8,128)(2,1)S(1)} %get-tuple-element.54), channel_id=1, source_target_pairs={{0,1},{1,2},{2,3},{3,4},{4,5},{5,6},{6,7},{7,8},{8,9},{9,10},{10,1... | collective-permute-start | bytes 147464 | tf_op jit(solution)/shard_map/ppermute | solution.py:576
  40.9 0.3 collective-permute-start.4
  41.2 1.5 %collective-permute-start.5 = (bf16[32,192]{1,0:T(8,128)(2,1)S(1)}, bf16[32,192]{1,0:T(8,128)(2,1)S(1)}, u32[]{:S(2)}, u32[]{:S(2)}) collective-permute-start(bf16[32,192]{1,0:T(8,128)(2,1)S(1)} %get-tuple-element.56), channel_id=1, source_target_pairs={{0,17},{1,18},{2,19},{3,20},{4,21},{5,22},{6,23},{7,24},{8,25},{9,... | collective-permute-start | bytes 36872 | tf_op jit(solution)/shard_map/ppermute | solution.py:578
  42.7 11.9 %collective-permute-done.5.refs_4_ = bf16[32,192]{1,0:T(8,128)(2,1)S(1)} collective-permute-done((bf16[32,192]{1,0:T(8,128)(2,1)S(1)}, bf16[32,192]{1,0:T(8,128)(2,1)S(1)}, u32[]{:S(2)}, u32[]{:S(2)}) %collective-permute-start.5) | collective-permute-done | bytes 12320 | tf_op jit(solution)/shard_map/ppermute | solution.py:578
  54.6 0.0 collective-permute-done.3.refs_2_
  54.6 0.1 collective-permute-done.4.refs_3_
  54.7 8.2 %shard_map.264 = (bf16[16,16,192]{2,1,0:T(8,128)(2,1)}, bf16[16,16,192]{2,1,0:T(8,128)(2,1)}, bf16[3584,128]{1,0:T(8,128)(2,1)}) custom-call(bf16[16,16,192]{2,1,0:T(8,128)(2,1)S(1)} %get-tuple-element.52.refs_0_, bf16[16,16,192]{2,1,0:T(8,128)(2,1)S(1)} %get-tuple-element.53.refs_1_, bf16[128,192]{1,0:T(8,128)(2,1)S(1)} %collective-permute-done.3.refs_2_, ...), custom_call_target="tpu_custom_call" | custom-call | flops 5000000000 | bytes 4000000 | tf_op jit(solution)/shard_map/pallas_call | solution.py:550
  62.9 0.0 all-to-all-done.1
  63.0 6.2 %all-to-all-start = ((bf16[128,7,4,128]{3,2,1,0:T(4,128)(2,1)}), bf16[128,7,4,128]{3,2,1,0:T(4,128)(2,1)S(1)}, u32[]{:S(2)}, u32[]{:S(2)}) async-start(bf16[128,7,4,128]{3,2,1,0:T(4,128)(2,1)} %bitcast.2), calls=%async_computation | async-start | bytes 1835008 | tf_op jit(solution)/shard_map/all_to_all | solution.py:586
  69.1 0.1 shard_map.265.other
  69.3 17.5 %all-to-all-done = bf16[128,7,4,128]{3,2,1,0:T(4,128)(2,1)S(1)} async-done(((bf16[128,7,4,128]{3,2,1,0:T(4,128)(2,1)}), bf16[128,7,4,128]{3,2,1,0:T(4,128)(2,1)S(1)}, u32[]{:S(2)}, u32[]{:S(2)}) %all-to-all-start) | async-done | bytes 917536 | tf_op jit(solution)/shard_map/all_to_all | solution.py:586
  86.8 0.2 shard_map.266
  87.0 31.2 %all_to_all.15 = bf16[128,56,128]{2,1,0:T(8,128)(2,1)S(1)} all-to-all(bf16[128,56,128]{2,1,0:T(8,128)(2,1)S(1)} %bitcast.11), channel_id=1, replica_groups=mesh['rows'=8,'cols'=16] {'rows','cols'}, dimensions={0} | all-to-all | bytes 3670016 | tf_op jit(solution)/shard_map/all_to_all | solution.py:586
  118.2 2.8 %unpack.1 = (f32[2,192]{1,0:T(2,128)}, f32[2,192]{1,0:T(2,128)}, f32[2,192,576]{2,1,0:T(8,128)}, f32[2,576]{1,0:T(2,128)}, f32[6,2,225]{2,1,0:T(2,128)}, /*index...) custom-call(bf16[7168,128]{1,0:T(8,128)(2,1)S(1)} %bitcast.10), custom_call_target="tpu_custom_call" | custom-call | tf_op jit(solution)/shard_map/unpack/pallas_call | solution.py:649
Async XLA Ops:
  6.5 12.4 %collective-permute-start = (bf16[128,192]{1,0:T(8,128)(2,1)S(1)}, bf16[128,192]{1,0:T(8,128)(2,1)S(1)}, u32[]{:S(2)}, u32[]{:S(2)}) collective-permute-start(bf16[128,192]{1,0:T(8,128)(2,1)S(1)} %get-tuple-element.49), channel_id=1, source_target_pairs={{0,15},{1,0},{2,1},{3,2},{4,3},{5,4},{6,5},{7,6},{8,7},{9,8},{10,9... | collective-permute-start | bytes 147464 | tf_op jit(solution)/shard_map/ppermute | solution.py:576
  7.9 10.9 %collective-permute-start.1 = (bf16[128,192]{1,0:T(8,128)(2,1)S(1)}, bf16[128,192]{1,0:T(8,128)(2,1)S(1)}, u32[]{:S(2)}, u32[]{:S(2)}) collective-permute-start(bf16[128,192]{1,0:T(8,128)(2,1)S(1)} %get-tuple-element.50), channel_id=1, source_target_pairs={{0,112},{16,0},{32,16},{48,32},{64,48},{80,64},{96,80},{112,96},{1... | collective-permute-start | bytes 147464 | tf_op jit(solution)/shard_map/ppermute | solution.py:577
  12.8 6.0 %collective-permute-start.2 = (bf16[32,192]{1,0:T(8,128)(2,1)S(1)}, bf16[32,192]{1,0:T(8,128)(2,1)S(1)}, u32[]{:S(2)}, u32[]{:S(2)}) collective-permute-start(bf16[32,192]{1,0:T(8,128)(2,1)S(1)} %get-tuple-element.51), channel_id=1, source_target_pairs={{0,127},{1,112},{2,113},{3,114},{4,115},{5,116},{6,117},{7,118},{8... | collective-permute-start | bytes 36872 | tf_op jit(solution)/shard_map/ppermute | solution.py:578
  29.8 33.2 %all-to-all-start.1 = ((bf16[128,7,4,128]{3,2,1,0:T(4,128)(2,1)}), bf16[128,7,4,128]{3,2,1,0:T(4,128)(2,1)S(1)}, u32[]{:S(2)}, u32[]{:S(2)}) async-start(bf16[128,7,4,128]{3,2,1,0:T(4,128)(2,1)} %bitcast.4), calls=%async_computation.1 | async-start | bytes 1835008 | tf_op jit(solution)/shard_map/all_to_all | solution.py:586
  37.7 16.9 %collective-permute-start.3 = (bf16[128,192]{1,0:T(8,128)(2,1)S(1)}, bf16[128,192]{1,0:T(8,128)(2,1)S(1)}, u32[]{:S(2)}, u32[]{:S(2)}) collective-permute-start(bf16[128,192]{1,0:T(8,128)(2,1)S(1)} %get-tuple-element.54), channel_id=1, source_target_pairs={{0,1},{1,2},{2,3},{3,4},{4,5},{5,6},{6,7},{7,8},{8,9},{9,10},{10,1... | collective-permute-start | bytes 147464 | tf_op jit(solution)/shard_map/ppermute | solution.py:576
  40.9 13.8 %collective-permute-start.4 = (bf16[128,192]{1,0:T(8,128)(2,1)S(1)}, bf16[128,192]{1,0:T(8,128)(2,1)S(1)}, u32[]{:S(2)}, u32[]{:S(2)}) collective-permute-start(bf16[128,192]{1,0:T(8,128)(2,1)S(1)} %get-tuple-element.55), channel_id=1, source_target_pairs={{0,16},{16,32},{32,48},{48,64},{64,80},{80,96},{96,112},{112,0},{1... | collective-permute-start | bytes 147464 | tf_op jit(solution)/shard_map/ppermute | solution.py:577
  41.2 13.4 %collective-permute-start.5 = (bf16[32,192]{1,0:T(8,128)(2,1)S(1)}, bf16[32,192]{1,0:T(8,128)(2,1)S(1)}, u32[]{:S(2)}, u32[]{:S(2)}) collective-permute-start(bf16[32,192]{1,0:T(8,128)(2,1)S(1)} %get-tuple-element.56), channel_id=1, source_target_pairs={{0,17},{1,18},{2,19},{3,20},{4,21},{5,22},{6,23},{7,24},{8,25},{9,... | collective-permute-start | bytes 36872 | tf_op jit(solution)/shard_map/ppermute | solution.py:578
  63.0 23.8 %all-to-all-start = ((bf16[128,7,4,128]{3,2,1,0:T(4,128)(2,1)}), bf16[128,7,4,128]{3,2,1,0:T(4,128)(2,1)S(1)}, u32[]{:S(2)}, u32[]{:S(2)}) async-start(bf16[128,7,4,128]{3,2,1,0:T(4,128)(2,1)} %bitcast.2), calls=%async_computation | async-start | bytes 1835008 | tf_op jit(solution)/shard_map/all_to_all | solution.py:586

commit v2 on v1

--- a/solution.py
+++ b/solution.py
@@ -6,7 +6,6 @@
 from jax.experimental import pallas as pl
 from jax.experimental.pallas import tpu as pltpu
 from jax.sharding import PartitionSpec as P
-
 
 F32 = jnp.float32
 BF16 = jnp.bfloat16
@@ -434,15 +433,16 @@
 def first_backward(*refs):
     out_in, back_in = refs[0:2]
     strips_in = refs[2:5]
-    far = dict(zip(BACK_NAMES, refs[5:17]))
-    xt_far = refs[17]
-    res_far = dict(zip(RES_NAMES, refs[18:24]))
-    output, grad, flat = refs[24:27]
-    grid, edge, vec, sems = refs[27:31]
-    par = dict(zip(BACK_NAMES, refs[31:43]))
-    small, du_ref, dpacked, rel_sum = refs[43:47]
-    res = dict(zip(RES_NAMES, refs[47:53]))
-    xt = refs[53]
+    flat_two = refs[5]
+    far = dict(zip(BACK_NAMES, refs[6:18]))
+    xt_far = refs[18]
+    res_far = dict(zip(RES_NAMES, refs[19:25]))
+    output, grad, kept, sent = refs[25:29]
+    grid, edge, vec, sems = refs[29:33]
+    par = dict(zip(BACK_NAMES, refs[33:45]))
+    small, du_ref, dpacked, rel_sum = refs[45:49]
+    res = dict(zip(RES_NAMES, refs[49:55]))
+    xt, flat = refs[55:]
     need = Copies(sems)
     start_params(need, VEC_NAMES + ("dw",), far, par, 0)
     need.start("slope", res_far["slope"], res["slope"])
@@ -468,66 +468,65 @@
     grid_put(grid, to_tokens(dx))
     for r in range(TILE):
         grad[r] = grid[r, 0:TILE, 0:C].astype(BF16)
+    even = lax.axis_index("cols") % 2 == 0
+    for at in range(0, FLAT, 256):
+        rows = slice(at, at + 256)
+        kept[rows, :] = jnp.where(even, flat[rows, :], flat_two[rows, :])
+        sent[rows, :] = jnp.where(even, flat_two[rows, :], flat[rows, :])
     need.rest()
 
 
-def add_parts(parts, share, fold):
-    step = share if share % 8 == 0 else 2 * share
-    total = jnp.zeros((step, 128), F32)
-    for at in range(0, FLAT, step):
-        total = total + parts[at : at + step, :].astype(F32)
-    if step == share:
-        return total
-    fold[0:step, :] = total
-    return fold[0:share, :] + fold[share:step, :]
-
-
-def sum_parts(parts, out, fold):
-    out[...] = add_parts(parts, out.shape[0], fold)
-
-
-def sum_spread(parts, other, out, fold):
-    share = other.shape[0]
-    total = add_parts(parts, share, fold)
-    fold[0:share, :] = other[...]
-    fold[share : 2 * share, :] = total
-    total = fold[0 : 2 * share, :].astype(BF16)
-    for at in range(0, 2 * FLAT, 2 * share):
-        out[at : at + 2 * share, :] = total
-
-
-def unpack(share, both, *outs):
-    ng, nb, qw_far, qb, rel, pw_far, pb, mg, mb, uw_far, ub, dw_far, db, wide, flats, qw, pw, uw, dw, sems = outs
+def add_pair(kept, got, out):
+    for at in range(0, FLAT, 256):
+        rows = slice(at, at + 256)
+        out[rows, :] = (kept[rows, :].astype(F32) + got[rows, :].astype(F32)).astype(BF16)
+
+
+def sum_spread(share, parts, out):
+    total = jnp.zeros((share, 128), F32)
+    for at in range(0, FLAT, share):
+        total = total + parts[at : at + share, :].astype(F32)
+    total = total.astype(BF16)
+    for at in range(0, FLAT, share):
+        out[at : at + share, :] = total
+
+
+def unpack(mine, other, *outs):
+    ng, nb, qw_far, qb, rel, pw_far, pb, mg, mb, uw_far, ub, dw_far, db, qw, pw, uw, dw, sems = outs
     copies = Copies(sems)
     factor = outs_factor
     flip = (iota((256, 256), 0) + iota((256, 256), 1) == 255).astype(BF16)
-    wide[...] = both[...].astype(F32) * factor
+    parity = lax.axis_index("cols") % 2
     for b in range(2):
-        flat = flats.at[b]
-        for at in range(0, FLAT, share):
-            flat[at : at + share, :] = wide[2 * at + (1 - b) * share : 2 * at + (2 - b) * share, :]
+
+        def raw(at, n):
+            return jnp.where(parity == b, mine[at : at + n, :], other[at : at + n, :])
+
+        def rows(at, n):
+            return raw(at, n).astype(F32) * factor
+
         for j in range(4):
-            qw[b, :, 128 * j : 128 * j + 128] = flat[C * j : C * j + C, :]
-        tail = flat[768:960, :]
+            qw[b, :, 128 * j : 128 * j + 128] = rows(C * j, C)
+        tail = rows(768, C)
         qw[b, :, 512:576] = tail[:, 0:64]
+        copies.start(("qw", b), qw.at[b], qw_far.at[b])
         pw[b, :, 128:192] = pltpu.roll(tail, 64, 1)[:, 0:64]
-        pw[b, :, 0:128] = flat[960:1152, :]
-        copies.start(("qw", b), qw.at[b], qw_far.at[b])
+        pw[b, :, 0:128] = rows(960, C)
         copies.start(("pw", b), pw.at[b], pw_far.at[b])
         for j in range(6):
-            uw[b, :, 128 * j : 128 * j + 128] = flat[1152 + C * j : 1152 + C * j + C, :]
-            dw[b, :, 128 * j : 128 * j + 128] = flat[2304 + C * j : 2304 + C * j + C, :]
+            uw[b, :, 128 * j : 128 * j + 128] = rows(1152 + C * j, C)
         copies.start(("uw", b), uw.at[b], uw_far.at[b])
+        for j in range(6):
+            dw[b, :, 128 * j : 128 * j + 128] = rows(2304 + C * j, C)
         copies.start(("dw", b), dw.at[b], dw_far.at[b])
+        small = rows(SMALL, 48)
         for at, ref in ((0, ng), (2, nb), (4, qb), (9, pb), (11, mg), (13, mb), (15, ub), (21, db)):
             n = ref.shape[-1]
-            at = at + SMALL
             for i in range(0, n, 128):
                 w = min(128, n - i)
-                ref[b : b + 1, i : i + w] = flat[at + i // 128 : at + i // 128 + 1, 0:w]
-        table = jnp.concatenate([flat[SMALL + 24 : SMALL + 32, :], flat[SMALL + 32 : SMALL + 40, :]], axis=1)
-        high, mid, low = split3(table)
-        table = dot_nn(high, flip) + (dot_nn(mid, flip) + dot_nn(low, flip))
+                ref[b : b + 1, i : i + w] = small[at + i // 128 : at + i // 128 + 1, 0:w]
+        table = jnp.concatenate([raw(SMALL + 24, 8), raw(SMALL + 32, 8)], axis=1)
+        table = dot_nn(table, flip) * factor
         for h in range(HEADS):
             rel[h, b : b + 1, :] = table[h : h + 1, 0 : SPAN * SPAN]
     copies.rest()
@@ -546,13 +545,14 @@
 FAR = pl.BlockSpec(memory_space=pltpu.HBM)
 
 
-def call(kernel, args, far_args, outs, far_outs, scratch, flops):
+def call(kernel, name, args, far_args, outs, far_outs, scratch, flops):
     return pl.pallas_call(
         kernel,
         in_specs=[VMEM] * len(args) + [FAR] * len(far_args),
         out_specs=[VMEM] * len(outs) + [FAR] * len(far_outs),
         out_shape=list(outs) + [pltpu.HBM(o.shape, o.dtype) for o in far_outs],
         scratch_shapes=scratch,
+        name=name,
         compiler_params=pltpu.CompilerParams(vmem_limit_bytes=30 * 2**20),
         cost_estimate=pl.CostEstimate(flops=flops, transcendentals=0, bytes_accessed=4000000),
     )(*[near(a) for a in args], *[pltpu.with_memory_space_constraint(a, pltpu.HBM) for a in far_args])
@@ -573,21 +573,27 @@
         for r in range(n_rows)
         for c in range(n_cols)
     ]
-    col_strip = lax.ppermute(col_strip, "cols", along)
-    row_strip = lax.ppermute(row_strip, "rows", down)
-    corner = lax.ppermute(corner, ("rows", "cols"), both)
-    return [col_strip, row_strip, corner]
+    return [
+        lax.ppermute(col_strip, "cols", along),
+        lax.ppermute(row_strip, "rows", down),
+        lax.ppermute(corner, ("rows", "cols"), both),
+    ]
+
+
+def swap(value):
+    return lax.ppermute(value, "cols", [(c, c ^ 1) for c in range(lax.axis_size("cols"))])
 
 
 def send_parts(value):
-    n = lax.axis_size("rows") * lax.axis_size("cols")
-    share = value.shape[0] // n
-    shape = (n, share, 128) if share % 8 == 0 else (n, share // 4, 4, 128)
-    got = lax.all_to_all(value.reshape(shape), ("rows", "cols"), 0, 0, tiled=True)
+    n_cols = lax.axis_size("cols")
+    n = lax.axis_size("rows") * n_cols
+    groups = [[d for d in range(n) if d % n_cols % 2 == p] for p in range(2)]
+    parts = value.reshape(n // 2, 2 * FLAT // n, 128)
+    got = lax.all_to_all(parts, ("rows", "cols"), 0, 0, axis_index_groups=groups, tiled=True)
     return got.reshape(value.shape)
 
 
-def both_blocks(imagery, cotangent, *params):
+def per_device(imagery, cotangent, *params):
     params = list(params)
     params[4] = params[4].transpose(1, 0, 2)
     params[11] = params[11].swapaxes(1, 2)
@@ -612,6 +618,7 @@
     sems = pltpu.SemaphoreType.DMA((32,))
     one = call(
         first_forward,
+        "first_forward",
         (),
         (imagery, cotangent, *params),
         [held] + strips,
@@ -622,6 +629,7 @@
     own, got, xt, res = one[0], exchange(one[1:4], -1), one[4], one[5:]
     two = call(
         second_block,
+        "second_block",
         (own, *got),
         (cotangent, *params),
         [held, held] + strips + [packed_grads],
@@ -630,33 +638,34 @@
         10**10,
     )
     got = exchange(two[2:5], 1)
-    output, grad, flat_one = call(
+    output, grad, kept, sent = call(
         first_backward,
-        (two[0], two[1], *got),
+        "first_backward",
+        (two[0], two[1], *got, two[5]),
         (*[par[n] for n in BACK_NAMES], xt, *res),
-        [shaped(tile), shaped(tile), packed_grads],
+        [shaped(tile), shaped(tile), packed_grads, packed_grads],
         [],
-        [grid, edge, vec, sems] + [par_vmem[n] for n in BACK_NAMES] + work + res_vmem + [pltpu.VMEM((C, TOK), BF16)],
+        [grid, edge, vec, sems]
+        + [par_vmem[n] for n in BACK_NAMES]
+        + work
+        + res_vmem
+        + [pltpu.VMEM((C, TOK), BF16), packed_grads],
         5 * 10**9,
     )
-    parts_two = send_parts(two[5])
-    parts_one = send_parts(flat_one)
-    share = FLAT // (lax.axis_size("rows") * lax.axis_size("cols"))
-    fold = pltpu.VMEM((max(2 * share, 8), 128), F32)
-    sum_two = call(sum_parts, (parts_two,), (), [pltpu.VMEM((share, 128), F32)], [], [fold], 10**6)[0]
-    both = call(sum_spread, (parts_one, sum_two), (), [pltpu.VMEM((2 * FLAT, 128), BF16)], [], [fold], 10**6)[0]
+    pair = call(add_pair, "add_pair", (kept, swap(sent)), (), [packed_grads], [], [], 10**6)[0]
+    share = 2 * FLAT // (lax.axis_size("rows") * lax.axis_size("cols"))
+    spread = functools.partial(sum_spread, share)
+    mine = send_parts(call(spread, "sum_spread", (send_parts(pair),), (), [packed_grads], [], [], 10**6)[0])
     weights = [pltpu.VMEM((2,) + PAR_SHAPES[n], F32) for n in ("qw", "pw", "uw", "dw")]
     grads = pl.pallas_call(
-        functools.partial(unpack, share),
-        in_specs=[VMEM],
+        unpack,
+        in_specs=[VMEM, VMEM],
         out_specs=[FAR if n in WEIGHTS else VMEM for n in PAR_NAMES],
         out_shape=[shaped(p.shape, F32) for p in params],
-        scratch_shapes=[pltpu.VMEM((2 * FLAT, 128), F32), pltpu.VMEM((2, FLAT, 128), F32)]
-        + weights
-        + [pltpu.SemaphoreType.DMA((8,))],
+        scratch_shapes=weights + [pltpu.SemaphoreType.DMA((8,))],
         name="unpack",
         compiler_params=pltpu.CompilerParams(vmem_limit_bytes=30 * 2**20),
-    )(near(send_parts(both)))
+    )(near(mine), near(swap(mine)))
     grads = list(grads)
     grads[4] = grads[4].transpose(1, 0, 2)
     grads[11] = grads[11].swapaxes(1, 2)
@@ -666,7 +675,7 @@
 def solution(mesh):
     tile = P("rows", "cols", None)
     return jax.shard_map(
-        both_blocks,
+        per_device,
         mesh=mesh,
         in_specs=(tile, tile) + (P(),) * 13,
         out_specs=(tile, tile) + (P(),) * 13,

time: 122 us -> 101 us (0.83)
  waiting for transfers between devices: 30.4 us -> 12.1 us
  starting transfers between devices: 30.6 us -> 19.1 us
  blocking collectives: 31.2 us -> 41.8 us
    all_to_all x2 -> x0, waiting for transfers between devices: 17.5 us -> none  [send_parts(): lax.all_to_all(value.reshape(shape), ('rows', 'cols'), 0, 0, tiled=True)]
    all_to_all x2 -> x0, starting transfers between devices: 14.1 us -> none  [send_parts(): lax.all_to_all(value.reshape(shape), ('rows', 'cols'), 0, 0, tiled=True)]
    all_to_all x1 -> x2, blocking collectives: 31.2 us -> 41.8 us  [send_parts(): lax.all_to_all(parts, ('rows', 'cols'), 0, 0, axis_index_groups=groups, t...]
    ppermute x6 -> x8, starting transfers between devices: 16.5 us -> 19.1 us  [the longest x2 6.94 us: swap(): lax.ppermute(value, 'cols', [(c, c ^ 1) for c in range(lax.axis_size('col...]
    ppermute x6 -> x8, waiting for transfers between devices: 12.9 us -> 12.1 us  [the longest x2 7.85 us: exchange(): lax.ppermute(corner, ('rows', 'cols'), both)]
  transfers between devices with their start and end apart: 8 -> 8, of which waited for: 4 -> 4; matrix products, arithmetic and copies ran while one was open for 0% -> 0% of each run, Pallas kernels for 7% -> 0%
where the time goes in v2:
time: 101 us
  blocking collectives  41.8 us (41%)
  Pallas kernels  27 us (27%)
  starting transfers between devices  19.1 us (19%)
  waiting for transfers between devices  12.1 us (12%)
    all_to_all x2, blocking collectives, send_parts(): lax.all_to_all(parts, ('rows', 'cols'), 0, 0, axis_index_groups=groups, t...  41.8 us
    pallas_call x5, Pallas kernels, call(): pl.pallas_call(kernel, in_specs=[VMEM] * len(args) + [FAR] * len(far_args...  24.3 us
    ppermute x2, waiting for transfers between devices, exchange(): lax.ppermute(corner, ('rows', 'cols'), both)  7.85 us
    ppermute x2, starting transfers between devices, swap(): lax.ppermute(value, 'cols', [(c, c ^ 1) for c in range(lax.axis_size('col...  6.94 us
    ppermute x2, starting transfers between devices, exchange(): lax.ppermute(corner, ('rows', 'cols'), both)  5.16 us
    ppermute x2, starting transfers between devices, exchange(): lax.ppermute(row_strip, 'rows', down)  4.89 us
    ppermute x2, waiting for transfers between devices, swap(): lax.ppermute(value, 'cols', [(c, c ^ 1) for c in range(lax.axis_size('col...  4.2 us
    pallas_call x1, Pallas kernels, per_device(): pl.pallas_call(unpack, in_specs=[VMEM, VMEM], out_specs=[FAR if n in WEIG...  2.67 us
  transfers between devices with their start and end apart: 8, of which 4 were waited for; matrix products, arithmetic and copies ran while one was open for 0% of the time, Pallas kernels for 0%

profile of v2, /device:TPU:1, one launch (start us, length us, event | category | flops | bytes accessed | tf_op | source)
XLA Modules:
  0.0 100.8 jit_solution(18048803881035630328)
XLA Ops:
  0.6 5.8 %first_forward.1 = (bf16[16,16,192]{2,1,0:T(8,128)(2,1)S(1)}, bf16[128,192]{1,0:T(8,128)(2,1)S(1)}, bf16[128,192]{1,0:T(8,128)(2,1)S(1)}, bf16[32,192]{1,0:T(8,1...) custom-call(bf16[16,16,192]{2,1,0:T(8,128)(2,1)} %refs_0_.1, ...), custom_call_target="tpu_custom_call" | custom-call | flops 5000000000 | bytes 4000000 | tf_op jit(solution)/shard_map/first_forward/pallas_call | solution.py:549
  6.5 1.4 %collective-permute-start = (bf16[128,192]{1,0:T(8,128)(2,1)S(1)}, bf16[128,192]{1,0:T(8,128)(2,1)S(1)}, u32[]{:S(2)}, u32[]{:S(2)}) collective-permute-start(bf16[128,192]{1,0:T(8,128)(2,1)S(1)} %get-tuple-element.50), channel_id=1, source_target_pairs={{0,15},{1,0},{2,1},{3,2},{4,3},{5,4},{6,5},{7,6},{8,7},{9,8},{10,9... | collective-permute-start | bytes 147464 | tf_op jit(solution)/shard_map/ppermute | solution.py:577
  7.9 4.9 %collective-permute-start.1 = (bf16[128,192]{1,0:T(8,128)(2,1)S(1)}, bf16[128,192]{1,0:T(8,128)(2,1)S(1)}, u32[]{:S(2)}, u32[]{:S(2)}) collective-permute-start(bf16[128,192]{1,0:T(8,128)(2,1)S(1)} %get-tuple-element.51), channel_id=1, source_target_pairs={{0,112},{16,0},{32,16},{48,32},{64,48},{80,64},{96,80},{112,96},{1... | collective-permute-start | bytes 147464 | tf_op jit(solution)/shard_map/ppermute | solution.py:578
  12.8 5.2 %collective-permute-start.2 = (bf16[32,192]{1,0:T(8,128)(2,1)S(1)}, bf16[32,192]{1,0:T(8,128)(2,1)S(1)}, u32[]{:S(2)}, u32[]{:S(2)}) collective-permute-start(bf16[32,192]{1,0:T(8,128)(2,1)S(1)} %get-tuple-element.52), channel_id=1, source_target_pairs={{0,127},{1,112},{2,113},{3,114},{4,115},{5,116},{6,117},{7,118},{8... | collective-permute-start | bytes 36872 | tf_op jit(solution)/shard_map/ppermute | solution.py:579
  18.0 0.9 collective-permute-done.2.refs_3_
  18.8 0.0 collective-permute-done.refs_1_
  18.8 0.0 collective-permute-done.1.refs_2_
  18.8 9.9 %second_block.1 = (bf16[16,16,192]{2,1,0:T(8,128)(2,1)S(1)}, bf16[16,16,192]{2,1,0:T(8,128)(2,1)S(1)}, bf16[128,192]{1,0:T(8,128)(2,1)S(1)}, bf16[128,192]{1,0:T...) custom-call(bf16[16,16,192]{2,1,0:T(8,128)(2,1)S(1)} %get-tuple-element.49.refs_0_, ...), custom_call_target="tpu_custom_call" | custom-call | flops 10000000000 | bytes 4000000 | tf_op jit(solution)/shard_map/second_block/pallas_call | solution.py:549
  28.8 0.7 collective-permute-start.3
  29.4 0.0 collective-permute-start.4
  29.4 0.0 collective-permute-start.5
  29.4 7.0 %collective-permute-done.5.refs_4_ = bf16[32,192]{1,0:T(8,128)(2,1)S(1)} collective-permute-done((bf16[32,192]{1,0:T(8,128)(2,1)S(1)}, bf16[32,192]{1,0:T(8,128)(2,1)S(1)}, u32[]{:S(2)}, u32[]{:S(2)}) %collective-permute-start.5) | collective-permute-done | bytes 12320 | tf_op jit(solution)/shard_map/ppermute | solution.py:579
  36.4 0.0 collective-permute-done.3.refs_2_
  36.4 0.0 collective-permute-done.4.refs_3_
  36.4 8.2 %first_backward.1 = (bf16[16,16,192]{2,1,0:T(8,128)(2,1)}, bf16[16,16,192]{2,1,0:T(8,128)(2,1)}, bf16[3584,128]{1,0:T(8,128)(2,1)S(1)}, bf16[3584,128]{1,0:T(8,128)(2,1)S(1)}) custom-call(bf16[16,16,192]{2,1,0:T(8,128)(2,1)S(1)} %get-tuple-element.53.refs_0_, bf16[16,16,192]{2,1,0:T(8,128)(2,1)S(1)} %get-tuple-element.54.refs_1_, ...), custom_call_target="tpu_custom_call" | custom-call | flops 5000000000 | bytes 4000000 | tf_op jit(solution)/shard_map/first_backward/pallas_call | solution.py:549
  44.6 3.9 %collective-permute-start.6 = (bf16[3584,128]{1,0:T(8,128)(2,1)S(1)}, bf16[3584,128]{1,0:T(8,128)(2,1)S(1)}, u32[]{:S(2)}, u32[]{:S(2)}) collective-permute-start(bf16[3584,128]{1,0:T(8,128)(2,1)S(1)} %get-tuple-element.69), channel_id=1, source_target_pairs={{0,1},{1,0},{2,3},{3,2},{4,5},{5,4},{6,7},{7,6},{8,9},{9,8},{10,11... | collective-permute-start | bytes 2752520 | tf_op jit(solution)/shard_map/ppermute | solution.py:584
  48.5 2.1 %collective-permute-done.6.got = bf16[3584,128]{1,0:T(8,128)(2,1)S(1)} collective-permute-done((bf16[3584,128]{1,0:T(8,128)(2,1)S(1)}, bf16[3584,128]{1,0:T(8,128)(2,1)S(1)}, u32[]{:S(2)}, u32[]{:S(2)}) %collective-permute-start.6) | collective-permute-done | bytes 917536 | tf_op jit(solution)/shard_map/ppermute | solution.py:584
  50.6 0.2 add_pair.1
  50.8 21.9 %all_to_all.10 = bf16[64,56,128]{2,1,0:T(8,128)(2,1)S(1)} all-to-all(bf16[64,56,128]{2,1,0:T(8,128)(2,1)S(1)} %bitcast.12), channel_id=1, replica_groups={{0,2,4,6,8,10,12,14,16,18,20,22,24,26,28,30,32,34,36,38,40,42,44,46,48,..., dimensions={0} | all-to-all | bytes 1835008 | tf_op jit(solution)/shard_map/all_to_all | solution.py:592
  72.7 0.2 sum_spread.1
  72.9 19.9 %all_to_all.11 = bf16[64,56,128]{2,1,0:T(8,128)(2,1)S(1)} all-to-all(bf16[64,56,128]{2,1,0:T(8,128)(2,1)S(1)} %bitcast.11), channel_id=1, replica_groups={{0,2,4,6,8,10,12,14,16,18,20,22,24,26,28,30,32,34,36,38,40,42,44,46,48,..., dimensions={0} | all-to-all | bytes 1835008 | tf_op jit(solution)/shard_map/all_to_all | solution.py:592
  92.8 3.0 %collective-permute-start.7 = (bf16[3584,128]{1,0:T(8,128)(2,1)S(1)}, bf16[3584,128]{1,0:T(8,128)(2,1)S(1)}, u32[]{:S(2)}, u32[]{:S(2)}) collective-permute-start(bf16[3584,128]{1,0:T(8,128)(2,1)S(1)} %bitcast.8), channel_id=1, source_target_pairs={{0,1},{1,0},{2,3},{3,2},{4,5},{5,4},{6,7},{7,6},{8,9},{9,8},{10,11... | collective-permute-start | bytes 2752520 | tf_op jit(solution)/shard_map/ppermute | solution.py:584
  95.8 2.1 %collective-permute-done.7.other = bf16[3584,128]{1,0:T(8,128)(2,1)S(1)} collective-permute-done((bf16[3584,128]{1,0:T(8,128)(2,1)S(1)}, bf16[3584,128]{1,0:T(8,128)(2,1)S(1)}, u32[]{:S(2)}, u32[]{:S(2)}) %collective-permute-start.7) | collective-permute-done | bytes 917536 | tf_op jit(solution)/shard_map/ppermute | solution.py:584
  97.9 2.7 %unpack.1 = (f32[2,192]{1,0:T(2,128)}, f32[2,192]{1,0:T(2,128)}, f32[2,192,576]{2,1,0:T(8,128)}, f32[2,576]{1,0:T(2,128)}, f32[6,2,225]{2,1,0:T(2,128)}, /*index...) custom-call(bf16[3584,128]{1,0:T(8,128)(2,1)S(1)} %bitcast.9, ...), custom_call_target="tpu_custom_call" | custom-call | tf_op jit(solution)/shard_map/unpack/pallas_call | solution.py:660
Async XLA Ops:
  6.5 12.4 %collective-permute-start = (bf16[128,192]{1,0:T(8,128)(2,1)S(1)}, bf16[128,192]{1,0:T(8,128)(2,1)S(1)}, u32[]{:S(2)}, u32[]{:S(2)}) collective-permute-start(bf16[128,192]{1,0:T(8,128)(2,1)S(1)} %get-tuple-element.50), channel_id=1, source_target_pairs={{0,15},{1,0},{2,1},{3,2},{4,3},{5,4},{6,5},{7,6},{8,7},{9,8},{10,9... | collective-permute-start | bytes 147464 | tf_op jit(solution)/shard_map/ppermute | solution.py:577
  7.9 10.9 %collective-permute-start.1 = (bf16[128,192]{1,0:T(8,128)(2,1)S(1)}, bf16[128,192]{1,0:T(8,128)(2,1)S(1)}, u32[]{:S(2)}, u32[]{:S(2)}) collective-permute-start(bf16[128,192]{1,0:T(8,128)(2,1)S(1)} %get-tuple-element.51), channel_id=1, source_target_pairs={{0,112},{16,0},{32,16},{48,32},{64,48},{80,64},{96,80},{112,96},{1... | collective-permute-start | bytes 147464 | tf_op jit(solution)/shard_map/ppermute | solution.py:578
  12.8 6.0 %collective-permute-start.2 = (bf16[32,192]{1,0:T(8,128)(2,1)S(1)}, bf16[32,192]{1,0:T(8,128)(2,1)S(1)}, u32[]{:S(2)}, u32[]{:S(2)}) collective-permute-start(bf16[32,192]{1,0:T(8,128)(2,1)S(1)} %get-tuple-element.52), channel_id=1, source_target_pairs={{0,127},{1,112},{2,113},{3,114},{4,115},{5,116},{6,117},{7,118},{8... | collective-permute-start | bytes 36872 | tf_op jit(solution)/shard_map/ppermute | solution.py:579
  28.8 7.7 %collective-permute-start.3 = (bf16[128,192]{1,0:T(8,128)(2,1)S(1)}, bf16[128,192]{1,0:T(8,128)(2,1)S(1)}, u32[]{:S(2)}, u32[]{:S(2)}) collective-permute-start(bf16[128,192]{1,0:T(8,128)(2,1)S(1)} %get-tuple-element.55), channel_id=1, source_target_pairs={{0,1},{1,2},{2,3},{3,4},{4,5},{5,6},{6,7},{7,8},{8,9},{9,10},{10,1... | collective-permute-start | bytes 147464 | tf_op jit(solution)/shard_map/ppermute | solution.py:577
  29.4 7.0 %collective-permute-start.4 = (bf16[128,192]{1,0:T(8,128)(2,1)S(1)}, bf16[128,192]{1,0:T(8,128)(2,1)S(1)}, u32[]{:S(2)}, u32[]{:S(2)}) collective-permute-start(bf16[128,192]{1,0:T(8,128)(2,1)S(1)} %get-tuple-element.56), channel_id=1, source_target_pairs={{0,16},{16,32},{32,48},{48,64},{64,80},{80,96},{96,112},{112,0},{1... | collective-permute-start | bytes 147464 | tf_op jit(solution)/shard_map/ppermute | solution.py:578
  29.4 7.0 %collective-permute-start.5 = (bf16[32,192]{1,0:T(8,128)(2,1)S(1)}, bf16[32,192]{1,0:T(8,128)(2,1)S(1)}, u32[]{:S(2)}, u32[]{:S(2)}) collective-permute-start(bf16[32,192]{1,0:T(8,128)(2,1)S(1)} %get-tuple-element.57), channel_id=1, source_target_pairs={{0,17},{1,18},{2,19},{3,20},{4,21},{5,22},{6,23},{7,24},{8,25},{9,... | collective-permute-start | bytes 36872 | tf_op jit(solution)/shard_map/ppermute | solution.py:579
  44.6 6.0 %collective-permute-start.6 = (bf16[3584,128]{1,0:T(8,128)(2,1)S(1)}, bf16[3584,128]{1,0:T(8,128)(2,1)S(1)}, u32[]{:S(2)}, u32[]{:S(2)}) collective-permute-start(bf16[3584,128]{1,0:T(8,128)(2,1)S(1)} %get-tuple-element.69), channel_id=1, source_target_pairs={{0,1},{1,0},{2,3},{3,2},{4,5},{5,4},{6,7},{7,6},{8,9},{9,8},{10,11... | collective-permute-start | bytes 2752520 | tf_op jit(solution)/shard_map/ppermute | solution.py:584
  92.8 5.1 %collective-permute-start.7 = (bf16[3584,128]{1,0:T(8,128)(2,1)S(1)}, bf16[3584,128]{1,0:T(8,128)(2,1)S(1)}, u32[]{:S(2)}, u32[]{:S(2)}) collective-permute-start(bf16[3584,128]{1,0:T(8,128)(2,1)S(1)} %bitcast.8), channel_id=1, source_target_pairs={{0,1},{1,0},{2,3},{3,2},{4,5},{5,4},{6,7},{7,6},{8,9},{9,8},{10,11... | collective-permute-start | bytes 2752520 | tf_op jit(solution)/shard_map/ppermute | solution.py:584

commit v3 on v2

--- a/solution.py
+++ b/solution.py
@@ -6,6 +6,7 @@
 from jax.experimental import pallas as pl
 from jax.experimental.pallas import tpu as pltpu
 from jax.sharding import PartitionSpec as P
+
 
 F32 = jnp.float32
 BF16 = jnp.bfloat16
@@ -171,33 +172,62 @@
             flat[first : first + C, :] = wide[:, j : j + 128]
 
 
-def backward(dout, x, par, need, cols, res, flat, small, du_ref, dpacked, rel_sum):
-    left = halves()
+def mlp_grads(g, flat, small):
+    ones = jnp.ones((8, TOK), BF16)
+    small[...] = jnp.zeros(small.shape, F32)
+    put_row(small, 21, dot_nt(ones, g["dout"][...]))
+    put_row(small, 15, dot_nt(ones, g["du"][...]))
+    put_row(small, 13, dot_nt(ones, g["dn2"][...]))
+    put_row(small, 11, dot_nt(ones, g["dg2"][...]))
+    put_pairs(flat, 1152, g["n2"][...], g["du"], MLP)
+    put_pairs(flat, 2304, g["dout"][...], g["hidden"], MLP)
+
+
+def attention_grads(g, flat, small):
     ones = jnp.ones((8, TOK), BF16)
     none = jnp.zeros((64, TOK), BF16)
-    small[...] = jnp.zeros(small.shape, F32)
-    put_row(small, 21, dot_nt(ones, dout))
+    put_row(small, 9, dot_nt(ones, g["dmid"][...]))
+    flat[960:1152, :] = dot_nt(g["mixed"][...], g["dmid"][0:128, :]).astype(BF16)
+    mirror = ((127 - iota((128, 128), 0)) == spread(iota((128, 128), 1))).astype(BF16)
+    for h in range(HEADS):
+        high, mid, _ = split3(g["rel"][h])
+        back = dot_nt(high, mirror) + dot_nt(mid, mirror)
+        total = jnp.zeros((8, 256), F32)
+        for ky in range(8):
+            wide = jnp.concatenate([back[8 * ky : 8 * ky + 8], jnp.zeros((8, 128), F32)], axis=1)
+            total = total + pltpu.roll(wide, 121 - SPAN * (7 - ky), 1, stride=1, stride_axis=0)
+        total = jnp.sum(total, axis=0, keepdims=True)
+        small[24 + h : 25 + h, :] = total[:, 0:128]
+        small[32 + h : 33 + h, :] = total[:, 128:256]
+    put_pairs(flat, 0, g["n1"][...], g["dpacked"], 512)
+    tail = dot_nt(g["n1"][...], jnp.concatenate([g["dpacked"][512:576, :], none], axis=0))
+    tail = tail + dot_nt(g["mixed"][...], jnp.concatenate([none, g["dmid"][128:192, :]], axis=0))
+    flat[768:960, :] = tail.astype(BF16)
+    put_row(small, 4, dot_nt(ones, g["dpacked"][...]))
+    put_row(small, 2, dot_nt(ones, g["dn1"][...]))
+    put_row(small, 0, dot_nt(ones, g["dg1"][...]))
+    flat[SMALL : SMALL + 48, :] = small[...].astype(BF16)
+    flat[SMALL + 48 : FLAT, :] = jnp.zeros((FLAT - SMALL - 48, 128), BF16)
+
+
+def backward(x, par, need, cols, res, g, after_mlp):
+    left = halves()
+    dout = g["dout"][...]
     need("dw", "slope")
     for i in range(0, MLP, 128):
         dh = dot_tn(par["dw"][:, i : i + 128], dout).astype(BF16).astype(F32)
-        du = (dh * res["slope"][i : i + 128, :].astype(F32)).astype(BF16)
-        du_ref[i : i + 128, :] = du
+        g["du"][i : i + 128, :] = (dh * res["slope"][i : i + 128, :].astype(F32)).astype(BF16)
     need("middle", "uw")
-    middle = res["middle"][...].astype(F32)
-    xhat, rstd = norm_fwd(middle)
-    normed = (xhat * cols[0:C, 3:4] + cols[0:C, 4:5]).astype(BF16)
-    put_pairs(flat, 1152, normed, du_ref, MLP)
-    need("hidden")
-    put_pairs(flat, 2304, dout, res["hidden"], MLP)
-    put_row(small, 15, dot_nt(ones, du_ref[...]))
-    dn = dot_nn(par["uw"][...], du_ref[...]).astype(BF16)
-    put_row(small, 13, dot_nt(ones, dn))
+    xhat, rstd = norm_fwd(res["middle"][...].astype(F32))
+    g["n2"][...] = (xhat * cols[0:C, 3:4] + cols[0:C, 4:5]).astype(BF16)
+    dn = dot_nn(par["uw"][...], g["du"][...]).astype(BF16)
+    g["dn2"][...] = dn
     dn = dn.astype(F32)
-    put_row(small, 11, dot_nt(ones, (dn * xhat).astype(BF16)))
+    g["dg2"][...] = (dn * xhat).astype(BF16)
     dmid = (dout.astype(F32) + norm_bwd(dn, xhat, rstd, cols[0:C, 3:4])).astype(BF16)
+    g["dmid"][...] = dmid
+    after_mlp()
     need("pw", "mixed")
-    put_row(small, 9, dot_nt(ones, dmid))
-    flat[960:1152, :] = dot_nt(res["mixed"][...], dmid[0:128]).astype(BF16)
     dmixed = dot_nn(par["pw"][...], dmid).astype(BF16)
     need("packed", "attn")
     for h in range(HEADS):
@@ -213,35 +243,18 @@
             ds = a * (da - jnp.sum(da * a, axis=0, keepdims=True))
             drel = ds if drel is None else drel + ds
             wide = stack_windows(ds * SCALE, left)
-            dpacked[DIM * h : DIM * h + DIM, lanes] = dot_nn(k, wide).astype(BF16)
-            dpacked[C + DIM * h : C + DIM * h + DIM, lanes] = dot_nt(q, wide).astype(BF16)
-            dpacked[2 * C + DIM * h : 2 * C + DIM * h + DIM, lanes] = dot_nt(dm, stack_windows(a, left)).astype(BF16)
-        rel_sum[h] = drel
-    mirror = ((127 - iota((128, 128), 0)) == spread(iota((128, 128), 1))).astype(BF16)
-    for h in range(HEADS):
-        high, mid, _ = split3(rel_sum[h])
-        back = dot_nt(high, mirror) + dot_nt(mid, mirror)
-        total = jnp.zeros((8, 256), F32)
-        for ky in range(8):
-            wide = jnp.concatenate([back[8 * ky : 8 * ky + 8], jnp.zeros((8, 128), F32)], axis=1)
-            total = total + pltpu.roll(wide, 121 - SPAN * (7 - ky), 1, stride=1, stride_axis=0)
-        total = jnp.sum(total, axis=0, keepdims=True)
-        small[24 + h : 25 + h, :] = total[:, 0:128]
-        small[32 + h : 33 + h, :] = total[:, 128:256]
+            g["dpacked"][DIM * h : DIM * h + DIM, lanes] = dot_nn(k, wide).astype(BF16)
+            g["dpacked"][C + DIM * h : C + DIM * h + DIM, lanes] = dot_nt(q, wide).astype(BF16)
+            dv = dot_nt(dm, stack_windows(a, left)).astype(BF16)
+            g["dpacked"][2 * C + DIM * h : 2 * C + DIM * h + DIM, lanes] = dv
+        g["rel"][h] = drel
     xhat, rstd = norm_fwd(x)
-    normed = (xhat * cols[0:C, 0:1] + cols[0:C, 1:2]).astype(BF16)
-    put_pairs(flat, 0, normed, dpacked, 512)
-    tail = dot_nt(normed, jnp.concatenate([dpacked[512:576, :], none], axis=0))
-    tail = tail + dot_nt(res["mixed"][...], jnp.concatenate([none, dmid[128:192]], axis=0))
-    flat[768:960, :] = tail.astype(BF16)
-    put_row(small, 4, dot_nt(ones, dpacked[...]))
+    g["n1"][...] = (xhat * cols[0:C, 0:1] + cols[0:C, 1:2]).astype(BF16)
     need("qw")
-    dn = dot_nn(par["qw"][...], dpacked[...]).astype(BF16)
-    put_row(small, 2, dot_nt(ones, dn))
+    dn = dot_nn(par["qw"][...], g["dpacked"][...]).astype(BF16)
+    g["dn1"][...] = dn
     dn = dn.astype(F32)
-    put_row(small, 0, dot_nt(ones, (dn * xhat).astype(BF16)))
-    flat[SMALL : SMALL + 48, :] = small[...].astype(BF16)
-    flat[SMALL + 48 : FLAT, :] = jnp.zeros((FLAT - SMALL - 48, 128), BF16)
+    g["dg1"][...] = (dn * xhat).astype(BF16)
     return dmid.astype(F32) + norm_bwd(dn, xhat, rstd, cols[0:C, 0:1])
 
 
@@ -299,6 +312,8 @@
 
 PAR_NAMES = ("ng", "nb", "qw", "qb", "rel", "pw", "pb", "mg", "mb", "uw", "ub", "dw", "db")
 RES_NAMES = ("packed", "attn", "mixed", "middle", "hidden", "slope")
+GRAD_NAMES = ("dout", "n1", "n2", "dmid", "dn1", "dn2", "dg1", "dg2", "du", "dpacked", "rel")
+GRAD_SHAPES = ((C, TOK),) * 8 + ((MLP, TOK), (576, TOK), (HEADS, 64, 128))
 RES_SHAPES = ((576, TOK), (12, 64, 128), (C, TOK), (C, TOK), (MLP, TOK), (MLP, TOK))
 
 
@@ -391,12 +406,11 @@
     far = dict(zip(PAR_NAMES, refs[5:18]))
     out_own, back_own = refs[18:20]
     strips = refs[20:23]
-    flat = refs[23]
-    grid, edge, vec, table, bias, sems = refs[24:30]
-    par = dict(zip(PAR_NAMES, refs[30:43]))
-    small, du_ref, dpacked, rel_sum = refs[43:47]
-    res = dict(zip(RES_NAMES, refs[47:53]))
-    cotangent = refs[53]
+    g = dict(zip(GRAD_NAMES + ("hidden", "mixed"), refs[23:36]))
+    grid, edge, vec, table, bias, sems = refs[36:42]
+    par = dict(zip(PAR_NAMES, refs[42:55]))
+    res = dict(zip(("packed", "attn", "middle", "slope"), refs[55:59]), hidden=g["hidden"], mixed=g["mixed"])
+    cotangent = refs[59]
     need = Copies(sems)
     start_params(need, VEC_NAMES, far, par, 1)
     start_params(need, ("rel", "qw", "pw"), far, par, 1)
@@ -411,15 +425,15 @@
     cols = load_columns(vec, par, 1)
     need("rel")
     position_bias(par, 1, table, bias)
-    out = forward(x, par, need, cols, bias, res, zones, nothing)
     need("cotangent")
     fill_grid(grid, edge, cotangent, strips_in, 1, 0, 0, 16, 16)
-    dout = to_channels(grid_get(grid, 4, 4)).astype(BF16)
+    g["dout"][...] = to_channels(grid_get(grid, 4, 4)).astype(BF16)
+    out = forward(x, par, need, cols, bias, res, zones, nothing)
     grid_put(grid, to_tokens(out.astype(F32)))
     for r in range(TILE):
         out_own[r] = grid[r, 0:TILE, 0:C].astype(BF16)
     emit_strips(grid, edge, strips, 0, 12, 12)
-    dx = backward(dout, x, par, need, cols, res, flat, small, du_ref, dpacked, rel_sum)
+    dx = backward(x, par, need, cols, res, g, nothing)
     grid_put(grid, to_tokens(dx))
     for r in range(TILE):
         back_own[r] = grid[r, 0:TILE, 0:C].astype(BF16)
@@ -427,25 +441,35 @@
     need.rest()
 
 
+def second_grads(*refs):
+    g = dict(zip(GRAD_NAMES + ("hidden", "mixed"), refs[0:13]))
+    flat, small = refs[13:]
+    mlp_grads(g, flat, small)
+    attention_grads(g, flat, small)
+
+
 BACK_NAMES = VEC_NAMES + WEIGHTS
 
 
 def first_backward(*refs):
-    out_in, back_in = refs[0:2]
-    strips_in = refs[2:5]
-    flat_two = refs[5]
-    far = dict(zip(BACK_NAMES, refs[6:18]))
-    xt_far = refs[18]
-    res_far = dict(zip(RES_NAMES, refs[19:25]))
-    output, grad, kept, sent = refs[25:29]
-    grid, edge, vec, sems = refs[29:33]
-    par = dict(zip(BACK_NAMES, refs[33:45]))
-    small, du_ref, dpacked, rel_sum = refs[45:49]
-    res = dict(zip(RES_NAMES, refs[49:55]))
-    xt, flat = refs[55:]
+    back_in = refs[0]
+    strips_in = refs[1:4]
+    flat_two = refs[4]
+    far = dict(zip(BACK_NAMES, refs[5:17]))
+    xt_far = refs[17]
+    res_far = dict(zip(RES_NAMES, refs[18:24]))
+    dx_channels, kept, sent = refs[24:27]
+    grid, edge, vec, sems = refs[27:31]
+    par = dict(zip(BACK_NAMES, refs[31:43]))
+    g = dict(zip(GRAD_NAMES, refs[43:54]))
+    res = dict(zip(RES_NAMES, refs[54:60]))
+    xt, flat, small = refs[60:]
+    g["hidden"] = res["hidden"]
+    g["mixed"] = res["mixed"]
     need = Copies(sems)
-    start_params(need, VEC_NAMES + ("dw",), far, par, 0)
+    start_params(need, ("dw",), far, par, 0)
     need.start("slope", res_far["slope"], res["slope"])
+    start_params(need, VEC_NAMES, far, par, 0)
     need.start("middle", res_far["middle"], res["middle"])
     start_params(need, ("uw",), far, par, 0)
     need.start("hidden", res_far["hidden"], res["hidden"])
@@ -456,24 +480,33 @@
     start_params(need, ("qw",), far, par, 0)
     need.start("xt", xt_far, xt)
     fill_grid(grid, edge, back_in, strips_in, 1, 4, 8, 0, 4)
-    dout = to_channels(grid_get(grid, 0, 4)).astype(BF16)
-    fill_grid(grid, edge, out_in, strips_in, 0, 4, 8, 0, 4)
-    for r in range(TILE):
-        output[r] = grid[r, 4:20, 0:C].astype(BF16)
+    g["dout"][...] = to_channels(grid_get(grid, 0, 4)).astype(BF16)
     need(*VEC_NAMES)
     cols = load_columns(vec, par, 0)
     need("xt")
     x = xt[...].astype(F32)
-    dx = backward(dout, x, par, need, cols, res, flat, small, du_ref, dpacked, rel_sum)
-    grid_put(grid, to_tokens(dx))
-    for r in range(TILE):
-        grad[r] = grid[r, 0:TILE, 0:C].astype(BF16)
+
+    def after_mlp():
+        need("hidden")
+        mlp_grads(g, flat, small)
+
+    dx_channels[...] = backward(x, par, need, cols, res, g, after_mlp).astype(BF16)
+    attention_grads(g, flat, small)
     even = lax.axis_index("cols") % 2 == 0
     for at in range(0, FLAT, 256):
         rows = slice(at, at + 256)
         kept[rows, :] = jnp.where(even, flat[rows, :], flat_two[rows, :])
         sent[rows, :] = jnp.where(even, flat_two[rows, :], flat[rows, :])
     need.rest()
+
+
+def make_tiles(out_own, col_in, row_in, corner_in, dx_channels, output, grad, grid, edge):
+    fill_grid(grid, edge, out_own, (col_in, row_in, corner_in), 0, 4, 8, 0, 4)
+    for r in range(TILE):
+        output[r] = grid[r, 4:20, 0:C].astype(BF16)
+    grid_put(grid, to_tokens(dx_channels[...].astype(F32)))
+    for r in range(TILE):
+        grad[r] = grid[r, 0:TILE, 0:C].astype(BF16)
 
 
 def add_pair(kept, got, out):
@@ -491,35 +524,45 @@
         out[at : at + share, :] = total
 
 
-def unpack(mine, other, *outs):
-    ng, nb, qw_far, qb, rel, pw_far, pb, mg, mb, uw_far, ub, dw_far, db, qw, pw, uw, dw, sems = outs
-    copies = Copies(sems)
+def unpack_weights(rows, b, near_refs, far_refs, copies):
+    qw, pw, uw, dw = near_refs
+    for j in range(4):
+        qw[:, 128 * j : 128 * j + 128] = rows(C * j, C)
+    tail = rows(768, C)
+    qw[:, 512:576] = tail[:, 0:64]
+    copies.start("qw", qw, far_refs[0].at[b])
+    pw[:, 128:192] = pltpu.roll(tail, 64, 1)[:, 0:64]
+    pw[:, 0:128] = rows(960, C)
+    copies.start("pw", pw, far_refs[1].at[b])
+    for j in range(6):
+        uw[:, 128 * j : 128 * j + 128] = rows(1152 + C * j, C)
+    copies.start("uw", uw, far_refs[2].at[b])
+    for j in range(6):
+        dw[:, 128 * j : 128 * j + 128] = rows(2304 + C * j, C)
+    copies.start("dw", dw, far_refs[3].at[b])
+
+
+def unpack_mine(mine, *refs):
+    copies = Copies(refs[8])
+    parity = lax.axis_index("cols") % 2
+    unpack_weights(lambda at, n: mine[at : at + n, :].astype(F32) * outs_factor, parity, refs[4:8], refs[0:4], copies)
+    copies.rest()
+
+
+def unpack_rest(mine, other, *refs):
+    ng, nb, qw_far, qb, rel, pw_far, pb, mg, mb, uw_far, ub, dw_far, db = refs[4:17]
+    copies = Copies(refs[21])
     factor = outs_factor
+    parity = lax.axis_index("cols") % 2
+    far_refs = (qw_far, pw_far, uw_far, dw_far)
+    unpack_weights(lambda at, n: other[at : at + n, :].astype(F32) * factor, 1 - parity, refs[17:21], far_refs, copies)
     flip = (iota((256, 256), 0) + iota((256, 256), 1) == 255).astype(BF16)
-    parity = lax.axis_index("cols") % 2
     for b in range(2):
 
         def raw(at, n):
             return jnp.where(parity == b, mine[at : at + n, :], other[at : at + n, :])
 
-        def rows(at, n):
-            return raw(at, n).astype(F32) * factor
-
-        for j in range(4):
-            qw[b, :, 128 * j : 128 * j + 128] = rows(C * j, C)
-        tail = rows(768, C)
-        qw[b, :, 512:576] = tail[:, 0:64]
-        copies.start(("qw", b), qw.at[b], qw_far.at[b])
-        pw[b, :, 128:192] = pltpu.roll(tail, 64, 1)[:, 0:64]
-        pw[b, :, 0:128] = rows(960, C)
-        copies.start(("pw", b), pw.at[b], pw_far.at[b])
-        for j in range(6):
-            uw[b, :, 128 * j : 128 * j + 128] = rows(1152 + C * j, C)
-        copies.start(("uw", b), uw.at[b], uw_far.at[b])
-        for j in range(6):
-            dw[b, :, 128 * j : 128 * j + 128] = rows(2304 + C * j, C)
-        copies.start(("dw", b), dw.at[b], dw_far.at[b])
-        small = rows(SMALL, 48)
+        small = raw(SMALL, 48).astype(F32) * factor
         for at, ref in ((0, ng), (2, nb), (4, qb), (9, pb), (11, mg), (13, mb), (15, ub), (21, db)):
             n = ref.shape[-1]
             for i in range(0, n, 128):
@@ -545,14 +588,13 @@
 FAR = pl.BlockSpec(memory_space=pltpu.HBM)
 
 
-def call(kernel, name, args, far_args, outs, far_outs, scratch, flops):
+def call(kernel, args, far_args, outs, far_outs, scratch, flops, plain=()):
     return pl.pallas_call(
         kernel,
         in_specs=[VMEM] * len(args) + [FAR] * len(far_args),
-        out_specs=[VMEM] * len(outs) + [FAR] * len(far_outs),
-        out_shape=list(outs) + [pltpu.HBM(o.shape, o.dtype) for o in far_outs],
+        out_specs=[VMEM] * (len(outs) + len(plain)) + [FAR] * len(far_outs),
+        out_shape=list(outs) + list(plain) + [pltpu.HBM(o.shape, o.dtype) for o in far_outs],
         scratch_shapes=scratch,
-        name=name,
         compiler_params=pltpu.CompilerParams(vmem_limit_bytes=30 * 2**20),
         cost_estimate=pl.CostEstimate(flops=flops, transcendentals=0, bytes_accessed=4000000),
     )(*[near(a) for a in args], *[pltpu.with_memory_space_constraint(a, pltpu.HBM) for a in far_args])
@@ -593,7 +635,7 @@
     return got.reshape(value.shape)
 
 
-def per_device(imagery, cotangent, *params):
+def both_blocks(imagery, cotangent, *params):
     params = list(params)
     params[4] = params[4].transpose(1, 0, 2)
     params[11] = params[11].swapaxes(1, 2)
@@ -605,12 +647,6 @@
     edge = pltpu.VMEM((64, 256), F32)
     vec = pltpu.VMEM((128, MLP), F32)
     tables = [pltpu.VMEM((8, 256), F32), pltpu.VMEM((HEADS, 64, 128), F32)]
-    work = [
-        pltpu.VMEM((48, 128), F32),
-        pltpu.VMEM((MLP, TOK), BF16),
-        pltpu.VMEM((576, TOK), BF16),
-        pltpu.VMEM((HEADS, 64, 128), F32),
-    ]
     par = dict(zip(PAR_NAMES, params))
     par_kinds = {n: BF16 if n in WEIGHTS else F32 for n in PAR_NAMES}
     par_vmem = {n: pltpu.VMEM(PAR_SHAPES[n], par_kinds[n]) for n in PAR_NAMES}
@@ -618,7 +654,6 @@
     sems = pltpu.SemaphoreType.DMA((32,))
     one = call(
         first_forward,
-        "first_forward",
         (),
         (imagery, cotangent, *params),
         [held] + strips,
@@ -627,45 +662,54 @@
         5 * 10**9,
     )
     own, got, xt, res = one[0], exchange(one[1:4], -1), one[4], one[5:]
+    channels = pltpu.VMEM((C, TOK), BF16)
+    grad_vmem = [pltpu.VMEM(s, F32 if n == "rel" else BF16) for n, s in zip(GRAD_NAMES, GRAD_SHAPES)]
+    small = pltpu.VMEM((48, 128), F32)
     two = call(
         second_block,
-        "second_block",
         (own, *got),
         (cotangent, *params),
-        [held, held] + strips + [packed_grads],
+        [held, held] + strips + grad_vmem + [res_vmem[4], res_vmem[2]],
         [],
-        [grid, edge, vec] + tables + [sems] + list(par_vmem.values()) + work + res_vmem + [held],
+        [grid, edge, vec] + tables + [sems] + list(par_vmem.values()) + [res_vmem[i] for i in (0, 1, 3, 5)] + [held],
         10**10,
     )
     got = exchange(two[2:5], 1)
-    output, grad, kept, sent = call(
+    flat_two = call(second_grads, two[5:], (), [packed_grads], [], [small], 10**9)[0]
+    dx, kept, sent = call(
         first_backward,
-        "first_backward",
-        (two[0], two[1], *got, two[5]),
+        (two[1], *got, flat_two),
         (*[par[n] for n in BACK_NAMES], xt, *res),
-        [shaped(tile), shaped(tile), packed_grads, packed_grads],
+        [channels, packed_grads, packed_grads],
         [],
         [grid, edge, vec, sems]
         + [par_vmem[n] for n in BACK_NAMES]
-        + work
+        + grad_vmem
         + res_vmem
-        + [pltpu.VMEM((C, TOK), BF16), packed_grads],
+        + [channels, packed_grads, small],
         5 * 10**9,
     )
-    pair = call(add_pair, "add_pair", (kept, swap(sent)), (), [packed_grads], [], [], 10**6)[0]
+    sent = swap(sent)
+    tiles = [shaped(tile), shaped(tile)]
+    output, grad = call(make_tiles, (two[0], *got, dx), (), [], [], [grid, edge], 10**9, plain=tiles)
+    parts = send_parts(call(add_pair, (kept, sent), (), [packed_grads], [], [], 10**6)[0])
     share = 2 * FLAT // (lax.axis_size("rows") * lax.axis_size("cols"))
-    spread = functools.partial(sum_spread, share)
-    mine = send_parts(call(spread, "sum_spread", (send_parts(pair),), (), [packed_grads], [], [], 10**6)[0])
-    weights = [pltpu.VMEM((2,) + PAR_SHAPES[n], F32) for n in ("qw", "pw", "uw", "dw")]
+    spread_sum = functools.partial(sum_spread, share)
+    mine = send_parts(call(spread_sum, (parts,), (), [packed_grads], [], [], 10**6)[0])
+    weights = [pltpu.VMEM(PAR_SHAPES[n], F32) for n in WEIGHTS]
+    weights_far = [pltpu.HBM((2,) + PAR_SHAPES[n], F32) for n in WEIGHTS]
+    few_sems = pltpu.SemaphoreType.DMA((4,))
+    half = call(unpack_mine, (mine,), (), [], weights_far, weights + [few_sems], 10**9)
     grads = pl.pallas_call(
-        unpack,
-        in_specs=[VMEM, VMEM],
+        unpack_rest,
+        in_specs=[VMEM, VMEM] + [FAR] * 4,
         out_specs=[FAR if n in WEIGHTS else VMEM for n in PAR_NAMES],
-        out_shape=[shaped(p.shape, F32) for p in params],
-        scratch_shapes=weights + [pltpu.SemaphoreType.DMA((8,))],
-        name="unpack",
+        out_shape=[pltpu.HBM(p.shape, F32) if n in WEIGHTS else shaped(p.shape, F32) for n, p in zip(PAR_NAMES, params)],
+        scratch_shapes=weights + [few_sems],
+        input_output_aliases={2: 2, 3: 5, 4: 9, 5: 11},
+        name="unpack_rest",
         compiler_params=pltpu.CompilerParams(vmem_limit_bytes=30 * 2**20),
-    )(near(mine), near(swap(mine)))
+    )(near(mine), near(swap(mine)), *[pltpu.with_memory_space_constraint(h, pltpu.HBM) for h in half])
     grads = list(grads)
     grads[4] = grads[4].transpose(1, 0, 2)
     grads[11] = grads[11].swapaxes(1, 2)
@@ -675,7 +719,7 @@
 def solution(mesh):
     tile = P("rows", "cols", None)
     return jax.shard_map(
-        per_device,
+        both_blocks,
         mesh=mesh,
         in_specs=(tile, tile) + (P(),) * 13,
         out_specs=(tile, tile) + (P(),) * 13,

time: 101 us -> 96.9 us (0.959)
  waiting for transfers between devices: 12.1 us -> 7.59 us
    ppermute x2, waiting for transfers between devices: 7.85 us -> 5.06 us  [exchange(): lax.ppermute(corner, ('rows', 'cols'), both)]
    ppermute x2, waiting for transfers between devices: 4.2 us -> 2.1 us  [swap(): lax.ppermute(value, 'cols', [(c, c ^ 1) for c in range(lax.axis_size('col...]
    pallas_call x5 -> x8, Pallas kernels: 24.3 us -> 24.6 us  [call(): pl.pallas_call(kernel, in_specs=[VMEM] * len(args) + [FAR] * len(far_args...]
  transfers between devices with their start and end apart: 8 -> 8, of which waited for: 4 -> 4; matrix products, arithmetic and copies ran while one was open for 0% -> 0% of each run, Pallas kernels for 0% -> 3%
where the time goes in v3:
time: 96.9 us; the launch traced here: 96.6 us
  blocking collectives  42.5 us (44%)
  Pallas kernels  26.6 us (27%)
  starting transfers between devices  19 us (20%)
  waiting for transfers between devices  7.59 us (8%)
    all_to_all x2, blocking collectives, send_parts(): lax.all_to_all(parts, ('rows', 'cols'), 0, 0, axis_index_groups=groups, t...  42.5 us
    pallas_call x8, Pallas kernels, call(): pl.pallas_call(kernel, in_specs=[VMEM] * len(args) + [FAR] * len(far_args...  24.6 us
    ppermute x2, starting transfers between devices, swap(): lax.ppermute(value, 'cols', [(c, c ^ 1) for c in range(lax.axis_size('col...  6.69 us
    ppermute x2, starting transfers between devices, exchange(): lax.ppermute(corner, ('rows', 'cols'), both)  5.24 us
    ppermute x2, waiting for transfers between devices, exchange(): lax.ppermute(corner, ('rows', 'cols'), both)  5.06 us
    ppermute x2, starting transfers between devices, exchange(): lax.ppermute(row_strip, 'rows', down)  4.95 us
    ppermute x2, starting transfers between devices, exchange(): lax.ppermute(col_strip, 'cols', along)  2.11 us
    ppermute x2, waiting for transfers between devices, swap(): lax.ppermute(value, 'cols', [(c, c ^ 1) for c in range(lax.axis_size('col...  2.1 us
  transfers between devices with their start and end apart: 8, of which 4 were waited for; matrix products, arithmetic and copies ran while one was open for 0% of the time, Pallas kernels for 3%

profile of v3, /device:TPU:1, one launch (start us, length us, event | category | flops | bytes accessed | tf_op | source)
XLA Modules:
  0.0 96.6 jit_solution(15641379949171816091)
XLA Ops:
  0.6 5.8 %shard_map.262 = (bf16[16,16,192]{2,1,0:T(8,128)(2,1)S(1)}, bf16[128,192]{1,0:T(8,128)(2,1)S(1)}, bf16[128,192]{1,0:T(8,128)(2,1)S(1)}, bf16[32,192]{1,0:T(8,128...) custom-call(bf16[16,16,192]{2,1,0:T(8,128)(2,1)} %refs_0_.1, ...), custom_call_target="tpu_custom_call" | custom-call | flops 5000000000 | bytes 4000000 | tf_op jit(solution)/shard_map/pallas_call | solution.py:592
  6.5 1.4 %collective-permute-start = (bf16[128,192]{1,0:T(8,128)(2,1)S(1)}, bf16[128,192]{1,0:T(8,128)(2,1)S(1)}, u32[]{:S(2)}, u32[]{:S(2)}) collective-permute-start(bf16[128,192]{1,0:T(8,128)(2,1)S(1)} %get-tuple-element.67), channel_id=1, source_target_pairs={{0,15},{1,0},{2,1},{3,2},{4,3},{5,4},{6,5},{7,6},{8,7},{9,8},{10,9... | collective-permute-start | bytes 147464 | tf_op jit(solution)/shard_map/ppermute | solution.py:619
  7.9 4.9 %collective-permute-start.1 = (bf16[128,192]{1,0:T(8,128)(2,1)S(1)}, bf16[128,192]{1,0:T(8,128)(2,1)S(1)}, u32[]{:S(2)}, u32[]{:S(2)}) collective-permute-start(bf16[128,192]{1,0:T(8,128)(2,1)S(1)} %get-tuple-element.68), channel_id=1, source_target_pairs={{0,112},{16,0},{32,16},{48,32},{64,48},{80,64},{96,80},{112,96},{1... | collective-permute-start | bytes 147464 | tf_op jit(solution)/shard_map/ppermute | solution.py:620
  12.8 5.2 %collective-permute-start.2 = (bf16[32,192]{1,0:T(8,128)(2,1)S(1)}, bf16[32,192]{1,0:T(8,128)(2,1)S(1)}, u32[]{:S(2)}, u32[]{:S(2)}) collective-permute-start(bf16[32,192]{1,0:T(8,128)(2,1)S(1)} %get-tuple-element.69), channel_id=1, source_target_pairs={{0,127},{1,112},{2,113},{3,114},{4,115},{5,116},{6,117},{7,118},{8... | collective-permute-start | bytes 36872 | tf_op jit(solution)/shard_map/ppermute | solution.py:621
  18.0 0.9 collective-permute-done.2.refs_3_
  18.8 8.3 %shard_map.263 = (bf16[16,16,192]{2,1,0:T(8,128)(2,1)S(1)}, bf16[16,16,192]{2,1,0:T(8,128)(2,1)S(1)}, bf16[128,192]{1,0:T(8,128)(2,1)S(1)}, bf16[128,192]{1,0:T(...) custom-call(bf16[16,16,192]{2,1,0:T(8,128)(2,1)S(1)} %get-tuple-elem, ...), custom_call_target="tpu_custom_call" | custom-call | flops 10000000000 | bytes 4000000 | tf_op jit(solution)/shard_map/pallas_call | solution.py:592
  27.1 0.1 collective-permute-start.5
  27.2 0.7 collective-permute-start.3
  27.9 0.1 collective-permute-start.4
  27.9 1.1 %shard_map.264.refs_4_ = bf16[3584,128]{1,0:T(8,128)(2,1)S(1)} custom-call(bf16[192,256]{1,0:T(8,128)(2,1)S(1)} %get-tuple-element.75.refs_0_, bf16[192,256]{1,0:T(8,128)(2,1)S(1)} %get-tuple-element.76.refs_1_, bf16[192,256]{1,0:T(8,128)(2,1)S(1)} %get-tuple-element.77.refs_2_, bf16[192,256]{1,0:T(8,128)(2,1)S(1)} %get-tuple-element.78.refs_3_, ...), custom_call_target="tpu_custom_call" | custom-call | flops 1000000000 | bytes 4000000 | tf_op jit(solution)/shard_map/pallas_call | solution.py:592
  29.0 4.2 %collective-permute-done.5.refs_3_.corner_in = bf16[32,192]{1,0:T(8,128)(2,1)S(1)} collective-permute-done((bf16[32,192]{1,0:T(8,128)(2,1)S(1)}, bf16[32,192]{1,0:T(8,128)(2,1)S(1)}, u32[]{:S(2)}, u32[]{:S(2)}) %collective-permute-start.5) | collective-permute-done | bytes 12320 | tf_op jit(solution)/shard_map/ppermute | solution.py:621
  33.2 0.0 collective-permute-done.3.refs_1_.col_in
  33.2 0.4 collective-permute-done.4.refs_2_.row_in
  33.6 7.0 %shard_map.265 = (bf16[192,256]{1,0:T(8,128)(2,1)S(1)}, bf16[3584,128]{1,0:T(8,128)(2,1)S(1)}, bf16[3584,128]{1,0:T(8,128)(2,1)S(1)}) custom-call(bf16[16,16,192]{2,1,0:T(8,128)(2,1)S(1)} %get-tuple-element.74.refs_0_, bf16[128,192]{1,0:T(8,128)(2,1)S(1)} %collective-permute-done.3.refs_1_.col_in, ...), custom_call_target="tpu_custom_call" | custom-call | flops 5000000000 | bytes 4000000 | tf_op jit(solution)/shard_map/pallas_call | solution.py:592
  40.6 3.6 %collective-permute-start.6 = (bf16[3584,128]{1,0:T(8,128)(2,1)S(1)}, bf16[3584,128]{1,0:T(8,128)(2,1)S(1)}, u32[]{:S(2)}, u32[]{:S(2)}) collective-permute-start(bf16[3584,128]{1,0:T(8,128)(2,1)S(1)} %get-tuple-element.99), channel_id=1, source_target_pairs={{0,1},{1,0},{2,3},{3,2},{4,5},{5,4},{6,7},{7,6},{8,9},{9,8},{10,11... | collective-permute-start | bytes 2752520 | tf_op jit(solution)/shard_map/ppermute | solution.py:626
  44.2 2.1 %collective-permute-done.6.got = bf16[3584,128]{1,0:T(8,128)(2,1)S(1)} collective-permute-done((bf16[3584,128]{1,0:T(8,128)(2,1)S(1)}, bf16[3584,128]{1,0:T(8,128)(2,1)S(1)}, u32[]{:S(2)}, u32[]{:S(2)}) %collective-permute-start.6) | collective-permute-done | bytes 917536 | tf_op jit(solution)/shard_map/ppermute | solution.py:626
  46.3 0.2 shard_map.267
  46.5 22.6 %all_to_all.10 = bf16[64,56,128]{2,1,0:T(8,128)(2,1)S(1)} all-to-all(bf16[64,56,128]{2,1,0:T(8,128)(2,1)S(1)} %bitcast.13), channel_id=1, replica_groups={{0,2,4,6,8,10,12,14,16,18,20,22,24,26,28,30,32,34,36,38,40,42,44,46,48,..., dimensions={0} | all-to-all | bytes 1835008 | tf_op jit(solution)/shard_map/all_to_all | solution.py:634
  69.2 0.2 shard_map.268
  69.4 19.9 %all_to_all.11 = bf16[64,56,128]{2,1,0:T(8,128)(2,1)S(1)} all-to-all(bf16[64,56,128]{2,1,0:T(8,128)(2,1)S(1)} %bitcast.9), channel_id=1, replica_groups={{0,2,4,6,8,10,12,14,16,18,20,22,24,26,28,30,32,34,36,38,40,42,44,46,48,..., dimensions={0} | all-to-all | bytes 1835008 | tf_op jit(solution)/shard_map/all_to_all | solution.py:634
  89.3 3.1 %collective-permute-start.7 = (bf16[3584,128]{1,0:T(8,128)(2,1)S(1)}, bf16[3584,128]{1,0:T(8,128)(2,1)S(1)}, u32[]{:S(2)}, u32[]{:S(2)}) collective-permute-start(bf16[3584,128]{1,0:T(8,128)(2,1)S(1)} %bitcast.10), channel_id=1, source_target_pairs={{0,1},{1,0},{2,3},{3,2},{4,5},{5,4},{6,7},{7,6},{8,9},{9,8},{10,11... | collective-permute-start | bytes 2752520 | tf_op jit(solution)/shard_map/ppermute | solution.py:626
  92.4 0.8 shard_map.266
  93.1 1.3 %shard_map.269 = (f32[2,192,576]{2,1,0:T(8,128)}, f32[2,192,192]{2,1,0:T(8,128)}, f32[2,192,768]{2,1,0:T(8,128)}, f32[2,192,768]{2,1,0:T(8,128)}) custom-call(bf16[3584,128]{1,0:T(8,128)(2,1)S(1)} %bitcast.11), custom_call_target="tpu_custom_call" | custom-call | flops 1000000000 | bytes 4000000 | tf_op jit(solution)/shard_map/pallas_call | solution.py:592
  94.5 2.0 %unpack_rest.1 = (f32[2,192]{1,0:T(2,128)}, f32[2,192]{1,0:T(2,128)}, f32[2,192,576]{2,1,0:T(8,128)}, f32[2,576]{1,0:T(2,128)}, f32[6,2,225]{2,1,0:T(2,128)}, /*...) custom-call(bf16[3584,128]{1,0:T(8,128)(2,1)S(1)} %bitcast.12, ...), custom_call_target="tpu_custom_call", output_to_operand_aliasing={{2}: (2, {}), {5}: (3, {}), {9}: (4, {}), {11}: (5, {})} | custom-call | tf_op jit(solution)/shard_map/unpack_rest/pallas_call | solution.py:703
  (3 shorter events, 0.0 us)
Async XLA Ops:
  6.5 12.4 %collective-permute-start = (bf16[128,192]{1,0:T(8,128)(2,1)S(1)}, bf16[128,192]{1,0:T(8,128)(2,1)S(1)}, u32[]{:S(2)}, u32[]{:S(2)}) collective-permute-start(bf16[128,192]{1,0:T(8,128)(2,1)S(1)} %get-tuple-element.67), channel_id=1, source_target_pairs={{0,15},{1,0},{2,1},{3,2},{4,3},{5,4},{6,5},{7,6},{8,7},{9,8},{10,9... | collective-permute-start | bytes 147464 | tf_op jit(solution)/shard_map/ppermute | solution.py:619
  7.9 10.9 %collective-permute-start.1 = (bf16[128,192]{1,0:T(8,128)(2,1)S(1)}, bf16[128,192]{1,0:T(8,128)(2,1)S(1)}, u32[]{:S(2)}, u32[]{:S(2)}) collective-permute-start(bf16[128,192]{1,0:T(8,128)(2,1)S(1)} %get-tuple-element.68), channel_id=1, source_target_pairs={{0,112},{16,0},{32,16},{48,32},{64,48},{80,64},{96,80},{112,96},{1... | collective-permute-start | bytes 147464 | tf_op jit(solution)/shard_map/ppermute | solution.py:620
  12.8 6.0 %collective-permute-start.2 = (bf16[32,192]{1,0:T(8,128)(2,1)S(1)}, bf16[32,192]{1,0:T(8,128)(2,1)S(1)}, u32[]{:S(2)}, u32[]{:S(2)}) collective-permute-start(bf16[32,192]{1,0:T(8,128)(2,1)S(1)} %get-tuple-element.69), channel_id=1, source_target_pairs={{0,127},{1,112},{2,113},{3,114},{4,115},{5,116},{6,117},{7,118},{8... | collective-permute-start | bytes 36872 | tf_op jit(solution)/shard_map/ppermute | solution.py:621
  27.1 6.1 %collective-permute-start.5 = (bf16[32,192]{1,0:T(8,128)(2,1)S(1)}, bf16[32,192]{1,0:T(8,128)(2,1)S(1)}, u32[]{:S(2)}, u32[]{:S(2)}) collective-permute-start(bf16[32,192]{1,0:T(8,128)(2,1)S(1)} %get-tuple-element.73), channel_id=1, source_target_pairs={{0,17},{1,18},{2,19},{3,20},{4,21},{5,22},{6,23},{7,24},{8,25},{9,... | collective-permute-start | bytes 36872 | tf_op jit(solution)/shard_map/ppermute | solution.py:621
  27.2 6.0 %collective-permute-start.3 = (bf16[128,192]{1,0:T(8,128)(2,1)S(1)}, bf16[128,192]{1,0:T(8,128)(2,1)S(1)}, u32[]{:S(2)}, u32[]{:S(2)}) collective-permute-start(bf16[128,192]{1,0:T(8,128)(2,1)S(1)} %get-tuple-element.71), channel_id=1, source_target_pairs={{0,1},{1,2},{2,3},{3,4},{4,5},{5,6},{6,7},{7,8},{8,9},{9,10},{10,1... | collective-permute-start | bytes 147464 | tf_op jit(solution)/shard_map/ppermute | solution.py:619
  27.9 5.8 %collective-permute-start.4 = (bf16[128,192]{1,0:T(8,128)(2,1)S(1)}, bf16[128,192]{1,0:T(8,128)(2,1)S(1)}, u32[]{:S(2)}, u32[]{:S(2)}) collective-permute-start(bf16[128,192]{1,0:T(8,128)(2,1)S(1)} %get-tuple-element.72), channel_id=1, source_target_pairs={{0,16},{16,32},{32,48},{48,64},{64,80},{80,96},{96,112},{112,0},{1... | collective-permute-start | bytes 147464 | tf_op jit(solution)/shard_map/ppermute | solution.py:620
  40.6 5.7 %collective-permute-start.6 = (bf16[3584,128]{1,0:T(8,128)(2,1)S(1)}, bf16[3584,128]{1,0:T(8,128)(2,1)S(1)}, u32[]{:S(2)}, u32[]{:S(2)}) collective-permute-start(bf16[3584,128]{1,0:T(8,128)(2,1)S(1)} %get-tuple-element.99), channel_id=1, source_target_pairs={{0,1},{1,0},{2,3},{3,2},{4,5},{5,4},{6,7},{7,6},{8,9},{9,8},{10,11... | collective-permute-start | bytes 2752520 | tf_op jit(solution)/shard_map/ppermute | solution.py:626
  89.3 5.2 %collective-permute-start.7 = (bf16[3584,128]{1,0:T(8,128)(2,1)S(1)}, bf16[3584,128]{1,0:T(8,128)(2,1)S(1)}, u32[]{:S(2)}, u32[]{:S(2)}) collective-permute-start(bf16[3584,128]{1,0:T(8,128)(2,1)S(1)} %bitcast.10), channel_id=1, source_target_pairs={{0,1},{1,0},{2,3},{3,2},{4,5},{5,4},{6,7},{7,6},{8,9},{9,8},{10,11... | collective-permute-start | bytes 2752520 | tf_op jit(solution)/shard_map/ppermute | solution.py:626

commit v4 on v3

--- a/solution.py
+++ b/solution.py
@@ -153,8 +153,9 @@
         res["slope"][i : i + 128, :] = (half + u * (jnp.exp(-0.5 * u * u) * 0.3989422804014327)).astype(BF16)
     keep("middle")
     need("dw")
-    out = middle + dot_nn(par["dw"][...], res["hidden"][...]) + cols[0:C, 5:6]
-    return out.astype(BF16)
+    out = (middle + dot_nn(par["dw"][...], res["hidden"][...]) + cols[0:C, 5:6]).astype(BF16)
+    keep("hidden", "slope")
+    return out
 
 
 def put_row(small, at, row):
@@ -248,7 +249,8 @@
             dv = dot_nt(dm, stack_windows(a, left)).astype(BF16)
             g["dpacked"][2 * C + DIM * h : 2 * C + DIM * h + DIM, lanes] = dv
         g["rel"][h] = drel
-    xhat, rstd = norm_fwd(x)
+    need("xt")
+    xhat, rstd = norm_fwd(x[...].astype(F32))
     g["n1"][...] = (xhat * cols[0:C, 0:1] + cols[0:C, 1:2]).astype(BF16)
     need("qw")
     dn = dot_nn(par["qw"][...], g["dpacked"][...]).astype(BF16)
@@ -381,18 +383,15 @@
         grid[r, 0:TILE, 0:C] = imagery[r].astype(F32)
     x = to_channels(grid_get(grid, 0, 0))
     xt[...] = x.astype(BF16)
-    need(*VEC_NAMES)
+    need(*VEC_NAMES, "rel", "qw", "pw", "cotangent")
     cols = load_columns(vec, par, 0)
-    need("rel")
     position_bias(par, 0, table, bias)
-    need("cotangent")
     for r in range(TILE):
         grid[r, 0:TILE, 0:C] = cotangent[r].astype(F32)
     emit_strips(grid, edge, strips, 1, 0, 0)
     need.start("out xt", xt, xt_far)
     out = forward(x, par, need, cols, bias, res, None, keep)
     grid_put(grid, to_tokens(out.astype(F32)))
-    keep("hidden", "slope")
     for r in range(TILE):
         own[r] = grid[r, 0:TILE, 0:C].astype(BF16)
     emit_strips(grid, edge, strips, 0, 0, 0)
@@ -410,22 +409,20 @@
     grid, edge, vec, table, bias, sems = refs[36:42]
     par = dict(zip(PAR_NAMES, refs[42:55]))
     res = dict(zip(("packed", "attn", "middle", "slope"), refs[55:59]), hidden=g["hidden"], mixed=g["mixed"])
-    cotangent = refs[59]
+    cotangent, xt = refs[59:]
     need = Copies(sems)
-    start_params(need, VEC_NAMES, far, par, 1)
-    start_params(need, ("rel", "qw", "pw"), far, par, 1)
+    start_params(need, VEC_NAMES + ("rel",), far, par, 1)
     need.start("cotangent", cotangent_far, cotangent)
-    start_params(need, ("uw", "dw"), far, par, 1)
+    start_params(need, ("qw", "pw", "uw", "dw"), far, par, 1)
     last_row = lax.axis_index("rows") == lax.axis_size("rows") - 1
     last_col = lax.axis_index("cols") == lax.axis_size("cols") - 1
     zones = [same_zone(p, last_row, last_col) for p in range(2)]
     fill_grid(grid, edge, own_in, strips_in, 0, 0, 0, 16, 16)
     x = to_channels(grid_get(grid, 4, 4))
-    need(*VEC_NAMES)
+    xt[...] = x.astype(BF16)
+    need(*VEC_NAMES, "rel", "cotangent")
     cols = load_columns(vec, par, 1)
-    need("rel")
     position_bias(par, 1, table, bias)
-    need("cotangent")
     fill_grid(grid, edge, cotangent, strips_in, 1, 0, 0, 16, 16)
     g["dout"][...] = to_channels(grid_get(grid, 4, 4)).astype(BF16)
     out = forward(x, par, need, cols, bias, res, zones, nothing)
@@ -433,7 +430,7 @@
     for r in range(TILE):
         out_own[r] = grid[r, 0:TILE, 0:C].astype(BF16)
     emit_strips(grid, edge, strips, 0, 12, 12)
-    dx = backward(x, par, need, cols, res, g, nothing)
+    dx = backward(xt, par, need, cols, res, g, nothing)
     grid_put(grid, to_tokens(dx))
     for r in range(TILE):
         back_own[r] = grid[r, 0:TILE, 0:C].astype(BF16)
@@ -477,20 +474,18 @@
     start_params(need, ("pw",), far, par, 0)
     need.start("packed", res_far["packed"], res["packed"])
     need.start("attn", res_far["attn"], res["attn"])
+    need.start("xt", xt_far, xt)
     start_params(need, ("qw",), far, par, 0)
-    need.start("xt", xt_far, xt)
     fill_grid(grid, edge, back_in, strips_in, 1, 4, 8, 0, 4)
     g["dout"][...] = to_channels(grid_get(grid, 0, 4)).astype(BF16)
     need(*VEC_NAMES)
     cols = load_columns(vec, par, 0)
-    need("xt")
-    x = xt[...].astype(F32)
 
     def after_mlp():
         need("hidden")
         mlp_grads(g, flat, small)
 
-    dx_channels[...] = backward(x, par, need, cols, res, g, after_mlp).astype(BF16)
+    dx_channels[...] = backward(xt, par, need, cols, res, g, after_mlp).astype(BF16)
     attention_grads(g, flat, small)
     even = lax.axis_index("cols") % 2 == 0
     for at in range(0, FLAT, 256):
@@ -550,12 +545,12 @@
 
 
 def unpack_rest(mine, other, *refs):
-    ng, nb, qw_far, qb, rel, pw_far, pb, mg, mb, uw_far, ub, dw_far, db = refs[4:17]
-    copies = Copies(refs[21])
+    far = dict(zip(PAR_NAMES, refs[4:17]))
+    near_refs = dict(zip(PAR_NAMES, refs[17:30]))
+    copies = Copies(refs[30])
     factor = outs_factor
     parity = lax.axis_index("cols") % 2
-    far_refs = (qw_far, pw_far, uw_far, dw_far)
-    unpack_weights(lambda at, n: other[at : at + n, :].astype(F32) * factor, 1 - parity, refs[17:21], far_refs, copies)
+    unpack_weights(lambda at, n: other[at : at + n, :].astype(F32) * factor, 1 - parity, [near_refs[n] for n in WEIGHTS], [far[n] for n in WEIGHTS], copies)
     flip = (iota((256, 256), 0) + iota((256, 256), 1) == 255).astype(BF16)
     for b in range(2):
 
@@ -563,7 +558,8 @@
             return jnp.where(parity == b, mine[at : at + n, :], other[at : at + n, :])
 
         small = raw(SMALL, 48).astype(F32) * factor
-        for at, ref in ((0, ng), (2, nb), (4, qb), (9, pb), (11, mg), (13, mb), (15, ub), (21, db)):
+        for at, name in ((0, "ng"), (2, "nb"), (4, "qb"), (9, "pb"), (11, "mg"), (13, "mb"), (15, "ub"), (21, "db")):
+            ref = near_refs[name]
             n = ref.shape[-1]
             for i in range(0, n, 128):
                 w = min(128, n - i)
@@ -571,7 +567,9 @@
         table = jnp.concatenate([raw(SMALL + 24, 8), raw(SMALL + 32, 8)], axis=1)
         table = dot_nn(table, flip) * factor
         for h in range(HEADS):
-            rel[h, b : b + 1, :] = table[h : h + 1, 0 : SPAN * SPAN]
+            near_refs["rel"][h, b : b + 1, :] = table[h : h + 1, 0 : SPAN * SPAN]
+    for name in VEC_NAMES + ("rel",):
+        copies.start(name, near_refs[name], far[name])
     copies.rest()
 
 
@@ -661,7 +659,8 @@
         [grid, edge, vec] + tables + [sems] + list(par_vmem.values()) + res_vmem + [held, held, pltpu.VMEM((C, TOK), BF16)],
         5 * 10**9,
     )
-    own, got, xt, res = one[0], exchange(one[1:4], -1), one[4], one[5:]
+    own, xt, res = one[0], one[4], one[5:]
+    got = exchange(one[1:4], -1)
     channels = pltpu.VMEM((C, TOK), BF16)
     grad_vmem = [pltpu.VMEM(s, F32 if n == "rel" else BF16) for n, s in zip(GRAD_NAMES, GRAD_SHAPES)]
     small = pltpu.VMEM((48, 128), F32)
@@ -671,7 +670,12 @@
         (cotangent, *params),
         [held, held] + strips + grad_vmem + [res_vmem[4], res_vmem[2]],
         [],
-        [grid, edge, vec] + tables + [sems] + list(par_vmem.values()) + [res_vmem[i] for i in (0, 1, 3, 5)] + [held],
+        [grid, edge, vec]
+        + tables
+        + [sems]
+        + list(par_vmem.values())
+        + [res_vmem[i] for i in (0, 1, 3, 5)]
+        + [held, pltpu.VMEM((C, TOK), BF16)],
         10**10,
     )
     got = exchange(two[2:5], 1)
@@ -703,9 +707,9 @@
     grads = pl.pallas_call(
         unpack_rest,
         in_specs=[VMEM, VMEM] + [FAR] * 4,
-        out_specs=[FAR if n in WEIGHTS else VMEM for n in PAR_NAMES],
-        out_shape=[pltpu.HBM(p.shape, F32) if n in WEIGHTS else shaped(p.shape, F32) for n, p in zip(PAR_NAMES, params)],
-        scratch_shapes=weights + [few_sems],
+        out_specs=[FAR] * len(PAR_NAMES),
+        out_shape=[pltpu.HBM(p.shape, F32) for p in params],
+        scratch_shapes=[pltpu.VMEM(PAR_SHAPES[n], F32) for n in PAR_NAMES] + [pltpu.SemaphoreType.DMA((16,))],
         input_output_aliases={2: 2, 3: 5, 4: 9, 5: 11},
         name="unpack_rest",
         compiler_params=pltpu.CompilerParams(vmem_limit_bytes=30 * 2**20),

time: 96.9 us -> 95.5 us (0.986)
  Pallas kernels: 26.6 us -> 25.2 us
where the time goes in v4:
time: 95.5 us; the launch traced here: 95.2 us
  blocking collectives  42.5 us (45%)
  Pallas kernels  25.2 us (26%)
  starting transfers between devices  19 us (20%)
  waiting for transfers between devices  7.59 us (8%)
    all_to_all x2, blocking collectives, send_parts(): lax.all_to_all(parts, ('rows', 'cols'), 0, 0, axis_index_groups=groups, t...  42.5 us
    pallas_call x8, Pallas kernels, call(): pl.pallas_call(kernel, in_specs=[VMEM] * len(args) + [FAR] * len(far_args...  23.7 us
    ppermute x2, starting transfers between devices, swap(): lax.ppermute(value, 'cols', [(c, c ^ 1) for c in range(lax.axis_size('col...  6.69 us
    ppermute x2, starting transfers between devices, exchange(): lax.ppermute(corner, ('rows', 'cols'), both)  5.24 us
    ppermute x2, waiting for transfers between devices, exchange(): lax.ppermute(corner, ('rows', 'cols'), both)  5.06 us
    ppermute x2, starting transfers between devices, exchange(): lax.ppermute(row_strip, 'rows', down)  4.95 us
    ppermute x2, starting transfers between devices, exchange(): lax.ppermute(col_strip, 'cols', along)  2.11 us
    ppermute x2, waiting for transfers between devices, swap(): lax.ppermute(value, 'cols', [(c, c ^ 1) for c in range(lax.axis_size('col...  2.1 us
  transfers between devices with their start and end apart: 8, of which 4 were waited for; matrix products, arithmetic and copies ran while one was open for 0% of the time, Pallas kernels for 3%

profile of v4, /device:TPU:1, one launch (start us, length us, event | category | flops | bytes accessed | tf_op | source)
XLA Modules:
  0.0 95.2 jit_solution(14426373909099570617)
XLA Ops:
  0.6 5.6 %shard_map.262 = (bf16[16,16,192]{2,1,0:T(8,128)(2,1)S(1)}, bf16[128,192]{1,0:T(8,128)(2,1)S(1)}, bf16[128,192]{1,0:T(8,128)(2,1)S(1)}, bf16[32,192]{1,0:T(8,128...) custom-call(bf16[16,16,192]{2,1,0:T(8,128)(2,1)} %refs_0_.1, ...), custom_call_target="tpu_custom_call" | custom-call | flops 5000000000 | bytes 4000000 | tf_op jit(solution)/shard_map/pallas_call | solution.py:590
  6.2 1.5 %collective-permute-start = (bf16[128,192]{1,0:T(8,128)(2,1)S(1)}, bf16[128,192]{1,0:T(8,128)(2,1)S(1)}, u32[]{:S(2)}, u32[]{:S(2)}) collective-permute-start(bf16[128,192]{1,0:T(8,128)(2,1)S(1)} %get-tuple-element.67), channel_id=1, source_target_pairs={{0,15},{1,0},{2,1},{3,2},{4,3},{5,4},{6,5},{7,6},{8,7},{9,8},{10,9... | collective-permute-start | bytes 147464 | tf_op jit(solution)/shard_map/ppermute | solution.py:617
  7.7 4.9 %collective-permute-start.1 = (bf16[128,192]{1,0:T(8,128)(2,1)S(1)}, bf16[128,192]{1,0:T(8,128)(2,1)S(1)}, u32[]{:S(2)}, u32[]{:S(2)}) collective-permute-start(bf16[128,192]{1,0:T(8,128)(2,1)S(1)} %get-tuple-element.68), channel_id=1, source_target_pairs={{0,112},{16,0},{32,16},{48,32},{64,48},{80,64},{96,80},{112,96},{1... | collective-permute-start | bytes 147464 | tf_op jit(solution)/shard_map/ppermute | solution.py:618
  12.6 5.2 %collective-permute-start.2 = (bf16[32,192]{1,0:T(8,128)(2,1)S(1)}, bf16[32,192]{1,0:T(8,128)(2,1)S(1)}, u32[]{:S(2)}, u32[]{:S(2)}) collective-permute-start(bf16[32,192]{1,0:T(8,128)(2,1)S(1)} %get-tuple-element.69), channel_id=1, source_target_pairs={{0,127},{1,112},{2,113},{3,114},{4,115},{5,116},{6,117},{7,118},{8... | collective-permute-start | bytes 36872 | tf_op jit(solution)/shard_map/ppermute | solution.py:619
  17.7 0.9 collective-permute-done.2.refs_3_
  18.6 0.0 collective-permute-done.refs_1_
  18.6 8.1 %shard_map.263 = (bf16[16,16,192]{2,1,0:T(8,128)(2,1)S(1)}, bf16[16,16,192]{2,1,0:T(8,128)(2,1)S(1)}, bf16[128,192]{1,0:T(8,128)(2,1)S(1)}, bf16[128,192]{1,0:T(...) custom-call(bf16[16,16,192]{2,1,0:T(8,128)(2,1)S(1)} %get-tuple-elem, ...), custom_call_target="tpu_custom_call" | custom-call | flops 10000000000 | bytes 4000000 | tf_op jit(solution)/shard_map/pallas_call | solution.py:590
  26.7 0.1 collective-permute-start.5
  26.8 0.7 collective-permute-start.3
  27.5 0.1 collective-permute-start.4
  27.5 1.1 %shard_map.264.refs_4_ = bf16[3584,128]{1,0:T(8,128)(2,1)S(1)} custom-call(bf16[192,256]{1,0:T(8,128)(2,1)S(1)} %get-tuple-element.75.refs_0_, bf16[192,256]{1,0:T(8,128)(2,1)S(1)} %get-tuple-element.76.refs_1_, bf16[192,256]{1,0:T(8,128)(2,1)S(1)} %get-tuple-element.77.refs_2_, bf16[192,256]{1,0:T(8,128)(2,1)S(1)} %get-tuple-element.78.refs_3_, ...), custom_call_target="tpu_custom_call" | custom-call | flops 1000000000 | bytes 4000000 | tf_op jit(solution)/shard_map/pallas_call | solution.py:590
  28.6 4.2 %collective-permute-done.5.refs_3_.corner_in = bf16[32,192]{1,0:T(8,128)(2,1)S(1)} collective-permute-done((bf16[32,192]{1,0:T(8,128)(2,1)S(1)}, bf16[32,192]{1,0:T(8,128)(2,1)S(1)}, u32[]{:S(2)}, u32[]{:S(2)}) %collective-permute-start.5) | collective-permute-done | bytes 12320 | tf_op jit(solution)/shard_map/ppermute | solution.py:619
  32.8 0.4 collective-permute-done.4.refs_2_.row_in
  33.2 6.5 %shard_map.265 = (bf16[192,256]{1,0:T(8,128)(2,1)S(1)}, bf16[3584,128]{1,0:T(8,128)(2,1)S(1)}, bf16[3584,128]{1,0:T(8,128)(2,1)S(1)}) custom-call(bf16[16,16,192]{2,1,0:T(8,128)(2,1)S(1)} %get-tuple-element.74.refs_0_, bf16[128,192]{1,0:T(8,128)(2,1)S(1)} %collective-permute-done.3.refs_1_.col_in, ...), custom_call_target="tpu_custom_call" | custom-call | flops 5000000000 | bytes 4000000 | tf_op jit(solution)/shard_map/pallas_call | solution.py:590
  39.7 3.6 %collective-permute-start.6 = (bf16[3584,128]{1,0:T(8,128)(2,1)S(1)}, bf16[3584,128]{1,0:T(8,128)(2,1)S(1)}, u32[]{:S(2)}, u32[]{:S(2)}) collective-permute-start(bf16[3584,128]{1,0:T(8,128)(2,1)S(1)} %get-tuple-element.99), channel_id=1, source_target_pairs={{0,1},{1,0},{2,3},{3,2},{4,5},{5,4},{6,7},{7,6},{8,9},{9,8},{10,11... | collective-permute-start | bytes 2752520 | tf_op jit(solution)/shard_map/ppermute | solution.py:624
  43.3 2.1 %collective-permute-done.6.got = bf16[3584,128]{1,0:T(8,128)(2,1)S(1)} collective-permute-done((bf16[3584,128]{1,0:T(8,128)(2,1)S(1)}, bf16[3584,128]{1,0:T(8,128)(2,1)S(1)}, u32[]{:S(2)}, u32[]{:S(2)}) %collective-permute-start.6) | collective-permute-done | bytes 917536 | tf_op jit(solution)/shard_map/ppermute | solution.py:624
  45.4 0.2 shard_map.267
  45.6 22.6 %all_to_all.10 = bf16[64,56,128]{2,1,0:T(8,128)(2,1)S(1)} all-to-all(bf16[64,56,128]{2,1,0:T(8,128)(2,1)S(1)} %bitcast.13), channel_id=1, replica_groups={{0,2,4,6,8,10,12,14,16,18,20,22,24,26,28,30,32,34,36,38,40,42,44,46,48,..., dimensions={0} | all-to-all | bytes 1835008 | tf_op jit(solution)/shard_map/all_to_all | solution.py:632
  68.3 0.2 shard_map.268
  68.5 19.9 %all_to_all.11 = bf16[64,56,128]{2,1,0:T(8,128)(2,1)S(1)} all-to-all(bf16[64,56,128]{2,1,0:T(8,128)(2,1)S(1)} %bitcast.9), channel_id=1, replica_groups={{0,2,4,6,8,10,12,14,16,18,20,22,24,26,28,30,32,34,36,38,40,42,44,46,48,..., dimensions={0} | all-to-all | bytes 1835008 | tf_op jit(solution)/shard_map/all_to_all | solution.py:632
  88.3 3.1 %collective-permute-start.7 = (bf16[3584,128]{1,0:T(8,128)(2,1)S(1)}, bf16[3584,128]{1,0:T(8,128)(2,1)S(1)}, u32[]{:S(2)}, u32[]{:S(2)}) collective-permute-start(bf16[3584,128]{1,0:T(8,128)(2,1)S(1)} %bitcast.10), channel_id=1, source_target_pairs={{0,1},{1,0},{2,3},{3,2},{4,5},{5,4},{6,7},{7,6},{8,9},{9,8},{10,11... | collective-permute-start | bytes 2752520 | tf_op jit(solution)/shard_map/ppermute | solution.py:624
  91.4 0.8 shard_map.266
  92.2 1.3 %shard_map.269 = (f32[2,192,576]{2,1,0:T(8,128)}, f32[2,192,192]{2,1,0:T(8,128)}, f32[2,192,768]{2,1,0:T(8,128)}, f32[2,192,768]{2,1,0:T(8,128)}) custom-call(bf16[3584,128]{1,0:T(8,128)(2,1)S(1)} %bitcast.11), custom_call_target="tpu_custom_call" | custom-call | flops 1000000000 | bytes 4000000 | tf_op jit(solution)/shard_map/pallas_call | solution.py:590
  93.5 1.5 %unpack_rest.1 = (f32[2,192]{1,0:T(2,128)}, f32[2,192]{1,0:T(2,128)}, f32[2,192,576]{2,1,0:T(8,128)}, f32[2,576]{1,0:T(2,128)}, f32[6,2,225]{2,1,0:T(2,128)}, /*...) custom-call(bf16[3584,128]{1,0:T(8,128)(2,1)S(1)} %bitcast.12, ...), custom_call_target="tpu_custom_call", output_to_operand_aliasing={{2}: (2, {}), {5}: (3, {}), {9}: (4, {}), {11}: (5, {})} | custom-call | tf_op jit(solution)/shard_map/unpack_rest/pallas_call | solution.py:707
  (3 shorter events, 0.0 us)
Async XLA Ops:
  6.2 12.4 %collective-permute-start = (bf16[128,192]{1,0:T(8,128)(2,1)S(1)}, bf16[128,192]{1,0:T(8,128)(2,1)S(1)}, u32[]{:S(2)}, u32[]{:S(2)}) collective-permute-start(bf16[128,192]{1,0:T(8,128)(2,1)S(1)} %get-tuple-element.67), channel_id=1, source_target_pairs={{0,15},{1,0},{2,1},{3,2},{4,3},{5,4},{6,5},{7,6},{8,7},{9,8},{10,9... | collective-permute-start | bytes 147464 | tf_op jit(solution)/shard_map/ppermute | solution.py:617
  7.7 10.9 %collective-permute-start.1 = (bf16[128,192]{1,0:T(8,128)(2,1)S(1)}, bf16[128,192]{1,0:T(8,128)(2,1)S(1)}, u32[]{:S(2)}, u32[]{:S(2)}) collective-permute-start(bf16[128,192]{1,0:T(8,128)(2,1)S(1)} %get-tuple-element.68), channel_id=1, source_target_pairs={{0,112},{16,0},{32,16},{48,32},{64,48},{80,64},{96,80},{112,96},{1... | collective-permute-start | bytes 147464 | tf_op jit(solution)/shard_map/ppermute | solution.py:618
  12.6 6.0 %collective-permute-start.2 = (bf16[32,192]{1,0:T(8,128)(2,1)S(1)}, bf16[32,192]{1,0:T(8,128)(2,1)S(1)}, u32[]{:S(2)}, u32[]{:S(2)}) collective-permute-start(bf16[32,192]{1,0:T(8,128)(2,1)S(1)} %get-tuple-element.69), channel_id=1, source_target_pairs={{0,127},{1,112},{2,113},{3,114},{4,115},{5,116},{6,117},{7,118},{8... | collective-permute-start | bytes 36872 | tf_op jit(solution)/shard_map/ppermute | solution.py:619
  26.7 6.1 %collective-permute-start.5 = (bf16[32,192]{1,0:T(8,128)(2,1)S(1)}, bf16[32,192]{1,0:T(8,128)(2,1)S(1)}, u32[]{:S(2)}, u32[]{:S(2)}) collective-permute-start(bf16[32,192]{1,0:T(8,128)(2,1)S(1)} %get-tuple-element.73), channel_id=1, source_target_pairs={{0,17},{1,18},{2,19},{3,20},{4,21},{5,22},{6,23},{7,24},{8,25},{9,... | collective-permute-start | bytes 36872 | tf_op jit(solution)/shard_map/ppermute | solution.py:619
  26.8 6.0 %collective-permute-start.3 = (bf16[128,192]{1,0:T(8,128)(2,1)S(1)}, bf16[128,192]{1,0:T(8,128)(2,1)S(1)}, u32[]{:S(2)}, u32[]{:S(2)}) collective-permute-start(bf16[128,192]{1,0:T(8,128)(2,1)S(1)} %get-tuple-element.71), channel_id=1, source_target_pairs={{0,1},{1,2},{2,3},{3,4},{4,5},{5,6},{6,7},{7,8},{8,9},{9,10},{10,1... | collective-permute-start | bytes 147464 | tf_op jit(solution)/shard_map/ppermute | solution.py:617
  27.5 5.8 %collective-permute-start.4 = (bf16[128,192]{1,0:T(8,128)(2,1)S(1)}, bf16[128,192]{1,0:T(8,128)(2,1)S(1)}, u32[]{:S(2)}, u32[]{:S(2)}) collective-permute-start(bf16[128,192]{1,0:T(8,128)(2,1)S(1)} %get-tuple-element.72), channel_id=1, source_target_pairs={{0,16},{16,32},{32,48},{48,64},{64,80},{80,96},{96,112},{112,0},{1... | collective-permute-start | bytes 147464 | tf_op jit(solution)/shard_map/ppermute | solution.py:618
  39.7 5.7 %collective-permute-start.6 = (bf16[3584,128]{1,0:T(8,128)(2,1)S(1)}, bf16[3584,128]{1,0:T(8,128)(2,1)S(1)}, u32[]{:S(2)}, u32[]{:S(2)}) collective-permute-start(bf16[3584,128]{1,0:T(8,128)(2,1)S(1)} %get-tuple-element.99), channel_id=1, source_target_pairs={{0,1},{1,0},{2,3},{3,2},{4,5},{5,4},{6,7},{7,6},{8,9},{9,8},{10,11... | collective-permute-start | bytes 2752520 | tf_op jit(solution)/shard_map/ppermute | solution.py:624
  88.3 5.2 %collective-permute-start.7 = (bf16[3584,128]{1,0:T(8,128)(2,1)S(1)}, bf16[3584,128]{1,0:T(8,128)(2,1)S(1)}, u32[]{:S(2)}, u32[]{:S(2)}) collective-permute-start(bf16[3584,128]{1,0:T(8,128)(2,1)S(1)} %bitcast.10), channel_id=1, source_target_pairs={{0,1},{1,0},{2,3},{3,2},{4,5},{5,4},{6,7},{7,6},{8,9},{9,8},{10,11... | collective-permute-start | bytes 2752520 | tf_op jit(solution)/shard_map/ppermute | solution.py:624

commit v5 on v4

--- a/solution.py
+++ b/solution.py
@@ -118,25 +118,31 @@
     return keep
 
 
-def forward(x, par, need, cols, bias, res, zones, keep):
+UNITS = [(p, h, slice(128 * p, 128 * p + 128)) for p in range(2) for h in range(HEADS)]
+
+
+def forward(x, par, need, cols, bias, res, stage, zones, keep):
     left = halves()
     xhat, _ = norm_fwd(x)
     normed = (xhat * cols[0:C, 0:1] + cols[0:C, 1:2]).astype(BF16)
     need("qw")
     res["packed"][...] = (dot_tn(par["qw"][...], normed) + cols[0:576, 6:7]).astype(BF16)
-    for p in range(2):
-        lanes = slice(128 * p, 128 * p + 128)
-        for h in range(HEADS):
-            q = res["packed"][DIM * h : DIM * h + DIM, lanes]
-            k = res["packed"][C + DIM * h : C + DIM * h + DIM, lanes]
-            v = res["packed"][2 * C + DIM * h : 2 * C + DIM * h + DIM, lanes]
-            s = own_window(dot_tn(k, q), left) * SCALE + bias[h]
-            if zones is not None:
-                s = jnp.where(zones[p], s, MASKED)
-            e = jnp.exp(s - jnp.max(s, axis=0, keepdims=True))
-            a = e * (1.0 / jnp.sum(e, axis=0, keepdims=True))
-            res["attn"][p * HEADS + h] = a.astype(BF16)
-            res["mixed"][DIM * h : DIM * h + DIM, lanes] = dot_nn(v, stack_windows(a, left)).astype(BF16)
+    for p, h, lanes in UNITS:
+        q = res["packed"][DIM * h : DIM * h + DIM, lanes]
+        k = res["packed"][C + DIM * h : C + DIM * h + DIM, lanes]
+        s = own_window(dot_tn(k, q), left) * SCALE + bias[h]
+        if zones is not None:
+            s = jnp.where(zones[p], s, MASKED)
+        stage[p * HEADS + h] = s
+    for p, h, _ in UNITS:
+        s = stage[p * HEADS + h]
+        e = jnp.exp(s - jnp.max(s, axis=0, keepdims=True))
+        a = e * (1.0 / jnp.sum(e, axis=0, keepdims=True))
+        res["attn"][p * HEADS + h] = a.astype(BF16)
+    for p, h, lanes in UNITS:
+        v = res["packed"][2 * C + DIM * h : 2 * C + DIM * h + DIM, lanes]
+        wide = stack_windows(res["attn"][p * HEADS + h].astype(F32), left)
+        res["mixed"][DIM * h : DIM * h + DIM, lanes] = dot_nn(v, wide).astype(BF16)
     keep("packed")
     need("pw")
     middle = x + dot_tn(par["pw"][...], res["mixed"][...]) + cols[0:C, 2:3]
@@ -211,7 +217,7 @@
     flat[SMALL + 48 : FLAT, :] = jnp.zeros((FLAT - SMALL - 48, 128), BF16)
 
 
-def backward(x, par, need, cols, res, g, after_mlp):
+def backward(x, par, need, cols, res, stage, g, after_mlp):
     left = halves()
     dout = g["dout"][...]
     need("dw", "slope")
@@ -231,24 +237,27 @@
     need("pw", "mixed")
     dmixed = dot_nn(par["pw"][...], dmid).astype(BF16)
     need("packed", "attn")
+    for p, h, lanes in UNITS:
+        v = res["packed"][2 * C + DIM * h : 2 * C + DIM * h + DIM, lanes]
+        dm = dmixed[DIM * h : DIM * h + DIM, lanes]
+        stage[p * HEADS + h] = own_window(dot_tn(v, dm), left).astype(BF16).astype(F32)
+        dv = dot_nt(dm, stack_windows(res["attn"][p * HEADS + h].astype(F32), left)).astype(BF16)
+        g["dpacked"][2 * C + DIM * h : 2 * C + DIM * h + DIM, lanes] = dv
     for h in range(HEADS):
         drel = None
         for p in range(2):
-            lanes = slice(128 * p, 128 * p + 128)
-            q = res["packed"][DIM * h : DIM * h + DIM, lanes]
-            k = res["packed"][C + DIM * h : C + DIM * h + DIM, lanes]
-            v = res["packed"][2 * C + DIM * h : 2 * C + DIM * h + DIM, lanes]
             a = res["attn"][p * HEADS + h].astype(F32)
-            dm = dmixed[DIM * h : DIM * h + DIM, lanes]
-            da = own_window(dot_tn(v, dm), left).astype(BF16).astype(F32)
+            da = stage[p * HEADS + h]
             ds = a * (da - jnp.sum(da * a, axis=0, keepdims=True))
             drel = ds if drel is None else drel + ds
-            wide = stack_windows(ds * SCALE, left)
-            g["dpacked"][DIM * h : DIM * h + DIM, lanes] = dot_nn(k, wide).astype(BF16)
-            g["dpacked"][C + DIM * h : C + DIM * h + DIM, lanes] = dot_nt(q, wide).astype(BF16)
-            dv = dot_nt(dm, stack_windows(a, left)).astype(BF16)
-            g["dpacked"][2 * C + DIM * h : 2 * C + DIM * h + DIM, lanes] = dv
+            stage[p * HEADS + h] = ds * SCALE
         g["rel"][h] = drel
+    for p, h, lanes in UNITS:
+        q = res["packed"][DIM * h : DIM * h + DIM, lanes]
+        k = res["packed"][C + DIM * h : C + DIM * h + DIM, lanes]
+        wide = stack_windows(stage[p * HEADS + h], left)
+        g["dpacked"][DIM * h : DIM * h + DIM, lanes] = dot_nn(k, wide).astype(BF16)
+        g["dpacked"][C + DIM * h : C + DIM * h + DIM, lanes] = dot_nt(q, wide).astype(BF16)
     need("xt")
     xhat, rstd = norm_fwd(x[...].astype(F32))
     g["n1"][...] = (xhat * cols[0:C, 0:1] + cols[0:C, 1:2]).astype(BF16)
@@ -366,7 +375,7 @@
     grid, edge, vec, table, bias, sems = refs[26:32]
     par = dict(zip(PAR_NAMES, refs[32:45]))
     res = dict(zip(RES_NAMES, refs[45:51]))
-    imagery, cotangent, xt = refs[51:]
+    imagery, cotangent, xt, stage = refs[51:]
     need = Copies(sems)
     need.start("imagery", imagery_far, imagery)
     start_params(need, VEC_NAMES, far, par, 0)
@@ -390,7 +399,7 @@
         grid[r, 0:TILE, 0:C] = cotangent[r].astype(F32)
     emit_strips(grid, edge, strips, 1, 0, 0)
     need.start("out xt", xt, xt_far)
-    out = forward(x, par, need, cols, bias, res, None, keep)
+    out = forward(x, par, need, cols, bias, res, stage, None, keep)
     grid_put(grid, to_tokens(out.astype(F32)))
     for r in range(TILE):
         own[r] = grid[r, 0:TILE, 0:C].astype(BF16)
@@ -409,7 +418,7 @@
     grid, edge, vec, table, bias, sems = refs[36:42]
     par = dict(zip(PAR_NAMES, refs[42:55]))
     res = dict(zip(("packed", "attn", "middle", "slope"), refs[55:59]), hidden=g["hidden"], mixed=g["mixed"])
-    cotangent, xt = refs[59:]
+    cotangent, xt, stage = refs[59:]
     need = Copies(sems)
     start_params(need, VEC_NAMES + ("rel",), far, par, 1)
     need.start("cotangent", cotangent_far, cotangent)
@@ -425,12 +434,12 @@
     position_bias(par, 1, table, bias)
     fill_grid(grid, edge, cotangent, strips_in, 1, 0, 0, 16, 16)
     g["dout"][...] = to_channels(grid_get(grid, 4, 4)).astype(BF16)
-    out = forward(x, par, need, cols, bias, res, zones, nothing)
+    out = forward(x, par, need, cols, bias, res, stage, zones, nothing)
     grid_put(grid, to_tokens(out.astype(F32)))
     for r in range(TILE):
         out_own[r] = grid[r, 0:TILE, 0:C].astype(BF16)
     emit_strips(grid, edge, strips, 0, 12, 12)
-    dx = backward(xt, par, need, cols, res, g, nothing)
+    dx = backward(xt, par, need, cols, res, stage, g, nothing)
     grid_put(grid, to_tokens(dx))
     for r in range(TILE):
         back_own[r] = grid[r, 0:TILE, 0:C].astype(BF16)
@@ -460,7 +469,7 @@
     par = dict(zip(BACK_NAMES, refs[31:43]))
     g = dict(zip(GRAD_NAMES, refs[43:54]))
     res = dict(zip(RES_NAMES, refs[54:60]))
-    xt, flat, small = refs[60:]
+    xt, flat, small, stage = refs[60:]
     g["hidden"] = res["hidden"]
     g["mixed"] = res["mixed"]
     need = Copies(sems)
@@ -485,7 +494,7 @@
         need("hidden")
         mlp_grads(g, flat, small)
 
-    dx_channels[...] = backward(xt, par, need, cols, res, g, after_mlp).astype(BF16)
+    dx_channels[...] = backward(xt, par, need, cols, res, stage, g, after_mlp).astype(BF16)
     attention_grads(g, flat, small)
     even = lax.axis_index("cols") % 2 == 0
     for at in range(0, FLAT, 256):
@@ -650,13 +659,14 @@
     par_vmem = {n: pltpu.VMEM(PAR_SHAPES[n], par_kinds[n]) for n in PAR_NAMES}
     res_vmem = [pltpu.VMEM(s, BF16) for s in RES_SHAPES]
     sems = pltpu.SemaphoreType.DMA((32,))
+    stage = pltpu.VMEM((2 * HEADS, 64, 128), F32)
     one = call(
         first_forward,
         (),
         (imagery, cotangent, *params),
         [held] + strips,
         [shaped((C, TOK))] + [shaped(s) for s in RES_SHAPES],
-        [grid, edge, vec] + tables + [sems] + list(par_vmem.values()) + res_vmem + [held, held, pltpu.VMEM((C, TOK), BF16)],
+        [grid, edge, vec] + tables + [sems] + list(par_vmem.values()) + res_vmem + [held, held, pltpu.VMEM((C, TOK), BF16), stage],
         5 * 10**9,
     )
     own, xt, res = one[0], one[4], one[5:]
@@ -675,7 +685,7 @@
         + [sems]
         + list(par_vmem.values())
         + [res_vmem[i] for i in (0, 1, 3, 5)]
-        + [held, pltpu.VMEM((C, TOK), BF16)],
+        + [held, pltpu.VMEM((C, TOK), BF16), stage],
         10**10,
     )
     got = exchange(two[2:5], 1)
@@ -690,7 +700,7 @@
         + [par_vmem[n] for n in BACK_NAMES]
         + grad_vmem
         + res_vmem
-        + [channels, packed_grads, small],
+        + [channels, packed_grads, small, stage],
         5 * 10**9,
     )
     sent = swap(sent)

time: 95.5 us -> 90.4 us (0.947)
  Pallas kernels: 25.2 us -> 20 us
    pallas_call x8, Pallas kernels: 23.7 us -> 18.5 us  [call(): pl.pallas_call(kernel, in_specs=[VMEM] * len(args) + [FAR] * len(far_args...]
  transfers between devices with their start and end apart: 8 -> 8, of which waited for: 4 -> 4; matrix products, arithmetic and copies ran while one was open for 0% -> 0% of each run, Pallas kernels for 3% -> 4%
where the time goes in v5:
time: 90.4 us; the launch traced here: 90.2 us
  blocking collectives  42.7 us (47%)
  Pallas kernels  20 us (22%)
  starting transfers between devices  18.9 us (21%)
  waiting for transfers between devices  7.66 us (8%)
    all_to_all x2, blocking collectives, send_parts(): lax.all_to_all(parts, ('rows', 'cols'), 0, 0, axis_index_groups=groups, t...  42.7 us
    pallas_call x8, Pallas kernels, call(): pl.pallas_call(kernel, in_specs=[VMEM] * len(args) + [FAR] * len(far_args...  18.5 us
    ppermute x2, starting transfers between devices, swap(): lax.ppermute(value, 'cols', [(c, c ^ 1) for c in range(lax.axis_size('col...  6.7 us
    ppermute x2, starting transfers between devices, exchange(): lax.ppermute(corner, ('rows', 'cols'), both)  5.24 us
    ppermute x2, waiting for transfers between devices, exchange(): lax.ppermute(corner, ('rows', 'cols'), both)  5.12 us
    ppermute x2, starting transfers between devices, exchange(): lax.ppermute(row_strip, 'rows', down)  4.88 us
    ppermute x2, starting transfers between devices, exchange(): lax.ppermute(col_strip, 'cols', along)  2.11 us
    ppermute x2, waiting for transfers between devices, swap(): lax.ppermute(value, 'cols', [(c, c ^ 1) for c in range(lax.axis_size('col...  2.1 us
  transfers between devices with their start and end apart: 8, of which 4 were waited for; matrix products, arithmetic and copies ran while one was open for 0% of the time, Pallas kernels for 4%

profile of v5, /device:TPU:1, one launch (start us, length us, event | category | flops | bytes accessed | tf_op | source)
XLA Modules:
  0.0 90.2 jit_solution(9519506597859324390)
XLA Ops:
  0.6 4.5 %shard_map.262 = (bf16[16,16,192]{2,1,0:T(8,128)(2,1)S(1)}, bf16[128,192]{1,0:T(8,128)(2,1)S(1)}, bf16[128,192]{1,0:T(8,128)(2,1)S(1)}, bf16[32,192]{1,0:T(8,128...) custom-call(bf16[16,16,192]{2,1,0:T(8,128)(2,1)} %refs_0_.1, ...), custom_call_target="tpu_custom_call" | custom-call | flops 5000000000 | bytes 4000000 | tf_op jit(solution)/shard_map/pallas_call | solution.py:599
  5.1 1.4 %collective-permute-start = (bf16[128,192]{1,0:T(8,128)(2,1)S(1)}, bf16[128,192]{1,0:T(8,128)(2,1)S(1)}, u32[]{:S(2)}, u32[]{:S(2)}) collective-permute-start(bf16[128,192]{1,0:T(8,128)(2,1)S(1)} %get-tuple-element.67), channel_id=1, source_target_pairs={{0,15},{1,0},{2,1},{3,2},{4,3},{5,4},{6,5},{7,6},{8,7},{9,8},{10,9... | collective-permute-start | bytes 147464 | tf_op jit(solution)/shard_map/ppermute | solution.py:626
  6.6 4.9 %collective-permute-start.1 = (bf16[128,192]{1,0:T(8,128)(2,1)S(1)}, bf16[128,192]{1,0:T(8,128)(2,1)S(1)}, u32[]{:S(2)}, u32[]{:S(2)}) collective-permute-start(bf16[128,192]{1,0:T(8,128)(2,1)S(1)} %get-tuple-element.68), channel_id=1, source_target_pairs={{0,112},{16,0},{32,16},{48,32},{64,48},{80,64},{96,80},{112,96},{1... | collective-permute-start | bytes 147464 | tf_op jit(solution)/shard_map/ppermute | solution.py:627
  11.5 5.2 %collective-permute-start.2 = (bf16[32,192]{1,0:T(8,128)(2,1)S(1)}, bf16[32,192]{1,0:T(8,128)(2,1)S(1)}, u32[]{:S(2)}, u32[]{:S(2)}) collective-permute-start(bf16[32,192]{1,0:T(8,128)(2,1)S(1)} %get-tuple-element.69), channel_id=1, source_target_pairs={{0,127},{1,112},{2,113},{3,114},{4,115},{5,116},{6,117},{7,118},{8... | collective-permute-start | bytes 36872 | tf_op jit(solution)/shard_map/ppermute | solution.py:628
  16.6 0.9 collective-permute-done.2.refs_3_
  17.5 0.0 collective-permute-done.refs_1_
  17.5 0.0 collective-permute-done.1.refs_2_
  17.5 5.5 %shard_map.263 = (bf16[16,16,192]{2,1,0:T(8,128)(2,1)S(1)}, bf16[16,16,192]{2,1,0:T(8,128)(2,1)S(1)}, bf16[128,192]{1,0:T(8,128)(2,1)S(1)}, bf16[128,192]{1,0:T(...) custom-call(bf16[16,16,192]{2,1,0:T(8,128)(2,1)S(1)} %get-tuple-elem, ...), custom_call_target="tpu_custom_call" | custom-call | flops 10000000000 | bytes 4000000 | tf_op jit(solution)/shard_map/pallas_call | solution.py:599
  23.0 0.1 collective-permute-start.5
  23.1 0.7 collective-permute-start.3
  23.8 1.1 %shard_map.264.refs_4_ = bf16[3584,128]{1,0:T(8,128)(2,1)S(1)} custom-call(bf16[192,256]{1,0:T(8,128)(2,1)S(1)} %get-tuple-element.75.refs_0_, bf16[192,256]{1,0:T(8,128)(2,1)S(1)} %get-tuple-element.76.refs_1_, bf16[192,256]{1,0:T(8,128)(2,1)S(1)} %get-tuple-element.77.refs_2_, bf16[192,256]{1,0:T(8,128)(2,1)S(1)} %get-tuple-element.78.refs_3_, ...), custom_call_target="tpu_custom_call" | custom-call | flops 1000000000 | bytes 4000000 | tf_op jit(solution)/shard_map/pallas_call | solution.py:599
  24.8 4.3 %collective-permute-done.5.refs_3_.corner_in = bf16[32,192]{1,0:T(8,128)(2,1)S(1)} collective-permute-done((bf16[32,192]{1,0:T(8,128)(2,1)S(1)}, bf16[32,192]{1,0:T(8,128)(2,1)S(1)}, u32[]{:S(2)}, u32[]{:S(2)}) %collective-permute-start.5) | collective-permute-done | bytes 12320 | tf_op jit(solution)/shard_map/ppermute | solution.py:628
  29.1 0.4 collective-permute-done.4.refs_2_.row_in
  29.5 5.0 %shard_map.265 = (bf16[192,256]{1,0:T(8,128)(2,1)S(1)}, bf16[3584,128]{1,0:T(8,128)(2,1)S(1)}, bf16[3584,128]{1,0:T(8,128)(2,1)S(1)}) custom-call(bf16[16,16,192]{2,1,0:T(8,128)(2,1)S(1)} %get-tuple-element.74.refs_0_, bf16[128,192]{1,0:T(8,128)(2,1)S(1)} %collective-permute-done.3.refs_1_.col_in, ...), custom_call_target="tpu_custom_call" | custom-call | flops 5000000000 | bytes 4000000 | tf_op jit(solution)/shard_map/pallas_call | solution.py:599
  34.5 3.6 %collective-permute-start.6 = (bf16[3584,128]{1,0:T(8,128)(2,1)S(1)}, bf16[3584,128]{1,0:T(8,128)(2,1)S(1)}, u32[]{:S(2)}, u32[]{:S(2)}) collective-permute-start(bf16[3584,128]{1,0:T(8,128)(2,1)S(1)} %get-tuple-element.99), channel_id=1, source_target_pairs={{0,1},{1,0},{2,3},{3,2},{4,5},{5,4},{6,7},{7,6},{8,9},{9,8},{10,11... | collective-permute-start | bytes 2752520 | tf_op jit(solution)/shard_map/ppermute | solution.py:633
  38.1 2.1 %collective-permute-done.6.got = bf16[3584,128]{1,0:T(8,128)(2,1)S(1)} collective-permute-done((bf16[3584,128]{1,0:T(8,128)(2,1)S(1)}, bf16[3584,128]{1,0:T(8,128)(2,1)S(1)}, u32[]{:S(2)}, u32[]{:S(2)}) %collective-permute-start.6) | collective-permute-done | bytes 917536 | tf_op jit(solution)/shard_map/ppermute | solution.py:633
  40.2 0.2 shard_map.267
  40.4 22.8 %all_to_all.10 = bf16[64,56,128]{2,1,0:T(8,128)(2,1)S(1)} all-to-all(bf16[64,56,128]{2,1,0:T(8,128)(2,1)S(1)} %bitcast.13), channel_id=1, replica_groups={{0,2,4,6,8,10,12,14,16,18,20,22,24,26,28,30,32,34,36,38,40,42,44,46,48,..., dimensions={0} | all-to-all | bytes 1835008 | tf_op jit(solution)/shard_map/all_to_all | solution.py:641
  63.2 0.2 shard_map.268
  63.4 19.9 %all_to_all.11 = bf16[64,56,128]{2,1,0:T(8,128)(2,1)S(1)} all-to-all(bf16[64,56,128]{2,1,0:T(8,128)(2,1)S(1)} %bitcast.9), channel_id=1, replica_groups={{0,2,4,6,8,10,12,14,16,18,20,22,24,26,28,30,32,34,36,38,40,42,44,46,48,..., dimensions={0} | all-to-all | bytes 1835008 | tf_op jit(solution)/shard_map/all_to_all | solution.py:641
  83.3 3.1 %collective-permute-start.7 = (bf16[3584,128]{1,0:T(8,128)(2,1)S(1)}, bf16[3584,128]{1,0:T(8,128)(2,1)S(1)}, u32[]{:S(2)}, u32[]{:S(2)}) collective-permute-start(bf16[3584,128]{1,0:T(8,128)(2,1)S(1)} %bitcast.10), channel_id=1, source_target_pairs={{0,1},{1,0},{2,3},{3,2},{4,5},{5,4},{6,7},{7,6},{8,9},{9,8},{10,11... | collective-permute-start | bytes 2752520 | tf_op jit(solution)/shard_map/ppermute | solution.py:633
  86.4 0.8 shard_map.266
  87.2 1.3 %shard_map.269 = (f32[2,192,576]{2,1,0:T(8,128)}, f32[2,192,192]{2,1,0:T(8,128)}, f32[2,192,768]{2,1,0:T(8,128)}, f32[2,192,768]{2,1,0:T(8,128)}) custom-call(bf16[3584,128]{1,0:T(8,128)(2,1)S(1)} %bitcast.11), custom_call_target="tpu_custom_call" | custom-call | flops 1000000000 | bytes 4000000 | tf_op jit(solution)/shard_map/pallas_call | solution.py:599
  88.5 1.5 %unpack_rest.1 = (f32[2,192]{1,0:T(2,128)}, f32[2,192]{1,0:T(2,128)}, f32[2,192,576]{2,1,0:T(8,128)}, f32[2,576]{1,0:T(2,128)}, f32[6,2,225]{2,1,0:T(2,128)}, /*...) custom-call(bf16[3584,128]{1,0:T(8,128)(2,1)S(1)} %bitcast.12, ...), custom_call_target="tpu_custom_call", output_to_operand_aliasing={{2}: (2, {}), {5}: (3, {}), {9}: (4, {}), {11}: (5, {})} | custom-call | tf_op jit(solution)/shard_map/unpack_rest/pallas_call | solution.py:717
  (3 shorter events, 0.0 us)
Async XLA Ops:
  5.1 12.4 %collective-permute-start = (bf16[128,192]{1,0:T(8,128)(2,1)S(1)}, bf16[128,192]{1,0:T(8,128)(2,1)S(1)}, u32[]{:S(2)}, u32[]{:S(2)}) collective-permute-start(bf16[128,192]{1,0:T(8,128)(2,1)S(1)} %get-tuple-element.67), channel_id=1, source_target_pairs={{0,15},{1,0},{2,1},{3,2},{4,3},{5,4},{6,5},{7,6},{8,7},{9,8},{10,9... | collective-permute-start | bytes 147464 | tf_op jit(solution)/shard_map/ppermute | solution.py:626
  6.6 10.9 %collective-permute-start.1 = (bf16[128,192]{1,0:T(8,128)(2,1)S(1)}, bf16[128,192]{1,0:T(8,128)(2,1)S(1)}, u32[]{:S(2)}, u32[]{:S(2)}) collective-permute-start(bf16[128,192]{1,0:T(8,128)(2,1)S(1)} %get-tuple-element.68), channel_id=1, source_target_pairs={{0,112},{16,0},{32,16},{48,32},{64,48},{80,64},{96,80},{112,96},{1... | collective-permute-start | bytes 147464 | tf_op jit(solution)/shard_map/ppermute | solution.py:627
  11.5 6.0 %collective-permute-start.2 = (bf16[32,192]{1,0:T(8,128)(2,1)S(1)}, bf16[32,192]{1,0:T(8,128)(2,1)S(1)}, u32[]{:S(2)}, u32[]{:S(2)}) collective-permute-start(bf16[32,192]{1,0:T(8,128)(2,1)S(1)} %get-tuple-element.69), channel_id=1, source_target_pairs={{0,127},{1,112},{2,113},{3,114},{4,115},{5,116},{6,117},{7,118},{8... | collective-permute-start | bytes 36872 | tf_op jit(solution)/shard_map/ppermute | solution.py:628
  23.0 6.1 %collective-permute-start.5 = (bf16[32,192]{1,0:T(8,128)(2,1)S(1)}, bf16[32,192]{1,0:T(8,128)(2,1)S(1)}, u32[]{:S(2)}, u32[]{:S(2)}) collective-permute-start(bf16[32,192]{1,0:T(8,128)(2,1)S(1)} %get-tuple-element.73), channel_id=1, source_target_pairs={{0,17},{1,18},{2,19},{3,20},{4,21},{5,22},{6,23},{7,24},{8,25},{9,... | collective-permute-start | bytes 36872 | tf_op jit(solution)/shard_map/ppermute | solution.py:628
  23.1 6.0 %collective-permute-start.3 = (bf16[128,192]{1,0:T(8,128)(2,1)S(1)}, bf16[128,192]{1,0:T(8,128)(2,1)S(1)}, u32[]{:S(2)}, u32[]{:S(2)}) collective-permute-start(bf16[128,192]{1,0:T(8,128)(2,1)S(1)} %get-tuple-element.71), channel_id=1, source_target_pairs={{0,1},{1,2},{2,3},{3,4},{4,5},{5,6},{6,7},{7,8},{8,9},{9,10},{10,1... | collective-permute-start | bytes 147464 | tf_op jit(solution)/shard_map/ppermute | solution.py:626
  23.8 5.8 %collective-permute-start.4 = (bf16[128,192]{1,0:T(8,128)(2,1)S(1)}, bf16[128,192]{1,0:T(8,128)(2,1)S(1)}, u32[]{:S(2)}, u32[]{:S(2)}) collective-permute-start(bf16[128,192]{1,0:T(8,128)(2,1)S(1)} %get-tuple-element.72), channel_id=1, source_target_pairs={{0,16},{16,32},{32,48},{48,64},{64,80},{80,96},{96,112},{112,0},{1... | collective-permute-start | bytes 147464 | tf_op jit(solution)/shard_map/ppermute | solution.py:627
  34.5 5.7 %collective-permute-start.6 = (bf16[3584,128]{1,0:T(8,128)(2,1)S(1)}, bf16[3584,128]{1,0:T(8,128)(2,1)S(1)}, u32[]{:S(2)}, u32[]{:S(2)}) collective-permute-start(bf16[3584,128]{1,0:T(8,128)(2,1)S(1)} %get-tuple-element.99), channel_id=1, source_target_pairs={{0,1},{1,0},{2,3},{3,2},{4,5},{5,4},{6,7},{7,6},{8,9},{9,8},{10,11... | collective-permute-start | bytes 2752520 | tf_op jit(solution)/shard_map/ppermute | solution.py:633
  83.3 5.2 %collective-permute-start.7 = (bf16[3584,128]{1,0:T(8,128)(2,1)S(1)}, bf16[3584,128]{1,0:T(8,128)(2,1)S(1)}, u32[]{:S(2)}, u32[]{:S(2)}) collective-permute-start(bf16[3584,128]{1,0:T(8,128)(2,1)S(1)} %bitcast.10), channel_id=1, source_target_pairs={{0,1},{1,0},{2,3},{3,2},{4,5},{5,4},{6,7},{7,6},{8,9},{9,8},{10,11... | collective-permute-start | bytes 2752520 | tf_op jit(solution)/shard_map/ppermute | solution.py:633

commit v6 on v5

--- a/solution.py
+++ b/solution.py
@@ -24,6 +24,10 @@
 MASKED = -1e30
 
 
+class Box(dict):
+    __getattr__ = dict.__getitem__
+
+
 def dot_tn(a, b):
     return lax.dot_general(a, b, (((0,), (0,)), ((), ())), preferred_element_type=F32)
 
@@ -94,7 +98,7 @@
 def position_bias(par, b, table, bias):
     table[...] = jnp.zeros((8, 256), F32)
     for h in range(HEADS):
-        table[h : h + 1, 0 : SPAN * SPAN] = par["rel"][h, b : b + 1, :]
+        table[h : h + 1, 0 : SPAN * SPAN] = par.rel[h, b : b + 1, :]
     select = (iota((128, 128), 0) == spread(iota((128, 128), 1))).astype(BF16)
     for h in range(HEADS):
         row = jnp.broadcast_to(table[h : h + 1, :], (8, 256))
@@ -126,10 +130,10 @@
     xhat, _ = norm_fwd(x)
     normed = (xhat * cols[0:C, 0:1] + cols[0:C, 1:2]).astype(BF16)
     need("qw")
-    res["packed"][...] = (dot_tn(par["qw"][...], normed) + cols[0:576, 6:7]).astype(BF16)
+    res.packed[...] = (dot_tn(par.qw[...], normed) + cols[0:576, 6:7]).astype(BF16)
     for p, h, lanes in UNITS:
-        q = res["packed"][DIM * h : DIM * h + DIM, lanes]
-        k = res["packed"][C + DIM * h : C + DIM * h + DIM, lanes]
+        q = res.packed[DIM * h : DIM * h + DIM, lanes]
+        k = res.packed[C + DIM * h : C + DIM * h + DIM, lanes]
         s = own_window(dot_tn(k, q), left) * SCALE + bias[h]
         if zones is not None:
             s = jnp.where(zones[p], s, MASKED)
@@ -138,28 +142,28 @@
         s = stage[p * HEADS + h]
         e = jnp.exp(s - jnp.max(s, axis=0, keepdims=True))
         a = e * (1.0 / jnp.sum(e, axis=0, keepdims=True))
-        res["attn"][p * HEADS + h] = a.astype(BF16)
+        res.attn[p * HEADS + h] = a.astype(BF16)
     for p, h, lanes in UNITS:
-        v = res["packed"][2 * C + DIM * h : 2 * C + DIM * h + DIM, lanes]
-        wide = stack_windows(res["attn"][p * HEADS + h].astype(F32), left)
-        res["mixed"][DIM * h : DIM * h + DIM, lanes] = dot_nn(v, wide).astype(BF16)
+        v = res.packed[2 * C + DIM * h : 2 * C + DIM * h + DIM, lanes]
+        wide = stack_windows(res.attn[p * HEADS + h].astype(F32), left)
+        res.mixed[DIM * h : DIM * h + DIM, lanes] = dot_nn(v, wide).astype(BF16)
     keep("packed")
     need("pw")
-    middle = x + dot_tn(par["pw"][...], res["mixed"][...]) + cols[0:C, 2:3]
-    res["middle"][...] = middle.astype(BF16)
-    middle = res["middle"][...].astype(F32)
+    middle = x + dot_tn(par.pw[...], res.mixed[...]) + cols[0:C, 2:3]
+    res.middle[...] = middle.astype(BF16)
+    middle = res.middle[...].astype(F32)
     xhat, _ = norm_fwd(middle)
     normed = (xhat * cols[0:C, 3:4] + cols[0:C, 4:5]).astype(BF16)
     keep("attn", "mixed")
     need("uw")
     for i in range(0, MLP, 128):
-        u = dot_tn(par["uw"][:, i : i + 128], normed) + cols[i : i + 128, 7:8]
+        u = dot_tn(par.uw[:, i : i + 128], normed) + cols[i : i + 128, 7:8]
         half = 0.5 + 0.5 * lax.erf(u * (0.5**0.5))
-        res["hidden"][i : i + 128, :] = (u * half).astype(BF16)
-        res["slope"][i : i + 128, :] = (half + u * (jnp.exp(-0.5 * u * u) * 0.3989422804014327)).astype(BF16)
+        res.hidden[i : i + 128, :] = (u * half).astype(BF16)
+        res.slope[i : i + 128, :] = (half + u * (jnp.exp(-0.5 * u * u) * 0.3989422804014327)).astype(BF16)
     keep("middle")
     need("dw")
-    out = (middle + dot_nn(par["dw"][...], res["hidden"][...]) + cols[0:C, 5:6]).astype(BF16)
+    out = (middle + dot_nn(par.dw[...], res.hidden[...]) + cols[0:C, 5:6]).astype(BF16)
     keep("hidden", "slope")
     return out
 
@@ -182,22 +186,22 @@
 def mlp_grads(g, flat, small):
     ones = jnp.ones((8, TOK), BF16)
     small[...] = jnp.zeros(small.shape, F32)
-    put_row(small, 21, dot_nt(ones, g["dout"][...]))
-    put_row(small, 15, dot_nt(ones, g["du"][...]))
-    put_row(small, 13, dot_nt(ones, g["dn2"][...]))
-    put_row(small, 11, dot_nt(ones, g["dg2"][...]))
-    put_pairs(flat, 1152, g["n2"][...], g["du"], MLP)
-    put_pairs(flat, 2304, g["dout"][...], g["hidden"], MLP)
+    put_row(small, 21, dot_nt(ones, g.dout[...]))
+    put_row(small, 15, dot_nt(ones, g.du[...]))
+    put_row(small, 13, dot_nt(ones, g.dn2[...]))
+    put_row(small, 11, dot_nt(ones, g.dg2[...]))
+    put_pairs(flat, 1152, g.n2[...], g.du, MLP)
+    put_pairs(flat, 2304, g.dout[...], g.hidden, MLP)
 
 
 def attention_grads(g, flat, small):
     ones = jnp.ones((8, TOK), BF16)
     none = jnp.zeros((64, TOK), BF16)
-    put_row(small, 9, dot_nt(ones, g["dmid"][...]))
-    flat[960:1152, :] = dot_nt(g["mixed"][...], g["dmid"][0:128, :]).astype(BF16)
+    put_row(small, 9, dot_nt(ones, g.dmid[...]))
+    flat[960:1152, :] = dot_nt(g.mixed[...], g.dmid[0:128, :]).astype(BF16)
     mirror = ((127 - iota((128, 128), 0)) == spread(iota((128, 128), 1))).astype(BF16)
     for h in range(HEADS):
-        high, mid, _ = split3(g["rel"][h])
+        high, mid, _ = split3(g.rel[h])
         back = dot_nt(high, mirror) + dot_nt(mid, mirror)
         total = jnp.zeros((8, 256), F32)
         for ky in range(8):
@@ -206,66 +210,66 @@
         total = jnp.sum(total, axis=0, keepdims=True)
         small[24 + h : 25 + h, :] = total[:, 0:128]
         small[32 + h : 33 + h, :] = total[:, 128:256]
-    put_pairs(flat, 0, g["n1"][...], g["dpacked"], 512)
-    tail = dot_nt(g["n1"][...], jnp.concatenate([g["dpacked"][512:576, :], none], axis=0))
-    tail = tail + dot_nt(g["mixed"][...], jnp.concatenate([none, g["dmid"][128:192, :]], axis=0))
+    put_pairs(flat, 0, g.n1[...], g.dpacked, 512)
+    tail = dot_nt(g.n1[...], jnp.concatenate([g.dpacked[512:576, :], none], axis=0))
+    tail = tail + dot_nt(g.mixed[...], jnp.concatenate([none, g.dmid[128:192, :]], axis=0))
     flat[768:960, :] = tail.astype(BF16)
-    put_row(small, 4, dot_nt(ones, g["dpacked"][...]))
-    put_row(small, 2, dot_nt(ones, g["dn1"][...]))
-    put_row(small, 0, dot_nt(ones, g["dg1"][...]))
+    put_row(small, 4, dot_nt(ones, g.dpacked[...]))
+    put_row(small, 2, dot_nt(ones, g.dn1[...]))
+    put_row(small, 0, dot_nt(ones, g.dg1[...]))
     flat[SMALL : SMALL + 48, :] = small[...].astype(BF16)
     flat[SMALL + 48 : FLAT, :] = jnp.zeros((FLAT - SMALL - 48, 128), BF16)
 
 
 def backward(x, par, need, cols, res, stage, g, after_mlp):
     left = halves()
-    dout = g["dout"][...]
+    dout = g.dout[...]
     need("dw", "slope")
     for i in range(0, MLP, 128):
-        dh = dot_tn(par["dw"][:, i : i + 128], dout).astype(BF16).astype(F32)
-        g["du"][i : i + 128, :] = (dh * res["slope"][i : i + 128, :].astype(F32)).astype(BF16)
+        dh = dot_tn(par.dw[:, i : i + 128], dout).astype(BF16).astype(F32)
+        g.du[i : i + 128, :] = (dh * res.slope[i : i + 128, :].astype(F32)).astype(BF16)
     need("middle", "uw")
-    xhat, rstd = norm_fwd(res["middle"][...].astype(F32))
-    g["n2"][...] = (xhat * cols[0:C, 3:4] + cols[0:C, 4:5]).astype(BF16)
-    dn = dot_nn(par["uw"][...], g["du"][...]).astype(BF16)
-    g["dn2"][...] = dn
+    xhat, rstd = norm_fwd(res.middle[...].astype(F32))
+    g.n2[...] = (xhat * cols[0:C, 3:4] + cols[0:C, 4:5]).astype(BF16)
+    dn = dot_nn(par.uw[...], g.du[...]).astype(BF16)
+    g.dn2[...] = dn
     dn = dn.astype(F32)
-    g["dg2"][...] = (dn * xhat).astype(BF16)
+    g.dg2[...] = (dn * xhat).astype(BF16)
     dmid = (dout.astype(F32) + norm_bwd(dn, xhat, rstd, cols[0:C, 3:4])).astype(BF16)
-    g["dmid"][...] = dmid
+    g.dmid[...] = dmid
     after_mlp()
     need("pw", "mixed")
-    dmixed = dot_nn(par["pw"][...], dmid).astype(BF16)
+    dmixed = dot_nn(par.pw[...], dmid).astype(BF16)
     need("packed", "attn")
     for p, h, lanes in UNITS:
-        v = res["packed"][2 * C + DIM * h : 2 * C + DIM * h + DIM, lanes]
+        v = res.packed[2 * C + DIM * h : 2 * C + DIM * h + DIM, lanes]
         dm = dmixed[DIM * h : DIM * h + DIM, lanes]
         stage[p * HEADS + h] = own_window(dot_tn(v, dm), left).astype(BF16).astype(F32)
-        dv = dot_nt(dm, stack_windows(res["attn"][p * HEADS + h].astype(F32), left)).astype(BF16)
-        g["dpacked"][2 * C + DIM * h : 2 * C + DIM * h + DIM, lanes] = dv
+        dv = dot_nt(dm, stack_windows(res.attn[p * HEADS + h].astype(F32), left)).astype(BF16)
+        g.dpacked[2 * C + DIM * h : 2 * C + DIM * h + DIM, lanes] = dv
     for h in range(HEADS):
         drel = None
         for p in range(2):
-            a = res["attn"][p * HEADS + h].astype(F32)
+            a = res.attn[p * HEADS + h].astype(F32)
             da = stage[p * HEADS + h]
             ds = a * (da - jnp.sum(da * a, axis=0, keepdims=True))
             drel = ds if drel is None else drel + ds
             stage[p * HEADS + h] = ds * SCALE
-        g["rel"][h] = drel
+        g.rel[h] = drel
     for p, h, lanes in UNITS:
-        q = res["packed"][DIM * h : DIM * h + DIM, lanes]
-        k = res["packed"][C + DIM * h : C + DIM * h + DIM, lanes]
+        q = res.packed[DIM * h : DIM * h + DIM, lanes]
+        k = res.packed[C + DIM * h : C + DIM * h + DIM, lanes]
         wide = stack_windows(stage[p * HEADS + h], left)
-        g["dpacked"][DIM * h : DIM * h + DIM, lanes] = dot_nn(k, wide).astype(BF16)
-        g["dpacked"][C + DIM * h : C + DIM * h + DIM, lanes] = dot_nt(q, wide).astype(BF16)
+        g.dpacked[DIM * h : DIM * h + DIM, lanes] = dot_nn(k, wide).astype(BF16)
+        g.dpacked[C + DIM * h : C + DIM * h + DIM, lanes] = dot_nt(q, wide).astype(BF16)
     need("xt")
     xhat, rstd = norm_fwd(x[...].astype(F32))
-    g["n1"][...] = (xhat * cols[0:C, 0:1] + cols[0:C, 1:2]).astype(BF16)
+    g.n1[...] = (xhat * cols[0:C, 0:1] + cols[0:C, 1:2]).astype(BF16)
     need("qw")
-    dn = dot_nn(par["qw"][...], g["dpacked"][...]).astype(BF16)
-    g["dn1"][...] = dn
+    dn = dot_nn(par.qw[...], g.dpacked[...]).astype(BF16)
+    g.dn1[...] = dn
     dn = dn.astype(F32)
-    g["dg1"][...] = (dn * xhat).astype(BF16)
+    g.dg1[...] = (dn * xhat).astype(BF16)
     return dmid.astype(F32) + norm_bwd(dn, xhat, rstd, cols[0:C, 0:1])
 
 
@@ -367,14 +371,14 @@
 
 def first_forward(*refs):
     imagery_far, cotangent_far = refs[0:2]
-    far = dict(zip(PAR_NAMES, refs[2:15]))
+    far = Box(zip(PAR_NAMES, refs[2:15]))
     own = refs[15]
     strips = refs[16:19]
     xt_far = refs[19]
-    res_far = dict(zip(RES_NAMES, refs[20:26]))
+    res_far = Box(zip(RES_NAMES, refs[20:26]))
     grid, edge, vec, table, bias, sems = refs[26:32]
-    par = dict(zip(PAR_NAMES, refs[32:45]))
-    res = dict(zip(RES_NAMES, refs[45:51]))
+    par = Box(zip(PAR_NAMES, refs[32:45]))
+    res = Box(zip(RES_NAMES, refs[45:51]))
     imagery, cotangent, xt, stage = refs[51:]
     need = Copies(sems)
     need.start("imagery", imagery_far, imagery)
@@ -411,13 +415,13 @@
     own_in = refs[0]
     strips_in = refs[1:4]
     cotangent_far = refs[4]
-    far = dict(zip(PAR_NAMES, refs[5:18]))
+    far = Box(zip(PAR_NAMES, refs[5:18]))
     out_own, back_own = refs[18:20]
     strips = refs[20:23]
-    g = dict(zip(GRAD_NAMES + ("hidden", "mixed"), refs[23:36]))
+    g = Box(zip(GRAD_NAMES + ("hidden", "mixed"), refs[23:36]))
     grid, edge, vec, table, bias, sems = refs[36:42]
-    par = dict(zip(PAR_NAMES, refs[42:55]))
-    res = dict(zip(("packed", "attn", "middle", "slope"), refs[55:59]), hidden=g["hidden"], mixed=g["mixed"])
+    par = Box(zip(PAR_NAMES, refs[42:55]))
+    res = Box(zip(("packed", "attn", "middle", "slope"), refs[55:59]), hidden=g.hidden, mixed=g.mixed)
     cotangent, xt, stage = refs[59:]
     need = Copies(sems)
     start_params(need, VEC_NAMES + ("rel",), far, par, 1)
@@ -433,7 +437,7 @@
     cols = load_columns(vec, par, 1)
     position_bias(par, 1, table, bias)
     fill_grid(grid, edge, cotangent, strips_in, 1, 0, 0, 16, 16)
-    g["dout"][...] = to_channels(grid_get(grid, 4, 4)).astype(BF16)
+    g.dout[...] = to_channels(grid_get(grid, 4, 4)).astype(BF16)
     out = forward(x, par, need, cols, bias, res, stage, zones, nothing)
     grid_put(grid, to_tokens(out.astype(F32)))
     for r in range(TILE):
@@ -448,7 +452,7 @@
 
 
 def second_grads(*refs):
-    g = dict(zip(GRAD_NAMES + ("hidden", "mixed"), refs[0:13]))
+    g = Box(zip(GRAD_NAMES + ("hidden", "mixed"), refs[0:13]))
     flat, small = refs[13:]
     mlp_grads(g, flat, small)
     attention_grads(g, flat, small)
@@ -461,32 +465,31 @@
     back_in = refs[0]
     strips_in = refs[1:4]
     flat_two = refs[4]
-    far = dict(zip(BACK_NAMES, refs[5:17]))
+    far = Box(zip(BACK_NAMES, refs[5:17]))
     xt_far = refs[17]
-    res_far = dict(zip(RES_NAMES, refs[18:24]))
+    res_far = Box(zip(RES_NAMES, refs[18:24]))
     dx_channels, kept, sent = refs[24:27]
     grid, edge, vec, sems = refs[27:31]
-    par = dict(zip(BACK_NAMES, refs[31:43]))
-    g = dict(zip(GRAD_NAMES, refs[43:54]))
-    res = dict(zip(RES_NAMES, refs[54:60]))
+    par = Box(zip(BACK_NAMES, refs[31:43]))
+    g = Box(zip(GRAD_NAMES, refs[43:54]))
+    res = Box(zip(RES_NAMES, refs[54:60]))
     xt, flat, small, stage = refs[60:]
-    g["hidden"] = res["hidden"]
-    g["mixed"] = res["mixed"]
+    g = Box(g, hidden=res.hidden, mixed=res.mixed)
     need = Copies(sems)
     start_params(need, ("dw",), far, par, 0)
-    need.start("slope", res_far["slope"], res["slope"])
+    need.start("slope", res_far.slope, res.slope)
     start_params(need, VEC_NAMES, far, par, 0)
-    need.start("middle", res_far["middle"], res["middle"])
+    need.start("middle", res_far.middle, res.middle)
     start_params(need, ("uw",), far, par, 0)
-    need.start("hidden", res_far["hidden"], res["hidden"])
-    need.start("mixed", res_far["mixed"], res["mixed"])
+    need.start("hidden", res_far.hidden, res.hidden)
+    need.start("mixed", res_far.mixed, res.mixed)
     start_params(need, ("pw",), far, par, 0)
-    need.start("packed", res_far["packed"], res["packed"])
-    need.start("attn", res_far["attn"], res["attn"])
+    need.start("packed", res_far.packed, res.packed)
+    need.start("attn", res_far.attn, res.attn)
     need.start("xt", xt_far, xt)
     start_params(need, ("qw",), far, par, 0)
     fill_grid(grid, edge, back_in, strips_in, 1, 4, 8, 0, 4)
-    g["dout"][...] = to_channels(grid_get(grid, 0, 4)).astype(BF16)
+    g.dout[...] = to_channels(grid_get(grid, 0, 4)).astype(BF16)
     need(*VEC_NAMES)
     cols = load_columns(vec, par, 0)
 
@@ -554,8 +557,8 @@
 
 
 def unpack_rest(mine, other, *refs):
-    far = dict(zip(PAR_NAMES, refs[4:17]))
-    near_refs = dict(zip(PAR_NAMES, refs[17:30]))
+    far = Box(zip(PAR_NAMES, refs[4:17]))
+    near_refs = Box(zip(PAR_NAMES, refs[17:30]))
     copies = Copies(refs[30])
     factor = outs_factor
     parity = lax.axis_index("cols") % 2
@@ -576,7 +579,7 @@
         table = jnp.concatenate([raw(SMALL + 24, 8), raw(SMALL + 32, 8)], axis=1)
         table = dot_nn(table, flip) * factor
         for h in range(HEADS):
-            near_refs["rel"][h, b : b + 1, :] = table[h : h + 1, 0 : SPAN * SPAN]
+            near_refs.rel[h, b : b + 1, :] = table[h : h + 1, 0 : SPAN * SPAN]
     for name in VEC_NAMES + ("rel",):
         copies.start(name, near_refs[name], far[name])
     copies.rest()
@@ -654,7 +657,7 @@
     edge = pltpu.VMEM((64, 256), F32)
     vec = pltpu.VMEM((128, MLP), F32)
     tables = [pltpu.VMEM((8, 256), F32), pltpu.VMEM((HEADS, 64, 128), F32)]
-    par = dict(zip(PAR_NAMES, params))
+    par = Box(zip(PAR_NAMES, params))
     par_kinds = {n: BF16 if n in WEIGHTS else F32 for n in PAR_NAMES}
     par_vmem = {n: pltpu.VMEM(PAR_SHAPES[n], par_kinds[n]) for n in PAR_NAMES}
     res_vmem = [pltpu.VMEM(s, BF16) for s in RES_SHAPES]
@@ -721,7 +724,6 @@
         out_shape=[pltpu.HBM(p.shape, F32) for p in params],
         scratch_shapes=[pltpu.VMEM(PAR_SHAPES[n], F32) for n in PAR_NAMES] + [pltpu.SemaphoreType.DMA((16,))],
         input_output_aliases={2: 2, 3: 5, 4: 9, 5: 11},
-        name="unpack_rest",
         compiler_params=pltpu.CompilerParams(vmem_limit_bytes=30 * 2**20),
     )(near(mine), near(swap(mine)), *[pltpu.with_memory_space_constraint(h, pltpu.HBM) for h in half])
     grads = list(grads)

time: 90.4 us -> 90.4 us (level)
  no operation moved by 1% of the time
where the time goes in v6:
time: 90.4 us; the launch traced here: 90.2 us
  blocking collectives  42.7 us (47%)
  Pallas kernels  20 us (22%)
  starting transfers between devices  18.9 us (21%)
  waiting for transfers between devices  7.66 us (8%)
    all_to_all x2, blocking collectives, send_parts(): lax.all_to_all(parts, ('rows', 'cols'), 0, 0, axis_index_groups=groups, t...  42.7 us
    pallas_call x8, Pallas kernels, call(): pl.pallas_call(kernel, in_specs=[VMEM] * len(args) + [FAR] * len(far_args...  18.5 us
    ppermute x2, starting transfers between devices, swap(): lax.ppermute(value, 'cols', [(c, c ^ 1) for c in range(lax.axis_size('col...  6.7 us
    ppermute x2, starting transfers between devices, exchange(): lax.ppermute(corner, ('rows', 'cols'), both)  5.24 us
    ppermute x2, waiting for transfers between devices, exchange(): lax.ppermute(corner, ('rows', 'cols'), both)  5.12 us
    ppermute x2, starting transfers between devices, exchange(): lax.ppermute(row_strip, 'rows', down)  4.88 us
    ppermute x2, starting transfers between devices, exchange(): lax.ppermute(col_strip, 'cols', along)  2.11 us
    ppermute x2, waiting for transfers between devices, swap(): lax.ppermute(value, 'cols', [(c, c ^ 1) for c in range(lax.axis_size('col...  2.1 us
  transfers between devices with their start and end apart: 8, of which 4 were waited for; matrix products, arithmetic and copies ran while one was open for 0% of the time, Pallas kernels for 4%

profile of v6, /device:TPU:1, one launch (start us, length us, event | category | flops | bytes accessed | tf_op | source)
XLA Modules:
  0.0 90.2 jit_solution(9519506597859324390)
XLA Ops:
  0.6 4.5 %shard_map.262 = (bf16[16,16,192]{2,1,0:T(8,128)(2,1)S(1)}, bf16[128,192]{1,0:T(8,128)(2,1)S(1)}, bf16[128,192]{1,0:T(8,128)(2,1)S(1)}, bf16[32,192]{1,0:T(8,128...) custom-call(bf16[16,16,192]{2,1,0:T(8,128)(2,1)} %refs_0_.1, ...), custom_call_target="tpu_custom_call" | custom-call | flops 5000000000 | bytes 4000000 | tf_op jit(solution)/shard_map/pallas_call | solution.py:602
  5.1 1.4 %collective-permute-start = (bf16[128,192]{1,0:T(8,128)(2,1)S(1)}, bf16[128,192]{1,0:T(8,128)(2,1)S(1)}, u32[]{:S(2)}, u32[]{:S(2)}) collective-permute-start(bf16[128,192]{1,0:T(8,128)(2,1)S(1)} %get-tuple-element.67), channel_id=1, source_target_pairs={{0,15},{1,0},{2,1},{3,2},{4,3},{5,4},{6,5},{7,6},{8,7},{9,8},{10,9... | collective-permute-start | bytes 147464 | tf_op jit(solution)/shard_map/ppermute | solution.py:629
  6.6 4.9 %collective-permute-start.1 = (bf16[128,192]{1,0:T(8,128)(2,1)S(1)}, bf16[128,192]{1,0:T(8,128)(2,1)S(1)}, u32[]{:S(2)}, u32[]{:S(2)}) collective-permute-start(bf16[128,192]{1,0:T(8,128)(2,1)S(1)} %get-tuple-element.68), channel_id=1, source_target_pairs={{0,112},{16,0},{32,16},{48,32},{64,48},{80,64},{96,80},{112,96},{1... | collective-permute-start | bytes 147464 | tf_op jit(solution)/shard_map/ppermute | solution.py:630
  11.5 5.2 %collective-permute-start.2 = (bf16[32,192]{1,0:T(8,128)(2,1)S(1)}, bf16[32,192]{1,0:T(8,128)(2,1)S(1)}, u32[]{:S(2)}, u32[]{:S(2)}) collective-permute-start(bf16[32,192]{1,0:T(8,128)(2,1)S(1)} %get-tuple-element.69), channel_id=1, source_target_pairs={{0,127},{1,112},{2,113},{3,114},{4,115},{5,116},{6,117},{7,118},{8... | collective-permute-start | bytes 36872 | tf_op jit(solution)/shard_map/ppermute | solution.py:631
  16.6 0.9 collective-permute-done.2.refs_3_
  17.5 0.0 collective-permute-done.refs_1_
  17.5 0.0 collective-permute-done.1.refs_2_
  17.5 5.5 %shard_map.263 = (bf16[16,16,192]{2,1,0:T(8,128)(2,1)S(1)}, bf16[16,16,192]{2,1,0:T(8,128)(2,1)S(1)}, bf16[128,192]{1,0:T(8,128)(2,1)S(1)}, bf16[128,192]{1,0:T(...) custom-call(bf16[16,16,192]{2,1,0:T(8,128)(2,1)S(1)} %get-tuple-elem, ...), custom_call_target="tpu_custom_call" | custom-call | flops 10000000000 | bytes 4000000 | tf_op jit(solution)/shard_map/pallas_call | solution.py:602
  23.0 0.1 collective-permute-start.5
  23.1 0.7 collective-permute-start.3
  23.8 1.1 %shard_map.264.refs_4_ = bf16[3584,128]{1,0:T(8,128)(2,1)S(1)} custom-call(bf16[192,256]{1,0:T(8,128)(2,1)S(1)} %get-tuple-element.75.refs_0_, bf16[192,256]{1,0:T(8,128)(2,1)S(1)} %get-tuple-element.76.refs_1_, bf16[192,256]{1,0:T(8,128)(2,1)S(1)} %get-tuple-element.77.refs_2_, bf16[192,256]{1,0:T(8,128)(2,1)S(1)} %get-tuple-element.78.refs_3_, ...), custom_call_target="tpu_custom_call" | custom-call | flops 1000000000 | bytes 4000000 | tf_op jit(solution)/shard_map/pallas_call | solution.py:602
  24.8 4.3 %collective-permute-done.5.refs_3_.corner_in = bf16[32,192]{1,0:T(8,128)(2,1)S(1)} collective-permute-done((bf16[32,192]{1,0:T(8,128)(2,1)S(1)}, bf16[32,192]{1,0:T(8,128)(2,1)S(1)}, u32[]{:S(2)}, u32[]{:S(2)}) %collective-permute-start.5) | collective-permute-done | bytes 12320 | tf_op jit(solution)/shard_map/ppermute | solution.py:631
  29.1 0.4 collective-permute-done.4.refs_2_.row_in
  29.5 5.0 %shard_map.265 = (bf16[192,256]{1,0:T(8,128)(2,1)S(1)}, bf16[3584,128]{1,0:T(8,128)(2,1)S(1)}, bf16[3584,128]{1,0:T(8,128)(2,1)S(1)}) custom-call(bf16[16,16,192]{2,1,0:T(8,128)(2,1)S(1)} %get-tuple-element.74.refs_0_, bf16[128,192]{1,0:T(8,128)(2,1)S(1)} %collective-permute-done.3.refs_1_.col_in, ...), custom_call_target="tpu_custom_call" | custom-call | flops 5000000000 | bytes 4000000 | tf_op jit(solution)/shard_map/pallas_call | solution.py:602
  34.5 3.6 %collective-permute-start.6 = (bf16[3584,128]{1,0:T(8,128)(2,1)S(1)}, bf16[3584,128]{1,0:T(8,128)(2,1)S(1)}, u32[]{:S(2)}, u32[]{:S(2)}) collective-permute-start(bf16[3584,128]{1,0:T(8,128)(2,1)S(1)} %get-tuple-element.99), channel_id=1, source_target_pairs={{0,1},{1,0},{2,3},{3,2},{4,5},{5,4},{6,7},{7,6},{8,9},{9,8},{10,11... | collective-permute-start | bytes 2752520 | tf_op jit(solution)/shard_map/ppermute | solution.py:636
  38.1 2.1 %collective-permute-done.6.got = bf16[3584,128]{1,0:T(8,128)(2,1)S(1)} collective-permute-done((bf16[3584,128]{1,0:T(8,128)(2,1)S(1)}, bf16[3584,128]{1,0:T(8,128)(2,1)S(1)}, u32[]{:S(2)}, u32[]{:S(2)}) %collective-permute-start.6) | collective-permute-done | bytes 917536 | tf_op jit(solution)/shard_map/ppermute | solution.py:636
  40.2 0.2 shard_map.267
  40.4 22.8 %all_to_all.10 = bf16[64,56,128]{2,1,0:T(8,128)(2,1)S(1)} all-to-all(bf16[64,56,128]{2,1,0:T(8,128)(2,1)S(1)} %bitcast.13), channel_id=1, replica_groups={{0,2,4,6,8,10,12,14,16,18,20,22,24,26,28,30,32,34,36,38,40,42,44,46,48,..., dimensions={0} | all-to-all | bytes 1835008 | tf_op jit(solution)/shard_map/all_to_all | solution.py:644
  63.2 0.2 shard_map.268
  63.4 19.9 %all_to_all.11 = bf16[64,56,128]{2,1,0:T(8,128)(2,1)S(1)} all-to-all(bf16[64,56,128]{2,1,0:T(8,128)(2,1)S(1)} %bitcast.9), channel_id=1, replica_groups={{0,2,4,6,8,10,12,14,16,18,20,22,24,26,28,30,32,34,36,38,40,42,44,46,48,..., dimensions={0} | all-to-all | bytes 1835008 | tf_op jit(solution)/shard_map/all_to_all | solution.py:644
  83.3 3.1 %collective-permute-start.7 = (bf16[3584,128]{1,0:T(8,128)(2,1)S(1)}, bf16[3584,128]{1,0:T(8,128)(2,1)S(1)}, u32[]{:S(2)}, u32[]{:S(2)}) collective-permute-start(bf16[3584,128]{1,0:T(8,128)(2,1)S(1)} %bitcast.10), channel_id=1, source_target_pairs={{0,1},{1,0},{2,3},{3,2},{4,5},{5,4},{6,7},{7,6},{8,9},{9,8},{10,11... | collective-permute-start | bytes 2752520 | tf_op jit(solution)/shard_map/ppermute | solution.py:636
  86.4 0.8 shard_map.266
  87.2 1.3 %shard_map.269 = (f32[2,192,576]{2,1,0:T(8,128)}, f32[2,192,192]{2,1,0:T(8,128)}, f32[2,192,768]{2,1,0:T(8,128)}, f32[2,192,768]{2,1,0:T(8,128)}) custom-call(bf16[3584,128]{1,0:T(8,128)(2,1)S(1)} %bitcast.11), custom_call_target="tpu_custom_call" | custom-call | flops 1000000000 | bytes 4000000 | tf_op jit(solution)/shard_map/pallas_call | solution.py:602
  88.5 1.5 %shard_map.270 = (f32[2,192]{1,0:T(2,128)}, f32[2,192]{1,0:T(2,128)}, f32[2,192,576]{2,1,0:T(8,128)}, f32[2,576]{1,0:T(2,128)}, f32[6,2,225]{2,1,0:T(2,128)}, /*...) custom-call(bf16[3584,128]{1,0:T(8,128)(2,1)S(1)} %bitcast.12, ...), custom_call_target="tpu_custom_call", output_to_operand_aliasing={{2}: (2, {}), {5}: (3, {}), {9}: (4, {}), {11}: (5, {})} | custom-call | tf_op jit(solution)/shard_map/pallas_call | solution.py:720
  (3 shorter events, 0.0 us)
Async XLA Ops:
  5.1 12.4 %collective-permute-start = (bf16[128,192]{1,0:T(8,128)(2,1)S(1)}, bf16[128,192]{1,0:T(8,128)(2,1)S(1)}, u32[]{:S(2)}, u32[]{:S(2)}) collective-permute-start(bf16[128,192]{1,0:T(8,128)(2,1)S(1)} %get-tuple-element.67), channel_id=1, source_target_pairs={{0,15},{1,0},{2,1},{3,2},{4,3},{5,4},{6,5},{7,6},{8,7},{9,8},{10,9... | collective-permute-start | bytes 147464 | tf_op jit(solution)/shard_map/ppermute | solution.py:629
  6.6 10.9 %collective-permute-start.1 = (bf16[128,192]{1,0:T(8,128)(2,1)S(1)}, bf16[128,192]{1,0:T(8,128)(2,1)S(1)}, u32[]{:S(2)}, u32[]{:S(2)}) collective-permute-start(bf16[128,192]{1,0:T(8,128)(2,1)S(1)} %get-tuple-element.68), channel_id=1, source_target_pairs={{0,112},{16,0},{32,16},{48,32},{64,48},{80,64},{96,80},{112,96},{1... | collective-permute-start | bytes 147464 | tf_op jit(solution)/shard_map/ppermute | solution.py:630
  11.5 6.0 %collective-permute-start.2 = (bf16[32,192]{1,0:T(8,128)(2,1)S(1)}, bf16[32,192]{1,0:T(8,128)(2,1)S(1)}, u32[]{:S(2)}, u32[]{:S(2)}) collective-permute-start(bf16[32,192]{1,0:T(8,128)(2,1)S(1)} %get-tuple-element.69), channel_id=1, source_target_pairs={{0,127},{1,112},{2,113},{3,114},{4,115},{5,116},{6,117},{7,118},{8... | collective-permute-start | bytes 36872 | tf_op jit(solution)/shard_map/ppermute | solution.py:631
  23.0 6.1 %collective-permute-start.5 = (bf16[32,192]{1,0:T(8,128)(2,1)S(1)}, bf16[32,192]{1,0:T(8,128)(2,1)S(1)}, u32[]{:S(2)}, u32[]{:S(2)}) collective-permute-start(bf16[32,192]{1,0:T(8,128)(2,1)S(1)} %get-tuple-element.73), channel_id=1, source_target_pairs={{0,17},{1,18},{2,19},{3,20},{4,21},{5,22},{6,23},{7,24},{8,25},{9,... | collective-permute-start | bytes 36872 | tf_op jit(solution)/shard_map/ppermute | solution.py:631
  23.1 6.0 %collective-permute-start.3 = (bf16[128,192]{1,0:T(8,128)(2,1)S(1)}, bf16[128,192]{1,0:T(8,128)(2,1)S(1)}, u32[]{:S(2)}, u32[]{:S(2)}) collective-permute-start(bf16[128,192]{1,0:T(8,128)(2,1)S(1)} %get-tuple-element.71), channel_id=1, source_target_pairs={{0,1},{1,2},{2,3},{3,4},{4,5},{5,6},{6,7},{7,8},{8,9},{9,10},{10,1... | collective-permute-start | bytes 147464 | tf_op jit(solution)/shard_map/ppermute | solution.py:629
  23.8 5.8 %collective-permute-start.4 = (bf16[128,192]{1,0:T(8,128)(2,1)S(1)}, bf16[128,192]{1,0:T(8,128)(2,1)S(1)}, u32[]{:S(2)}, u32[]{:S(2)}) collective-permute-start(bf16[128,192]{1,0:T(8,128)(2,1)S(1)} %get-tuple-element.72), channel_id=1, source_target_pairs={{0,16},{16,32},{32,48},{48,64},{64,80},{80,96},{96,112},{112,0},{1... | collective-permute-start | bytes 147464 | tf_op jit(solution)/shard_map/ppermute | solution.py:630
  34.5 5.7 %collective-permute-start.6 = (bf16[3584,128]{1,0:T(8,128)(2,1)S(1)}, bf16[3584,128]{1,0:T(8,128)(2,1)S(1)}, u32[]{:S(2)}, u32[]{:S(2)}) collective-permute-start(bf16[3584,128]{1,0:T(8,128)(2,1)S(1)} %get-tuple-element.99), channel_id=1, source_target_pairs={{0,1},{1,0},{2,3},{3,2},{4,5},{5,4},{6,7},{7,6},{8,9},{9,8},{10,11... | collective-permute-start | bytes 2752520 | tf_op jit(solution)/shard_map/ppermute | solution.py:636
  83.3 5.2 %collective-permute-start.7 = (bf16[3584,128]{1,0:T(8,128)(2,1)S(1)}, bf16[3584,128]{1,0:T(8,128)(2,1)S(1)}, u32[]{:S(2)}, u32[]{:S(2)}) collective-permute-start(bf16[3584,128]{1,0:T(8,128)(2,1)S(1)} %bitcast.10), channel_id=1, source_target_pairs={{0,1},{1,0},{2,3},{3,2},{4,5},{5,4},{6,7},{7,6},{8,9},{9,8},{10,11... | collective-permute-start | bytes 2752520 | tf_op jit(solution)/shard_map/ppermute | solution.py:636
